TPU v7x, 512 devices: a whole 4x4x16 slice. The times are simulated.
512 devices in a mesh: ens: 4 (over y), lat: 16 (over z), lon: 8 (over x, core).
Axes of the slice: x: 4, y: 4, z: 16, core: 2. Of those that a mesh axis runs over, the one named last changes fastest.
Arguments:
- maxima: float32 [128, 512, 4096], P('ens', 'lat', 'lon'), may hold values from 15 to 150
- latent: float32 [3, 512, 4096], P(None, 'lat', 'lon'), may hold values from 1 to 3, as said below
- coupling: float32 [3, 3], replicated, may hold values from -7.2 to 32, as said below
- local_precision: float32 [3, 512, 4096], P(None, 'lat', 'lon'), may hold values from 0.64 to 192, as said below
Outputs:
- solution: float32 [3, 512, 4096], P(None, 'lat', 'lon')
Inputs may be any that keep to these rules, and one draw needn't show every extreme that they name: latent[0] lies in 1 to 2.5, latent[1] in log 10 to log 20, latent[2] in 1 to 2.5. coupling is symmetric with a dominant positive diagonal. `local_precision`: positive.
All inputs are finite; a program needn't handle non-finite values.
Results may differ from a plain program's by a relative error of at most 0.0001.
Values sent between devices are 32-bit elements; how exact they have to be, the bound alone decides.
No kernel may reach another device: no remote copies, remote signals or barrier semaphores. Data moves between devices by JAX's collectives and lax.ppermute only.
A program may use at most 64 MiB of HBM per device.

v0:
```python
import jax
import jax.numpy as jnp
from jax import lax
from jax.sharding import Mesh
from jax.sharding import PartitionSpec as P

ITERS = 3
LON = ("lon_0", "lon_1")


def with_halo(value, sides, width):
    edges = {}
    for axis, dim in sides:
        devices, length = (lax.axis_size(axis), value.shape[dim])
        up = [(i, (i + 1) % devices) for i in range(devices - 1)]
        last = lax.slice_in_dim(value, length - width, length, axis=dim)
        first = lax.slice_in_dim(value, 0, width, axis=dim)
        edges[dim] = (
            lax.ppermute(last, axis, up),
            lax.ppermute(first, axis, [(b, a) for a, b in up]),
        )
    done = []
    for _, dim in sides:
        low, high = edges[dim]
        around = [(width, width) if d in done else (0, 0) for d in range(value.ndim)]
        value = jnp.concatenate([jnp.pad(low, around), value, jnp.pad(high, around)], axis=dim)
        done.append(dim)
    return value


def sent_to_all(value, axis):
    copies = jnp.broadcast_to(value, (lax.axis_size(axis), *value.shape))
    return lax.all_to_all(copies, axis, split_axis=0, concat_axis=0, tiled=True)


def over_copies(value, axis):
    return sent_to_all(value, axis).sum(axis=0)


def together(arrays, axis):
    ends = [0]
    for a in arrays:
        ends.append(ends[-1] + a.size)
    so_far = over_copies(jnp.concatenate([a.ravel() for a in arrays]), axis)
    return tuple((so_far[b:e].reshape(a.shape) for a, b, e in zip(arrays, ends, ends[1:])))


def one_axis_at_a_time(value, axes):
    far, near = axes
    nearer = over_copies(value, near)
    return over_copies(nearer, far)


def packed_total(arrays, axis):
    ends = [0]
    for a in arrays:
        ends.append(ends[-1] + a.size)
    so_far = one_axis_at_a_time(jnp.concatenate([a.ravel() for a in arrays]), axis)
    return tuple((so_far[b:e].reshape(a.shape) for a, b, e in zip(arrays, ends, ends[1:])))


def gev_terms(maxima, latent):
    loc_par = 10.0 * latent[0]
    scale_par = jnp.exp(latent[1])
    shape_par = 0.1 * latent[2]
    scaled = (maxima - loc_par) / scale_par
    inside = 1.0 + shape_par * scaled
    log_inside = jnp.log(inside)
    tail_term = jnp.exp(-log_inside / shape_par)
    common_term = (1.0 + shape_par - tail_term) / inside
    score_loc = 10.0 * common_term / scale_par
    score_scale = scaled * common_term - 1.0
    score_shape = 0.1 * (
        log_inside * (1.0 - tail_term) / (shape_par * shape_par) - scaled * common_term / shape_par
    )
    scores = jnp.stack([jnp.sum(score_loc, 0), jnp.sum(score_scale, 0), jnp.sum(score_shape, 0)])
    hessian = jnp.stack(
        [
            jnp.sum(score_loc * score_loc, 0),
            jnp.sum(score_loc * score_scale, 0),
            jnp.sum(score_loc * score_shape, 0),
            jnp.sum(score_scale * score_scale, 0),
            jnp.sum(score_scale * score_shape, 0),
            jnp.sum(score_shape * score_shape, 0),
        ]
    )
    return (scores, hessian)


def mix_rows(coupling, laplace_term):
    return jnp.stack(
        [
            coupling[0, 0] * laplace_term[0]
            + coupling[0, 1] * laplace_term[1]
            + coupling[0, 2] * laplace_term[2],
            coupling[1, 0] * laplace_term[0]
            + coupling[1, 1] * laplace_term[1]
            + coupling[1, 2] * laplace_term[2],
            coupling[2, 0] * laplace_term[0]
            + coupling[2, 1] * laplace_term[1]
            + coupling[2, 2] * laplace_term[2],
        ]
    )


def tile_pad(vector):
    return with_halo(vector, (("lat", 1), (LON, 2)), 1)


def prior_apply(vector, coupling, local_precision, padder):
    padded = padder(vector)
    beside = padded[:, 2:, 1:-1] + padded[:, :-2, 1:-1] + padded[:, 1:-1, 2:] + padded[:, 1:-1, :-2]
    laplace_term = 4.0 * vector - beside
    return mix_rows(coupling, laplace_term) + local_precision * vector


def hessian_apply(vector, hessian):
    return jnp.stack(
        [
            hessian[0] * vector[0] + hessian[1] * vector[1] + hessian[2] * vector[2],
            hessian[1] * vector[0] + hessian[3] * vector[1] + hessian[4] * vector[2],
            hessian[2] * vector[0] + hessian[4] * vector[1] + hessian[5] * vector[2],
        ]
    )


def quarter_sum(values):
    rows = values.reshape(-1, values.shape[-1])
    count = rows.shape[0] // lax.axis_size("ens")
    start = lax.axis_index("ens") * count
    return jnp.sum(lax.dynamic_slice_in_dim(rows, start, count, 0))


def per_device(maxima, latent, coupling, local_precision):
    scores_local, hessian_local = gev_terms(maxima, latent)
    scores, hessian = together((scores_local, hessian_local), "ens")

    def operate(vector):
        return prior_apply(vector, coupling, local_precision, tile_pad) + hessian_apply(
            vector, hessian
        )

    def two_products(residual, image):
        return packed_total(
            (quarter_sum(residual * residual), quarter_sum(residual * image)),
            (("ens", "lat"), ("lon_0", "lon_1")),
        )

    solution = latent
    residual = scores - prior_apply(latent, coupling, local_precision, tile_pad)
    image = operate(residual)
    norm_now, product = two_products(residual, image)
    step_size = norm_now / product
    direction, along = (residual, image)
    for iteration in range(ITERS):
        solution = solution + step_size * direction
        residual = residual - step_size * along
        if iteration + 1 < ITERS:
            image = operate(residual)
            norm_next, product = two_products(residual, image)
            factor = norm_next / norm_now
            step_size = norm_next / (product - factor * norm_next / step_size)
            direction = residual + factor * direction
            along = image + factor * along
            norm_now = norm_next
    return solution


def solution(mesh):
    split = Mesh(
        mesh.devices.reshape(mesh.shape["ens"], mesh.shape["lat"], 4, 2),
        ("ens", "lat", "lon_0", "lon_1"),
    )
    placed = (P("ens", "lat", LON), P(None, "lat", LON), P(), P(None, "lat", LON))
    return jax.shard_map(
        per_device, mesh=split, in_specs=placed, out_specs=P(None, "lat", LON), check_vma=False
    )
```

profile of v0, /device:TPU:1, one launch (start us, length us, event | category | flops | bytes accessed | tf_op | source)
XLA Modules:
  0.0 218.1 jit_solution(10310309852277898621)
XLA Ops:
  0.0 0.9 multiply_bitcast_fusion
  0.9 2.9 %subtract_multiply_fusion = (f32[32,32,512]{2,1,0:T(8,128)S(1)}, f32[32,32,512]{2,1,0:T(8,128)S(1)}, f32[32,32,512]{2,1,0:T(8,128)S(1)}) fusion(f32[32,512]{1,0:T(8,128)S(1)} %get-tuple-element.68, f32[32,512]{1,0:T(8,128)S(1)} %get-tuple-element.69, f32[32,512]{1,0:T(8,128)S(1)} %get-tuple-element.70, f32[32,32,512]{2,1,0:T(8,128)} %param.4, ...), kind=kLoop, calls=%fused_computation.6 | loop fusion | flops 8912896 | bytes 8716288 | tf_op jit(solution)/shard_map/mul | solution.py:73
  3.9 1.1 fusion.32
  5.3 2.6 %broadcast_in_dim.14 = f32[4,1,147456]{2,1,0:T(1,128)} broadcast(f32[147456]{0:T(1024)S(1)} %pad_maximum_fusion), dimensions={2} | broadcast | bytes 2949120 | tf_op jit(solution)/shard_map/broadcast_in_dim | solution.py:32
  7.9 5.1 %all-to-all-start = ((f32[4,1,147456]{2,1,0:T(1,128)}), f32[4,1,147456]{2,1,0:T(1,128)S(1)}, u32[]{:S(2)}, u32[]{:S(2)}) async-start(f32[4,1,147456]{2,1,0:T(1,128)} %broadcast_in_dim.14), calls=%async_computation | async-start | bytes 4718592 | tf_op jit(solution)/shard_map/all_to_all | solution.py:33
  13.1 7.4 %collective-permute-start.2 = (f32[3,32,1]{2,1,0:T(8,128)S(1)}, f32[3,32,1]{2,1,0:T(8,128)S(1)}, u32[]{:S(2)}, u32[]{:S(2)}) collective-permute-start(f32[3,32,1]{2,1,0:T(8,128)S(1)} %get-tuple-element.64), channel_id=1, source_target_pairs={{1,0},{2,1},{3,2},{4,3},{5,4},{6,5},{7,6},{9,8},{10,9},{11,10},{12... | collective-permute-start | bytes 1160 | tf_op jit(solution)/shard_map/ppermute | solution.py:20
  20.5 1.9 collective-permute-start.3
  22.5 1.3 collective-permute-start
  23.8 4.0 %collective-permute-start.1 = (f32[3,1,512]{2,1,0:T(1,128)S(1)}, f32[3,1,512]{2,1,0:T(1,128)S(1)}, u32[]{:S(2)}, u32[]{:S(2)}) collective-permute-start(f32[3,1,512]{2,1,0:T(1,128)S(1)} %get-tuple-element.66), channel_id=1, source_target_pairs={{0,8},{8,16},{16,24},{24,32},{32,40},{40,48},{48,56},{56,64},{64,7... | collective-permute-start | bytes 18440 | tf_op jit(solution)/shard_map/ppermute | solution.py:19
  27.8 0.7 fusion.49
  28.7 5.6 %multiply_add_fusion.13 = (f32[1,32,512]{2,1,0:T(8,128)S(1)}, f32[1,32,512]{2,1,0:T(8,128)S(1)}, f32[1,32,512]{2,1,0:T(8,128)S(1)}) fusion(f32[3,32,512]{2,1,0:T(8,128)S(1)} %fusion.20, f32[]{:T(128)} %bitcast.16, f32[]{:T(128)} %bitcast.15, f32[]{:T(128)} %bitcast.14, f32[]{:T(128)} %bitcast.19, f32[]{:T(128)} %bitcast.18, f32[]{:T(128)} %bitcast.17, ...), kind=kLoop, calls=%fused_computation.120 | loop fusion | flops 245760 | bytes 393252 | tf_op jit(solution)/shard_map/add | solution.py:93
  34.4 2.5 %all-to-all-done = f32[4,1,147456]{2,1,0:T(1,128)S(1)} async-done(((f32[4,1,147456]{2,1,0:T(1,128)}), f32[4,1,147456]{2,1,0:T(1,128)S(1)}, u32[]{:S(2)}, u32[]{:S(2)}) %all-to-all-start) | async-done | bytes 2359328 | tf_op jit(solution)/shard_map/all_to_all | solution.py:33
  36.8 4.9 %reduce_sum.207 = f32[147456]{0:T(1024)S(1)} reduce(f32[4,1,147456]{2,1,0:T(1,128)S(1)} %all-to-all-done, f32[]{:T(128)} %constant.5.clone.1), dimensions={0,1}, to_apply=%region_9.0 | reduce | flops 442368 | bytes 2949124 | tf_op jit(solution)/shard_map/reduce_sum | solution.py:37
  42.0 8.2 %collective-permute-start.6 = (f32[3,32,1]{2,1,0:T(8,128)S(1)}, f32[3,32,1]{2,1,0:T(8,128)S(1)}, u32[]{:S(2)}, u32[]{:S(2)}) collective-permute-start(f32[3,32,1]{2,1,0:T(8,128)S(1)} %get-tuple-element.57), channel_id=1, source_target_pairs={{1,0},{2,1},{3,2},{4,3},{5,4},{6,5},{7,6},{9,8},{10,9},{11,10},{12... | collective-permute-start | bytes 1160 | tf_op jit(solution)/shard_map/ppermute | solution.py:20
  50.3 3.0 %collective-permute-start.7 = (f32[3,32,1]{2,1,0:T(8,128)S(1)}, f32[3,32,1]{2,1,0:T(8,128)S(1)}, u32[]{:S(2)}, u32[]{:S(2)}) collective-permute-start(f32[3,32,1]{2,1,0:T(8,128)S(1)} %get-tuple-element.58), channel_id=1, source_target_pairs={{0,1},{1,2},{2,3},{3,4},{4,5},{5,6},{6,7},{8,9},{9,10},{10,11},{11... | collective-permute-start | bytes 1160 | tf_op jit(solution)/shard_map/ppermute | solution.py:19
  53.3 1.3 collective-permute-start.4
  54.6 4.2 %collective-permute-start.5 = (f32[3,1,512]{2,1,0:T(1,128)S(1)}, f32[3,1,512]{2,1,0:T(1,128)S(1)}, u32[]{:S(2)}, u32[]{:S(2)}) collective-permute-start(f32[3,1,512]{2,1,0:T(1,128)S(1)} %get-tuple-element.59), channel_id=1, source_target_pairs={{0,8},{8,16},{16,24},{24,32},{32,40},{40,48},{48,56},{56,64},{64,7... | collective-permute-start | bytes 18440 | tf_op jit(solution)/shard_map/ppermute | solution.py:19
  58.9 0.6 dynamic-slice_reduce_fusion.5
  59.8 5.6 %multiply_add_fusion.10 = (f32[1,32,512]{2,1,0:T(8,128)S(1)}, f32[1,32,512]{2,1,0:T(8,128)S(1)}, f32[1,32,512]{2,1,0:T(8,128)S(1)}) fusion(f32[3,32,512]{2,1,0:T(8,128)S(1)} %fusion.14, f32[]{:T(128)} %bitcast.16, f32[]{:T(128)} %bitcast.15, f32[]{:T(128)} %bitcast.14, f32[]{:T(128)} %bitcast.19, f32[]{:T(128)} %bitcast.18, f32[]{:T(128)} %bitcast.17, ...), kind=kLoop, calls=%fused_computation.117 | loop fusion | flops 245760 | bytes 393252 | tf_op jit(solution)/shard_map/add | solution.py:93
  65.5 0.7 dynamic-slice_reduce_fusion.4
  66.2 1.3 pad_maximum_fusion.26
  67.5 9.0 %all_to_all.42 = f32[8,1,2]{2,1,0:T(1,128)S(1)} all-to-all(f32[8,1,2]{2,1,0:T(1,128)S(1)} %broadcast_in_dim.30), channel_id=1, replica_groups=mesh['ens'=4,'lat'=16,'lon_0'=4,'lon_1'=2] {'lon_0','lon_1'}, dimensions={0} | all-to-all | bytes 128 | tf_op jit(solution)/shard_map/all_to_all | solution.py:33
  76.5 31.1 %all_to_all.43 = f32[64,1,2]{2,1,0:T(1,128)S(1)} all-to-all(f32[64,1,2]{2,1,0:T(1,128)S(1)} %broadcast_in_dim.31), channel_id=1, replica_groups=mesh['ens'=4,'lat'=16,'lon_0'=4,'lon_1'=2] {'ens','lat'}, dimensions={0} | all-to-all | bytes 1024 | tf_op jit(solution)/shard_map/all_to_all | solution.py:33
  107.7 0.6 fusion.52
  109.7 1.3 collective-permute-start.8
  111.0 4.0 %collective-permute-start.9 = (f32[3,1,512]{2,1,0:T(1,128)S(1)}, f32[3,1,512]{2,1,0:T(1,128)S(1)}, u32[]{:S(2)}, u32[]{:S(2)}) collective-permute-start(f32[3,1,512]{2,1,0:T(1,128)S(1)} %get-tuple-element.52), channel_id=1, source_target_pairs={{0,8},{8,16},{16,24},{24,32},{32,40},{40,48},{48,56},{56,64},{64,7... | collective-permute-start | bytes 18440 | tf_op jit(solution)/shard_map/ppermute | solution.py:19
  115.0 4.6 %collective-permute-start.10 = (f32[3,32,1]{2,1,0:T(8,128)S(1)}, f32[3,32,1]{2,1,0:T(8,128)S(1)}, u32[]{:S(2)}, u32[]{:S(2)}) collective-permute-start(f32[3,32,1]{2,1,0:T(8,128)S(1)} %get-tuple-element.50), channel_id=1, source_target_pairs={{1,0},{2,1},{3,2},{4,3},{5,4},{6,5},{7,6},{9,8},{10,9},{11,10},{12... | collective-permute-start | bytes 1160 | tf_op jit(solution)/shard_map/ppermute | solution.py:20
  119.6 2.1 collective-permute-start.11
  121.7 0.7 dynamic-slice_reduce_fusion.3
  122.4 0.5 collective-permute-done.11
  123.1 5.6 %multiply_add_fusion.7 = (f32[1,32,512]{2,1,0:T(8,128)S(1)}, f32[1,32,512]{2,1,0:T(8,128)S(1)}, f32[1,32,512]{2,1,0:T(8,128)S(1)}) fusion(f32[3,32,512]{2,1,0:T(8,128)S(1)} %fusion.8, f32[]{:T(128)} %bitcast.16, f32[]{:T(128)} %bitcast.15, f32[]{:T(128)} %bitcast.14, f32[]{:T(128)} %bitcast.19, f32[]{:T(128)} %bitcast.18, f32[]{:T(128)} %bitcast.17, ...), kind=kLoop, calls=%fused_computation.111 | loop fusion | flops 245760 | bytes 393252 | tf_op jit(solution)/shard_map/add | solution.py:93
  128.8 0.7 dynamic-slice_reduce_fusion.2
  129.5 1.4 pad_maximum_fusion.27
  130.9 9.0 %all_to_all.44 = f32[8,1,2]{2,1,0:T(1,128)S(1)} all-to-all(f32[8,1,2]{2,1,0:T(1,128)S(1)} %broadcast_in_dim.32), channel_id=1, replica_groups=mesh['ens'=4,'lat'=16,'lon_0'=4,'lon_1'=2] {'lon_0','lon_1'}, dimensions={0} | all-to-all | bytes 128 | tf_op jit(solution)/shard_map/all_to_all | solution.py:33
  139.9 18.1 %all_to_all.45 = f32[64,1,2]{2,1,0:T(1,128)S(1)} all-to-all(f32[64,1,2]{2,1,0:T(1,128)S(1)} %broadcast_in_dim.33), channel_id=1, replica_groups=mesh['ens'=4,'lat'=16,'lon_0'=4,'lon_1'=2] {'ens','lat'}, dimensions={0} | all-to-all | bytes 1024 | tf_op jit(solution)/shard_map/all_to_all | solution.py:33
  158.1 0.6 fusion.51
  163.5 4.0 %collective-permute-start.14 = (f32[3,32,1]{2,1,0:T(8,128)S(1)}, f32[3,32,1]{2,1,0:T(8,128)S(1)}, u32[]{:S(2)}, u32[]{:S(2)}) collective-permute-start(f32[3,32,1]{2,1,0:T(8,128)S(1)} %get-tuple-element.43), channel_id=1, source_target_pairs={{1,0},{2,1},{3,2},{4,3},{5,4},{6,5},{7,6},{9,8},{10,9},{11,10},{12... | collective-permute-start | bytes 1160 | tf_op jit(solution)/shard_map/ppermute | solution.py:20
  167.5 2.1 collective-permute-start.15
  169.6 1.3 collective-permute-start.12
  170.9 4.0 %collective-permute-start.13 = (f32[3,1,512]{2,1,0:T(1,128)S(1)}, f32[3,1,512]{2,1,0:T(1,128)S(1)}, u32[]{:S(2)}, u32[]{:S(2)}) collective-permute-start(f32[3,1,512]{2,1,0:T(1,128)S(1)} %get-tuple-element.45), channel_id=1, source_target_pairs={{0,8},{8,16},{16,24},{24,32},{32,40},{40,48},{48,56},{56,64},{64,7... | collective-permute-start | bytes 18440 | tf_op jit(solution)/shard_map/ppermute | solution.py:19
  175.0 0.7 collective-permute-done.13
  175.9 5.6 %multiply_add_fusion.4 = (f32[1,32,512]{2,1,0:T(8,128)S(1)}, f32[1,32,512]{2,1,0:T(8,128)S(1)}, f32[1,32,512]{2,1,0:T(8,128)S(1)}) fusion(f32[3,32,512]{2,1,0:T(8,128)S(1)} %fusion.2, f32[]{:T(128)} %bitcast.16, f32[]{:T(128)} %bitcast.15, f32[]{:T(128)} %bitcast.14, f32[]{:T(128)} %bitcast.19, f32[]{:T(128)} %bitcast.18, f32[]{:T(128)} %bitcast.17, ...), kind=kLoop, calls=%fused_computation.105 | loop fusion | flops 245760 | bytes 393252 | tf_op jit(solution)/shard_map/add | solution.py:93
  181.6 0.6 dynamic-slice_reduce_fusion
  182.2 1.3 pad_maximum_fusion.28
  183.5 8.4 %all_to_all.46 = f32[8,1,2]{2,1,0:T(1,128)S(1)} all-to-all(f32[8,1,2]{2,1,0:T(1,128)S(1)} %broadcast_in_dim.34), channel_id=1, replica_groups=mesh['ens'=4,'lat'=16,'lon_0'=4,'lon_1'=2] {'lon_0','lon_1'}, dimensions={0} | all-to-all | bytes 128 | tf_op jit(solution)/shard_map/all_to_all | solution.py:33
  191.9 21.0 %all_to_all.47 = f32[64,1,2]{2,1,0:T(1,128)S(1)} all-to-all(f32[64,1,2]{2,1,0:T(1,128)S(1)} %broadcast_in_dim.35), channel_id=1, replica_groups=mesh['ens'=4,'lat'=16,'lon_0'=4,'lon_1'=2] {'ens','lat'}, dimensions={0} | all-to-all | bytes 1024 | tf_op jit(solution)/shard_map/all_to_all | solution.py:33
  213.0 0.6 fusion.50
  217.4 0.8 multiply_add_fusion.1
  (72 shorter events, 2.7 us)
Async XLA Ops:
  7.9 5.1 %copy-start.1 = (f32[3,32,512]{2,1,0:T(8,128)S(1)}, f32[3,32,512]{2,1,0:T(8,128)}, u32[]{:S(2)}) copy-start(f32[3,32,512]{2,1,0:T(8,128)} %param.5) | copy-start | bytes 589828
  7.9 19.9 %copy-start.2 = (f32[3,3]{1,0:T(4,128)S(1)}, f32[3,3]{1,0:T(4,128)}, u32[]{:S(2)}) copy-start(f32[3,3]{1,0:T(4,128)} %param.6) | copy-start | bytes 112
  7.9 28.9 %all-to-all-start = ((f32[4,1,147456]{2,1,0:T(1,128)}), f32[4,1,147456]{2,1,0:T(1,128)S(1)}, u32[]{:S(2)}, u32[]{:S(2)}) async-start(f32[4,1,147456]{2,1,0:T(1,128)} %broadcast_in_dim.14), calls=%async_computation | async-start | bytes 4718592 | tf_op jit(solution)/shard_map/all_to_all | solution.py:33
  13.1 15.3 %collective-permute-start.2 = (f32[3,32,1]{2,1,0:T(8,128)S(1)}, f32[3,32,1]{2,1,0:T(8,128)S(1)}, u32[]{:S(2)}, u32[]{:S(2)}) collective-permute-start(f32[3,32,1]{2,1,0:T(8,128)S(1)} %get-tuple-element.64), channel_id=1, source_target_pairs={{1,0},{2,1},{3,2},{4,3},{5,4},{6,5},{7,6},{9,8},{10,9},{11,10},{12... | collective-permute-start | bytes 1160 | tf_op jit(solution)/shard_map/ppermute | solution.py:20
  20.5 7.9 %collective-permute-start.3 = (f32[3,32,1]{2,1,0:T(8,128)S(1)}, f32[3,32,1]{2,1,0:T(8,128)S(1)}, u32[]{:S(2)}, u32[]{:S(2)}) collective-permute-start(f32[3,32,1]{2,1,0:T(8,128)S(1)} %get-tuple-element.65), channel_id=1, source_target_pairs={{0,1},{1,2},{2,3},{3,4},{4,5},{5,6},{6,7},{8,9},{9,10},{10,11},{11... | collective-permute-start | bytes 1160 | tf_op jit(solution)/shard_map/ppermute | solution.py:19
  22.5 6.0 %collective-permute-start = (f32[3,1,512]{2,1,0:T(1,128)S(1)}, f32[3,1,512]{2,1,0:T(1,128)S(1)}, u32[]{:S(2)}, u32[]{:S(2)}) collective-permute-start(f32[3,1,512]{2,1,0:T(1,128)S(1)} %get-tuple-element.67), channel_id=1, source_target_pairs={{8,0},{16,8},{24,16},{32,24},{40,32},{48,40},{56,48},{64,56},{72,6... | collective-permute-start | bytes 18440 | tf_op jit(solution)/shard_map/ppermute | solution.py:20
  23.8 4.8 %collective-permute-start.1 = (f32[3,1,512]{2,1,0:T(1,128)S(1)}, f32[3,1,512]{2,1,0:T(1,128)S(1)}, u32[]{:S(2)}, u32[]{:S(2)}) collective-permute-start(f32[3,1,512]{2,1,0:T(1,128)S(1)} %get-tuple-element.66), channel_id=1, source_target_pairs={{0,8},{8,16},{16,24},{24,32},{32,40},{40,48},{48,56},{56,64},{64,7... | collective-permute-start | bytes 18440 | tf_op jit(solution)/shard_map/ppermute | solution.py:19
  28.7 13.1 %copy-start = (f32[3,32,512]{2,1,0:T(8,128)S(1)}, f32[3,32,512]{2,1,0:T(8,128)}, u32[]{:S(2)}) copy-start(f32[3,32,512]{2,1,0:T(8,128)} %param.7) | copy-start | bytes 589828
  42.0 17.5 %collective-permute-start.6 = (f32[3,32,1]{2,1,0:T(8,128)S(1)}, f32[3,32,1]{2,1,0:T(8,128)S(1)}, u32[]{:S(2)}, u32[]{:S(2)}) collective-permute-start(f32[3,32,1]{2,1,0:T(8,128)S(1)} %get-tuple-element.57), channel_id=1, source_target_pairs={{1,0},{2,1},{3,2},{4,3},{5,4},{6,5},{7,6},{9,8},{10,9},{11,10},{12... | collective-permute-start | bytes 1160 | tf_op jit(solution)/shard_map/ppermute | solution.py:20
  50.3 9.3 %collective-permute-start.7 = (f32[3,32,1]{2,1,0:T(8,128)S(1)}, f32[3,32,1]{2,1,0:T(8,128)S(1)}, u32[]{:S(2)}, u32[]{:S(2)}) collective-permute-start(f32[3,32,1]{2,1,0:T(8,128)S(1)} %get-tuple-element.58), channel_id=1, source_target_pairs={{0,1},{1,2},{2,3},{3,4},{4,5},{5,6},{6,7},{8,9},{9,10},{10,11},{11... | collective-permute-start | bytes 1160 | tf_op jit(solution)/shard_map/ppermute | solution.py:19
  53.3 6.3 %collective-permute-start.4 = (f32[3,1,512]{2,1,0:T(1,128)S(1)}, f32[3,1,512]{2,1,0:T(1,128)S(1)}, u32[]{:S(2)}, u32[]{:S(2)}) collective-permute-start(f32[3,1,512]{2,1,0:T(1,128)S(1)} %get-tuple-element.60), channel_id=1, source_target_pairs={{8,0},{16,8},{24,16},{32,24},{40,32},{48,40},{56,48},{64,56},{72,6... | collective-permute-start | bytes 18440 | tf_op jit(solution)/shard_map/ppermute | solution.py:20
  54.6 5.0 %collective-permute-start.5 = (f32[3,1,512]{2,1,0:T(1,128)S(1)}, f32[3,1,512]{2,1,0:T(1,128)S(1)}, u32[]{:S(2)}, u32[]{:S(2)}) collective-permute-start(f32[3,1,512]{2,1,0:T(1,128)S(1)} %get-tuple-element.59), channel_id=1, source_target_pairs={{0,8},{8,16},{16,24},{24,32},{32,40},{40,48},{48,56},{56,64},{64,7... | collective-permute-start | bytes 18440 | tf_op jit(solution)/shard_map/ppermute | solution.py:19
  109.7 13.2 %collective-permute-start.8 = (f32[3,1,512]{2,1,0:T(1,128)S(1)}, f32[3,1,512]{2,1,0:T(1,128)S(1)}, u32[]{:S(2)}, u32[]{:S(2)}) collective-permute-start(f32[3,1,512]{2,1,0:T(1,128)S(1)} %get-tuple-element.53), channel_id=1, source_target_pairs={{8,0},{16,8},{24,16},{32,24},{40,32},{48,40},{56,48},{64,56},{72,6... | collective-permute-start | bytes 18440 | tf_op jit(solution)/shard_map/ppermute | solution.py:20
  111.0 11.9 %collective-permute-start.9 = (f32[3,1,512]{2,1,0:T(1,128)S(1)}, f32[3,1,512]{2,1,0:T(1,128)S(1)}, u32[]{:S(2)}, u32[]{:S(2)}) collective-permute-start(f32[3,1,512]{2,1,0:T(1,128)S(1)} %get-tuple-element.52), channel_id=1, source_target_pairs={{0,8},{8,16},{16,24},{24,32},{32,40},{40,48},{48,56},{56,64},{64,7... | collective-permute-start | bytes 18440 | tf_op jit(solution)/shard_map/ppermute | solution.py:19
  115.0 7.4 %collective-permute-start.10 = (f32[3,32,1]{2,1,0:T(8,128)S(1)}, f32[3,32,1]{2,1,0:T(8,128)S(1)}, u32[]{:S(2)}, u32[]{:S(2)}) collective-permute-start(f32[3,32,1]{2,1,0:T(8,128)S(1)} %get-tuple-element.50), channel_id=1, source_target_pairs={{1,0},{2,1},{3,2},{4,3},{5,4},{6,5},{7,6},{9,8},{10,9},{11,10},{12... | collective-permute-start | bytes 1160 | tf_op jit(solution)/shard_map/ppermute | solution.py:20
  119.6 3.3 %collective-permute-start.11 = (f32[3,32,1]{2,1,0:T(8,128)S(1)}, f32[3,32,1]{2,1,0:T(8,128)S(1)}, u32[]{:S(2)}, u32[]{:S(2)}) collective-permute-start(f32[3,32,1]{2,1,0:T(8,128)S(1)} %get-tuple-element.51), channel_id=1, source_target_pairs={{0,1},{1,2},{2,3},{3,4},{4,5},{5,6},{6,7},{8,9},{9,10},{10,11},{11... | collective-permute-start | bytes 1160 | tf_op jit(solution)/shard_map/ppermute | solution.py:19
  163.5 11.5 %collective-permute-start.14 = (f32[3,32,1]{2,1,0:T(8,128)S(1)}, f32[3,32,1]{2,1,0:T(8,128)S(1)}, u32[]{:S(2)}, u32[]{:S(2)}) collective-permute-start(f32[3,32,1]{2,1,0:T(8,128)S(1)} %get-tuple-element.43), channel_id=1, source_target_pairs={{1,0},{2,1},{3,2},{4,3},{5,4},{6,5},{7,6},{9,8},{10,9},{11,10},{12... | collective-permute-start | bytes 1160 | tf_op jit(solution)/shard_map/ppermute | solution.py:20
  167.5 7.5 %collective-permute-start.15 = (f32[3,32,1]{2,1,0:T(8,128)S(1)}, f32[3,32,1]{2,1,0:T(8,128)S(1)}, u32[]{:S(2)}, u32[]{:S(2)}) collective-permute-start(f32[3,32,1]{2,1,0:T(8,128)S(1)} %get-tuple-element.44), channel_id=1, source_target_pairs={{0,1},{1,2},{2,3},{3,4},{4,5},{5,6},{6,7},{8,9},{9,10},{10,11},{11... | collective-permute-start | bytes 1160 | tf_op jit(solution)/shard_map/ppermute | solution.py:19
  169.6 5.4 %collective-permute-start.12 = (f32[3,1,512]{2,1,0:T(1,128)S(1)}, f32[3,1,512]{2,1,0:T(1,128)S(1)}, u32[]{:S(2)}, u32[]{:S(2)}) collective-permute-start(f32[3,1,512]{2,1,0:T(1,128)S(1)} %get-tuple-element.46), channel_id=1, source_target_pairs={{8,0},{16,8},{24,16},{32,24},{40,32},{48,40},{56,48},{64,56},{72,6... | collective-permute-start | bytes 18440 | tf_op jit(solution)/shard_map/ppermute | solution.py:20
  170.9 4.8 %collective-permute-start.13 = (f32[3,1,512]{2,1,0:T(1,128)S(1)}, f32[3,1,512]{2,1,0:T(1,128)S(1)}, u32[]{:S(2)}, u32[]{:S(2)}) collective-permute-start(f32[3,1,512]{2,1,0:T(1,128)S(1)} %get-tuple-element.45), channel_id=1, source_target_pairs={{0,8},{8,16},{16,24},{24,32},{32,40},{40,48},{48,56},{56,64},{64,7... | collective-permute-start | bytes 18440 | tf_op jit(solution)/shard_map/ppermute | solution.py:19
where the time goes:
time: 220 us; the launch traced here: 218 us
  blocking collectives  96.5 us (44%)
  starting transfers between devices  59.7 us (27%)
  other arithmetic  42.1 us (19%)
  between operations  10.2 us (5%)
  local copies, waits for them, and re-layouts  5.89 us (3%)
  waiting for transfers between devices  3.69 us (2%)
    all_to_all x6, blocking collectives, sent_to_all(): return lax.all_to_all(copies, axis, split_axis=0, concat_axis=0, tiled=True)  96.5 us
    ppermute x8, starting transfers between devices, with_halo(): lax.ppermute(first, axis, [(b, a) for a, b in up])  29.3 us
    ppermute x8, starting transfers between devices, with_halo(): lax.ppermute(last, axis, up)  25.2 us
    add x4, other arithmetic, mix_rows(): coupling[0, 0] * laplace_term[0] + coupling[0, 1] * laplace_term[1]  22.4 us
    reduce_sum x7, other arithmetic, over_copies(): return sent_to_all(value, axis).sum(axis=0)  5.26 us
    all_to_all x1, starting transfers between devices, sent_to_all(): return lax.all_to_all(copies, axis, split_axis=0, concat_axis=0, tiled=True)  5.13 us
  transfers between devices with their start and end apart: 17, of which 4 were waited for; matrix products, arithmetic and copies ran while one was open for 4% of the time, Pallas kernels for 0%

commit v1 on v0

--- a/solution.py
+++ b/solution.py
@@ -6,6 +6,7 @@
 
 ITERS = 3
 LON = ("lon_0", "lon_1")
+SCALE = 2.0**-10
 
 
 def with_halo(value, sides, width):
@@ -45,18 +46,32 @@
     return tuple((so_far[b:e].reshape(a.shape) for a, b, e in zip(arrays, ends, ends[1:])))
 
 
-def one_axis_at_a_time(value, axes):
-    far, near = axes
-    nearer = over_copies(value, near)
-    return over_copies(nearer, far)
+def moments_total(products):
+    packed = jnp.stack([jnp.sum(p) for p in products])[None]
+    return over_copies(over_copies(packed, LON), "lat")[0]
 
 
-def packed_total(arrays, axis):
-    ends = [0]
-    for a in arrays:
-        ends.append(ends[-1] + a.size)
-    so_far = one_axis_at_a_time(jnp.concatenate([a.ravel() for a in arrays]), axis)
-    return tuple((so_far[b:e].reshape(a.shape) for a, b, e in zip(arrays, ends, ends[1:])))
+def krylov_weights(m):
+    def inner(p, q, shift):
+        return sum(p[i] * q[j] * m[i + j + shift] for i in range(len(p)) for j in range(len(q)))
+
+    def combine(p, factor, q):
+        n = max(len(p), len(q))
+        p, q = (list(c) + [jnp.zeros((), m.dtype)] * (n - len(c)) for c in (p, q))
+        return [x + factor * y for x, y in zip(p, q)]
+
+    one, zero = jnp.ones((), m.dtype), jnp.zeros((), m.dtype)
+    weights, residual, direction = [zero], [one], [one]
+    norm_now = m[0]
+    for iteration in range(ITERS):
+        step_size = norm_now / inner(direction, direction, 1)
+        weights = combine(weights, step_size, direction)
+        if iteration + 1 < ITERS:
+            residual = combine(residual, -step_size, [zero] + direction)
+            norm_next = inner(residual, residual, 0)
+            direction = combine(residual, norm_next / norm_now, direction)
+            norm_now = norm_next
+    return [SCALE * w for w in weights]
 
 
 def gev_terms(maxima, latent):
@@ -124,46 +139,22 @@
     )
 
 
-def quarter_sum(values):
-    rows = values.reshape(-1, values.shape[-1])
-    count = rows.shape[0] // lax.axis_size("ens")
-    start = lax.axis_index("ens") * count
-    return jnp.sum(lax.dynamic_slice_in_dim(rows, start, count, 0))
-
-
 def per_device(maxima, latent, coupling, local_precision):
     scores_local, hessian_local = gev_terms(maxima, latent)
     scores, hessian = together((scores_local, hessian_local), "ens")
 
     def operate(vector):
-        return prior_apply(vector, coupling, local_precision, tile_pad) + hessian_apply(
-            vector, hessian
+        return SCALE * (
+            prior_apply(vector, coupling, local_precision, tile_pad)
+            + hessian_apply(vector, hessian)
         )
 
-    def two_products(residual, image):
-        return packed_total(
-            (quarter_sum(residual * residual), quarter_sum(residual * image)),
-            (("ens", "lat"), ("lon_0", "lon_1")),
-        )
-
-    solution = latent
-    residual = scores - prior_apply(latent, coupling, local_precision, tile_pad)
-    image = operate(residual)
-    norm_now, product = two_products(residual, image)
-    step_size = norm_now / product
-    direction, along = (residual, image)
-    for iteration in range(ITERS):
-        solution = solution + step_size * direction
-        residual = residual - step_size * along
-        if iteration + 1 < ITERS:
-            image = operate(residual)
-            norm_next, product = two_products(residual, image)
-            factor = norm_next / norm_now
-            step_size = norm_next / (product - factor * norm_next / step_size)
-            direction = residual + factor * direction
-            along = image + factor * along
-            norm_now = norm_next
-    return solution
+    basis = [scores - prior_apply(latent, coupling, local_precision, tile_pad)]
+    for _ in range(ITERS):
+        basis.append(operate(basis[-1]))
+    products = [basis[k // 2] * basis[k - k // 2] for k in range(2 * ITERS)]
+    weights = krylov_weights(moments_total(products))
+    return latent + weights[0] * basis[0] + weights[1] * basis[1] + weights[2] * basis[2]
 
 
 def solution(mesh):

time: 220 us -> 161 us (0.73)
  blocking collectives: 96.5 us -> 38.6 us
  other arithmetic: 42.1 us -> 35.1 us
  between operations: 10.2 us -> 13.8 us
  local copies, waits for them, and re-layouts: 5.89 us -> 8.52 us
    all_to_all x6 -> x2, blocking collectives: 96.5 us -> 38.6 us  [sent_to_all(): return lax.all_to_all(copies, axis, split_axis=0, concat_axis=0, tiled=True)]
    ppermute x8, starting transfers between devices: 29.3 us -> 24.9 us  [with_halo(): lax.ppermute(first, axis, [(b, a) for a, b in up])]
    concatenate x3 -> x0, other arithmetic: 3.99 us -> none  [packed_total(): jnp.concatenate([a.ravel() for a in arrays])]
    another operation x0 -> x1, local copies, waits for them, and re-layouts: none -> 3.85 us  [moments_total(): packed = jnp.stack([jnp.sum(p) for p in products])[None]]
    ppermute x8, starting transfers between devices: 25.2 us -> 28.8 us  [with_halo(): lax.ppermute(last, axis, up)]
    reduce_sum x5 -> x1, other arithmetic: 3.31 us -> 0.84 us  [moments_total(): packed = jnp.stack([jnp.sum(p) for p in products])[None]]
    reduce_sum x7 -> x3, other arithmetic: 5.26 us -> 4.99 us  [over_copies(): return sent_to_all(value, axis).sum(axis=0)]
  transfers between devices with their start and end apart: 17 -> 17, of which waited for: 4 -> 5; matrix products, arithmetic and copies ran while one was open for 4% -> 4% of each run, Pallas kernels for 0% -> 0%
where the time goes in v1:
time: 161 us; the launch traced here: 159 us
  starting transfers between devices  58.9 us (37%)
  blocking collectives  38.6 us (24%)
  other arithmetic  35.1 us (22%)
  between operations  13.8 us (9%)
  local copies, waits for them, and re-layouts  8.52 us (5%)
  waiting for transfers between devices  4.42 us (3%)
    all_to_all x2, blocking collectives, sent_to_all(): return lax.all_to_all(copies, axis, split_axis=0, concat_axis=0, tiled=True)  38.6 us
    ppermute x8, starting transfers between devices, with_halo(): lax.ppermute(last, axis, up)  28.8 us
    ppermute x8, starting transfers between devices, with_halo(): lax.ppermute(first, axis, [(b, a) for a, b in up])  24.9 us
    add x4, other arithmetic, mix_rows(): coupling[0, 0] * laplace_term[0] + coupling[0, 1] * laplace_term[1]  22.4 us
    all_to_all x1, starting transfers between devices, sent_to_all(): return lax.all_to_all(copies, axis, split_axis=0, concat_axis=0, tiled=True)  5.13 us
    reduce_sum x3, other arithmetic, over_copies(): return sent_to_all(value, axis).sum(axis=0)  4.99 us
    another operation x1, local copies, waits for them, and re-layouts, moments_total(): packed = jnp.stack([jnp.sum(p) for p in products])[None]  3.85 us
  transfers between devices with their start and end apart: 17, of which 5 were waited for; matrix products, arithmetic and copies ran while one was open for 4% of the time, Pallas kernels for 0%

profile of v1, /device:TPU:1, one launch (start us, length us, event | category | flops | bytes accessed | tf_op | source)
XLA Modules:
  0.0 159.4 jit_solution(2423262226946749055)
XLA Ops:
  0.0 0.9 multiply_bitcast_fusion
  0.9 2.9 %subtract_multiply_fusion = (f32[32,32,512]{2,1,0:T(8,128)S(1)}, f32[32,32,512]{2,1,0:T(8,128)S(1)}, f32[32,32,512]{2,1,0:T(8,128)S(1)}) fusion(f32[32,512]{1,0:T(8,128)S(1)} %get-tuple-element.70, f32[32,512]{1,0:T(8,128)S(1)} %get-tuple-element.71, f32[32,512]{1,0:T(8,128)S(1)} %get-tuple-element.72, f32[32,32,512]{2,1,0:T(8,128)} %param.4, ...), kind=kLoop, calls=%fused_computation.6 | loop fusion | flops 8912896 | bytes 8716288 | tf_op jit(solution)/shard_map/mul | solution.py:88
  3.9 1.1 fusion.33
  5.1 0.1 copy.22
  5.3 2.6 %broadcast_in_dim.6 = f32[4,1,147456]{2,1,0:T(1,128)} broadcast(f32[147456]{0:T(1024)S(1)} %pad_maximum_fusion), dimensions={2} | broadcast | bytes 2949120 | tf_op jit(solution)/shard_map/broadcast_in_dim | solution.py:33
  7.9 5.1 %all-to-all-start = ((f32[4,1,147456]{2,1,0:T(1,128)}), f32[4,1,147456]{2,1,0:T(1,128)S(1)}, u32[]{:S(2)}, u32[]{:S(2)}) async-start(f32[4,1,147456]{2,1,0:T(1,128)} %broadcast_in_dim.6), calls=%async_computation | async-start | bytes 4718592 | tf_op jit(solution)/shard_map/all_to_all | solution.py:34
  13.0 0.1 fusion.44
  13.1 7.4 %collective-permute-start.2 = (f32[3,32,1]{2,1,0:T(8,128)S(1)}, f32[3,32,1]{2,1,0:T(8,128)S(1)}, u32[]{:S(2)}, u32[]{:S(2)}) collective-permute-start(f32[3,32,1]{2,1,0:T(8,128)S(1)} %get-tuple-element.66), channel_id=1, source_target_pairs={{1,0},{2,1},{3,2},{4,3},{5,4},{6,5},{7,6},{9,8},{10,9},{11,10},{12... | collective-permute-start | bytes 1160 | tf_op jit(solution)/shard_map/ppermute | solution.py:21
  20.5 1.9 %collective-permute-start.3 = (f32[3,32,1]{2,1,0:T(8,128)S(1)}, f32[3,32,1]{2,1,0:T(8,128)S(1)}, u32[]{:S(2)}, u32[]{:S(2)}) collective-permute-start(f32[3,32,1]{2,1,0:T(8,128)S(1)} %get-tuple-element.67), channel_id=1, source_target_pairs={{0,1},{1,2},{2,3},{3,4},{4,5},{5,6},{6,7},{8,9},{9,10},{10,11},{11... | collective-permute-start | bytes 1160 | tf_op jit(solution)/shard_map/ppermute | solution.py:20
  22.5 1.3 collective-permute-start
  23.8 4.0 %collective-permute-start.1 = (f32[3,1,512]{2,1,0:T(1,128)S(1)}, f32[3,1,512]{2,1,0:T(1,128)S(1)}, u32[]{:S(2)}, u32[]{:S(2)}) collective-permute-start(f32[3,1,512]{2,1,0:T(1,128)S(1)} %get-tuple-element.68), channel_id=1, source_target_pairs={{0,8},{8,16},{16,24},{24,32},{32,40},{40,48},{48,56},{56,64},{64,7... | collective-permute-start | bytes 18440 | tf_op jit(solution)/shard_map/ppermute | solution.py:20
  27.8 0.7 fusion.46
  28.5 0.2 fusion.20
  28.7 5.6 %multiply_add_fusion.13 = (f32[1,32,512]{2,1,0:T(8,128)S(1)}, f32[1,32,512]{2,1,0:T(8,128)S(1)}, f32[1,32,512]{2,1,0:T(8,128)S(1)}) fusion(f32[3,32,512]{2,1,0:T(8,128)S(1)} %fusion.20, f32[]{:T(128)} %bitcast.16, f32[]{:T(128)} %bitcast.15, f32[]{:T(128)} %bitcast.14, f32[]{:T(128)} %bitcast.19, f32[]{:T(128)} %bitcast.18, f32[]{:T(128)} %bitcast.17, ...), kind=kLoop, calls=%fused_computation.127 | loop fusion | flops 245760 | bytes 393252 | tf_op jit(solution)/shard_map/add | solution.py:108
  34.4 2.5 %all-to-all-done = f32[4,1,147456]{2,1,0:T(1,128)S(1)} async-done(((f32[4,1,147456]{2,1,0:T(1,128)}), f32[4,1,147456]{2,1,0:T(1,128)S(1)}, u32[]{:S(2)}, u32[]{:S(2)}) %all-to-all-start) | async-done | bytes 2359328 | tf_op jit(solution)/shard_map/all_to_all | solution.py:34
  36.8 4.9 %reduce_sum.173 = f32[147456]{0:T(1024)S(1)} reduce(f32[4,1,147456]{2,1,0:T(1,128)S(1)} %all-to-all-done, f32[]{:T(128)} %constant.6.clone.1), dimensions={0,1}, to_apply=%region_9.0 | reduce | flops 442368 | bytes 2949124 | tf_op jit(solution)/shard_map/reduce_sum | solution.py:38
  41.9 0.1 fusion.42
  42.0 8.2 %collective-permute-start.6 = (f32[3,32,1]{2,1,0:T(8,128)S(1)}, f32[3,32,1]{2,1,0:T(8,128)S(1)}, u32[]{:S(2)}, u32[]{:S(2)}) collective-permute-start(f32[3,32,1]{2,1,0:T(8,128)S(1)} %get-tuple-element.59), channel_id=1, source_target_pairs={{1,0},{2,1},{3,2},{4,3},{5,4},{6,5},{7,6},{9,8},{10,9},{11,10},{12... | collective-permute-start | bytes 1160 | tf_op jit(solution)/shard_map/ppermute | solution.py:21
  50.3 3.0 %collective-permute-start.7 = (f32[3,32,1]{2,1,0:T(8,128)S(1)}, f32[3,32,1]{2,1,0:T(8,128)S(1)}, u32[]{:S(2)}, u32[]{:S(2)}) collective-permute-start(f32[3,32,1]{2,1,0:T(8,128)S(1)} %get-tuple-element.60), channel_id=1, source_target_pairs={{0,1},{1,2},{2,3},{3,4},{4,5},{5,6},{6,7},{8,9},{9,10},{10,11},{11... | collective-permute-start | bytes 1160 | tf_op jit(solution)/shard_map/ppermute | solution.py:20
  53.3 1.3 collective-permute-start.4
  54.6 4.2 %collective-permute-start.5 = (f32[3,1,512]{2,1,0:T(1,128)S(1)}, f32[3,1,512]{2,1,0:T(1,128)S(1)}, u32[]{:S(2)}, u32[]{:S(2)}) collective-permute-start(f32[3,1,512]{2,1,0:T(1,128)S(1)} %get-tuple-element.61), channel_id=1, source_target_pairs={{0,8},{8,16},{16,24},{24,32},{32,40},{40,48},{48,56},{56,64},{64,7... | collective-permute-start | bytes 18440 | tf_op jit(solution)/shard_map/ppermute | solution.py:20
  59.0 0.5 collective-permute-done.5
  59.5 0.2 fusion.14
  59.7 5.6 %multiply_add_fusion.10 = (f32[1,32,512]{2,1,0:T(8,128)S(1)}, f32[1,32,512]{2,1,0:T(8,128)S(1)}, f32[1,32,512]{2,1,0:T(8,128)S(1)}) fusion(f32[3,32,512]{2,1,0:T(8,128)S(1)} %fusion.14, f32[]{:T(128)} %bitcast.16, f32[]{:T(128)} %bitcast.15, f32[]{:T(128)} %bitcast.14, f32[]{:T(128)} %bitcast.19, f32[]{:T(128)} %bitcast.18, f32[]{:T(128)} %bitcast.17, ...), kind=kLoop, calls=%fused_computation.124 | loop fusion | flops 245760 | bytes 393252 | tf_op jit(solution)/shard_map/add | solution.py:108
  65.3 0.1 broadcast_multiply_fusion.1
  65.4 0.1 fusion.40
  65.5 2.3 %collective-permute-start.10 = (f32[3,32,1]{2,1,0:T(8,128)S(1)}, f32[3,32,1]{2,1,0:T(8,128)S(1)}, u32[]{:S(2)}, u32[]{:S(2)}) collective-permute-start(f32[3,32,1]{2,1,0:T(8,128)S(1)} %get-tuple-element.52), channel_id=1, source_target_pairs={{1,0},{2,1},{3,2},{4,3},{5,4},{6,5},{7,6},{9,8},{10,9},{11,10},{12... | collective-permute-start | bytes 1160 | tf_op jit(solution)/shard_map/ppermute | solution.py:21
  67.8 3.3 %collective-permute-start.11 = (f32[3,32,1]{2,1,0:T(8,128)S(1)}, f32[3,32,1]{2,1,0:T(8,128)S(1)}, u32[]{:S(2)}, u32[]{:S(2)}) collective-permute-start(f32[3,32,1]{2,1,0:T(8,128)S(1)} %get-tuple-element.53), channel_id=1, source_target_pairs={{0,1},{1,2},{2,3},{3,4},{4,5},{5,6},{6,7},{8,9},{9,10},{10,11},{11... | collective-permute-start | bytes 1160 | tf_op jit(solution)/shard_map/ppermute | solution.py:20
  71.1 1.3 collective-permute-start.8
  72.4 4.5 %collective-permute-start.9 = (f32[3,1,512]{2,1,0:T(1,128)S(1)}, f32[3,1,512]{2,1,0:T(1,128)S(1)}, u32[]{:S(2)}, u32[]{:S(2)}) collective-permute-start(f32[3,1,512]{2,1,0:T(1,128)S(1)} %get-tuple-element.54), channel_id=1, source_target_pairs={{0,8},{8,16},{16,24},{24,32},{32,40},{40,48},{48,56},{56,64},{64,7... | collective-permute-start | bytes 18440 | tf_op jit(solution)/shard_map/ppermute | solution.py:20
  77.0 0.7 collective-permute-done.9
  77.6 0.2 fusion.8
  77.9 5.6 %multiply_add_fusion.7 = (f32[1,32,512]{2,1,0:T(8,128)S(1)}, f32[1,32,512]{2,1,0:T(8,128)S(1)}, f32[1,32,512]{2,1,0:T(8,128)S(1)}) fusion(f32[3,32,512]{2,1,0:T(8,128)S(1)} %fusion.8, f32[]{:T(128)} %bitcast.16, f32[]{:T(128)} %bitcast.15, f32[]{:T(128)} %bitcast.14, f32[]{:T(128)} %bitcast.19, f32[]{:T(128)} %bitcast.18, f32[]{:T(128)} %bitcast.17, ...), kind=kLoop, calls=%fused_computation.118 | loop fusion | flops 245760 | bytes 393252 | tf_op jit(solution)/shard_map/add | solution.py:108
  83.4 0.1 broadcast_multiply_fusion
  83.5 0.1 fusion.38
  83.6 1.9 %collective-permute-start.14 = (f32[3,32,1]{2,1,0:T(8,128)S(1)}, f32[3,32,1]{2,1,0:T(8,128)S(1)}, u32[]{:S(2)}, u32[]{:S(2)}) collective-permute-start(f32[3,32,1]{2,1,0:T(8,128)S(1)} %get-tuple-element.45), channel_id=1, source_target_pairs={{1,0},{2,1},{3,2},{4,3},{5,4},{6,5},{7,6},{9,8},{10,9},{11,10},{12... | collective-permute-start | bytes 1160 | tf_op jit(solution)/shard_map/ppermute | solution.py:21
  85.6 3.6 %collective-permute-start.15 = (f32[3,32,1]{2,1,0:T(8,128)S(1)}, f32[3,32,1]{2,1,0:T(8,128)S(1)}, u32[]{:S(2)}, u32[]{:S(2)}) collective-permute-start(f32[3,32,1]{2,1,0:T(8,128)S(1)} %get-tuple-element.46), channel_id=1, source_target_pairs={{0,1},{1,2},{2,3},{3,4},{4,5},{5,6},{6,7},{8,9},{9,10},{10,11},{11... | collective-permute-start | bytes 1160 | tf_op jit(solution)/shard_map/ppermute | solution.py:20
  89.2 1.3 collective-permute-start.12
  90.5 4.2 %collective-permute-start.13 = (f32[3,1,512]{2,1,0:T(1,128)S(1)}, f32[3,1,512]{2,1,0:T(1,128)S(1)}, u32[]{:S(2)}, u32[]{:S(2)}) collective-permute-start(f32[3,1,512]{2,1,0:T(1,128)S(1)} %get-tuple-element.47), channel_id=1, source_target_pairs={{0,8},{8,16},{16,24},{24,32},{32,40},{40,48},{48,56},{56,64},{64,7... | collective-permute-start | bytes 18440 | tf_op jit(solution)/shard_map/ppermute | solution.py:20
  94.8 0.7 collective-permute-done.13
  95.5 0.2 fusion.2
  95.7 5.6 %multiply_add_fusion.4 = (f32[1,32,512]{2,1,0:T(8,128)S(1)}, f32[1,32,512]{2,1,0:T(8,128)S(1)}, f32[1,32,512]{2,1,0:T(8,128)S(1)}) fusion(f32[3,32,512]{2,1,0:T(8,128)S(1)} %fusion.2, f32[]{:T(128)} %bitcast.16, f32[]{:T(128)} %bitcast.15, f32[]{:T(128)} %bitcast.14, f32[]{:T(128)} %bitcast.19, f32[]{:T(128)} %bitcast.18, f32[]{:T(128)} %bitcast.17, ...), kind=kLoop, calls=%fused_computation.112 | loop fusion | flops 245760 | bytes 393252 | tf_op jit(solution)/shard_map/add | solution.py:108
  101.3 0.8 fusion.30
  102.2 3.8 %stack.147 = f32[6]{0:T(128)S(1)} concatenate(f32[1]{0:T(128)} %bitcast.23, f32[1]{0:T(128)} %bitcast.30, f32[1]{0:T(128)} %bitcast.31, f32[1]{0:T(128)} %bitcast.38, f32[1]{0:T(128)} %bitcast.39, f32[1]{0:T(128)} %bitcast.46), dimensions={0} | concatenate | bytes 48 | tf_op jit(solution)/shard_map/stack | solution.py:50
  106.0 8.6 %all_to_all.16 = f32[8,1,6]{2,1,0:T(1,128)S(1)} all-to-all(f32[8,1,6]{2,1,0:T(1,128)S(1)} %broadcast_in_dim.7), channel_id=1, replica_groups=mesh['ens'=4,'lat'=16,'lon_0'=4,'lon_1'=2] {'lon_0','lon_1'}, dimensions={0} | all-to-all | bytes 384 | tf_op jit(solution)/shard_map/all_to_all | solution.py:34
  114.6 30.0 %all_to_all.17 = f32[16,1,6]{2,1,0:T(1,128)S(1)} all-to-all(f32[16,1,6]{2,1,0:T(1,128)S(1)} %broadcast_in_dim.8), channel_id=1, replica_groups=mesh['ens'=4,'lat'=16,'lon_0'=4,'lon_1'=2] {'lat'}, dimensions={0} | all-to-all | bytes 768 | tf_op jit(solution)/shard_map/all_to_all | solution.py:34
  144.7 0.7 fusion.47
  158.7 0.7 multiply_add_fusion.1
  (49 shorter events, 0.7 us)
Async XLA Ops:
  7.9 5.1 %copy-start = (f32[3,32,512]{2,1,0:T(8,128)S(1)}, f32[3,32,512]{2,1,0:T(8,128)}, u32[]{:S(2)}) copy-start(f32[3,32,512]{2,1,0:T(8,128)} %param.5) | copy-start | bytes 589828
  7.9 19.9 %copy-start.2 = (f32[3,3]{1,0:T(4,128)S(1)}, f32[3,3]{1,0:T(4,128)}, u32[]{:S(2)}) copy-start(f32[3,3]{1,0:T(4,128)} %param.6) | copy-start | bytes 112
  7.9 28.9 %all-to-all-start = ((f32[4,1,147456]{2,1,0:T(1,128)}), f32[4,1,147456]{2,1,0:T(1,128)S(1)}, u32[]{:S(2)}, u32[]{:S(2)}) async-start(f32[4,1,147456]{2,1,0:T(1,128)} %broadcast_in_dim.6), calls=%async_computation | async-start | bytes 4718592 | tf_op jit(solution)/shard_map/all_to_all | solution.py:34
  13.1 15.3 %collective-permute-start.2 = (f32[3,32,1]{2,1,0:T(8,128)S(1)}, f32[3,32,1]{2,1,0:T(8,128)S(1)}, u32[]{:S(2)}, u32[]{:S(2)}) collective-permute-start(f32[3,32,1]{2,1,0:T(8,128)S(1)} %get-tuple-element.66), channel_id=1, source_target_pairs={{1,0},{2,1},{3,2},{4,3},{5,4},{6,5},{7,6},{9,8},{10,9},{11,10},{12... | collective-permute-start | bytes 1160 | tf_op jit(solution)/shard_map/ppermute | solution.py:21
  20.5 7.9 %collective-permute-start.3 = (f32[3,32,1]{2,1,0:T(8,128)S(1)}, f32[3,32,1]{2,1,0:T(8,128)S(1)}, u32[]{:S(2)}, u32[]{:S(2)}) collective-permute-start(f32[3,32,1]{2,1,0:T(8,128)S(1)} %get-tuple-element.67), channel_id=1, source_target_pairs={{0,1},{1,2},{2,3},{3,4},{4,5},{5,6},{6,7},{8,9},{9,10},{10,11},{11... | collective-permute-start | bytes 1160 | tf_op jit(solution)/shard_map/ppermute | solution.py:20
  22.5 6.0 %collective-permute-start = (f32[3,1,512]{2,1,0:T(1,128)S(1)}, f32[3,1,512]{2,1,0:T(1,128)S(1)}, u32[]{:S(2)}, u32[]{:S(2)}) collective-permute-start(f32[3,1,512]{2,1,0:T(1,128)S(1)} %get-tuple-element.69), channel_id=1, source_target_pairs={{8,0},{16,8},{24,16},{32,24},{40,32},{48,40},{56,48},{64,56},{72,6... | collective-permute-start | bytes 18440 | tf_op jit(solution)/shard_map/ppermute | solution.py:21
  23.8 4.8 %collective-permute-start.1 = (f32[3,1,512]{2,1,0:T(1,128)S(1)}, f32[3,1,512]{2,1,0:T(1,128)S(1)}, u32[]{:S(2)}, u32[]{:S(2)}) collective-permute-start(f32[3,1,512]{2,1,0:T(1,128)S(1)} %get-tuple-element.68), channel_id=1, source_target_pairs={{0,8},{8,16},{16,24},{24,32},{32,40},{40,48},{48,56},{56,64},{64,7... | collective-permute-start | bytes 18440 | tf_op jit(solution)/shard_map/ppermute | solution.py:20
  28.7 13.1 %copy-start.1 = (f32[3,32,512]{2,1,0:T(8,128)S(1)}, f32[3,32,512]{2,1,0:T(8,128)}, u32[]{:S(2)}) copy-start(f32[3,32,512]{2,1,0:T(8,128)} %param.7) | copy-start | bytes 589828
  42.0 16.9 %collective-permute-start.6 = (f32[3,32,1]{2,1,0:T(8,128)S(1)}, f32[3,32,1]{2,1,0:T(8,128)S(1)}, u32[]{:S(2)}, u32[]{:S(2)}) collective-permute-start(f32[3,32,1]{2,1,0:T(8,128)S(1)} %get-tuple-element.59), channel_id=1, source_target_pairs={{1,0},{2,1},{3,2},{4,3},{5,4},{6,5},{7,6},{9,8},{10,9},{11,10},{12... | collective-permute-start | bytes 1160 | tf_op jit(solution)/shard_map/ppermute | solution.py:21
  50.3 8.7 %collective-permute-start.7 = (f32[3,32,1]{2,1,0:T(8,128)S(1)}, f32[3,32,1]{2,1,0:T(8,128)S(1)}, u32[]{:S(2)}, u32[]{:S(2)}) collective-permute-start(f32[3,32,1]{2,1,0:T(8,128)S(1)} %get-tuple-element.60), channel_id=1, source_target_pairs={{0,1},{1,2},{2,3},{3,4},{4,5},{5,6},{6,7},{8,9},{9,10},{10,11},{11... | collective-permute-start | bytes 1160 | tf_op jit(solution)/shard_map/ppermute | solution.py:20
  53.3 5.7 %collective-permute-start.4 = (f32[3,1,512]{2,1,0:T(1,128)S(1)}, f32[3,1,512]{2,1,0:T(1,128)S(1)}, u32[]{:S(2)}, u32[]{:S(2)}) collective-permute-start(f32[3,1,512]{2,1,0:T(1,128)S(1)} %get-tuple-element.62), channel_id=1, source_target_pairs={{8,0},{16,8},{24,16},{32,24},{40,32},{48,40},{56,48},{64,56},{72,6... | collective-permute-start | bytes 18440 | tf_op jit(solution)/shard_map/ppermute | solution.py:21
  54.6 4.9 %collective-permute-start.5 = (f32[3,1,512]{2,1,0:T(1,128)S(1)}, f32[3,1,512]{2,1,0:T(1,128)S(1)}, u32[]{:S(2)}, u32[]{:S(2)}) collective-permute-start(f32[3,1,512]{2,1,0:T(1,128)S(1)} %get-tuple-element.61), channel_id=1, source_target_pairs={{0,8},{8,16},{16,24},{24,32},{32,40},{40,48},{48,56},{56,64},{64,7... | collective-permute-start | bytes 18440 | tf_op jit(solution)/shard_map/ppermute | solution.py:20
  65.5 11.5 %collective-permute-start.10 = (f32[3,32,1]{2,1,0:T(8,128)S(1)}, f32[3,32,1]{2,1,0:T(8,128)S(1)}, u32[]{:S(2)}, u32[]{:S(2)}) collective-permute-start(f32[3,32,1]{2,1,0:T(8,128)S(1)} %get-tuple-element.52), channel_id=1, source_target_pairs={{1,0},{2,1},{3,2},{4,3},{5,4},{6,5},{7,6},{9,8},{10,9},{11,10},{12... | collective-permute-start | bytes 1160 | tf_op jit(solution)/shard_map/ppermute | solution.py:21
  67.8 9.2 %collective-permute-start.11 = (f32[3,32,1]{2,1,0:T(8,128)S(1)}, f32[3,32,1]{2,1,0:T(8,128)S(1)}, u32[]{:S(2)}, u32[]{:S(2)}) collective-permute-start(f32[3,32,1]{2,1,0:T(8,128)S(1)} %get-tuple-element.53), channel_id=1, source_target_pairs={{0,1},{1,2},{2,3},{3,4},{4,5},{5,6},{6,7},{8,9},{9,10},{10,11},{11... | collective-permute-start | bytes 1160 | tf_op jit(solution)/shard_map/ppermute | solution.py:20
  71.1 5.9 %collective-permute-start.8 = (f32[3,1,512]{2,1,0:T(1,128)S(1)}, f32[3,1,512]{2,1,0:T(1,128)S(1)}, u32[]{:S(2)}, u32[]{:S(2)}) collective-permute-start(f32[3,1,512]{2,1,0:T(1,128)S(1)} %get-tuple-element.55), channel_id=1, source_target_pairs={{8,0},{16,8},{24,16},{32,24},{40,32},{48,40},{56,48},{64,56},{72,6... | collective-permute-start | bytes 18440 | tf_op jit(solution)/shard_map/ppermute | solution.py:21
  72.4 5.3 %collective-permute-start.9 = (f32[3,1,512]{2,1,0:T(1,128)S(1)}, f32[3,1,512]{2,1,0:T(1,128)S(1)}, u32[]{:S(2)}, u32[]{:S(2)}) collective-permute-start(f32[3,1,512]{2,1,0:T(1,128)S(1)} %get-tuple-element.54), channel_id=1, source_target_pairs={{0,8},{8,16},{16,24},{24,32},{32,40},{40,48},{48,56},{56,64},{64,7... | collective-permute-start | bytes 18440 | tf_op jit(solution)/shard_map/ppermute | solution.py:20
  83.6 11.2 %collective-permute-start.14 = (f32[3,32,1]{2,1,0:T(8,128)S(1)}, f32[3,32,1]{2,1,0:T(8,128)S(1)}, u32[]{:S(2)}, u32[]{:S(2)}) collective-permute-start(f32[3,32,1]{2,1,0:T(8,128)S(1)} %get-tuple-element.45), channel_id=1, source_target_pairs={{1,0},{2,1},{3,2},{4,3},{5,4},{6,5},{7,6},{9,8},{10,9},{11,10},{12... | collective-permute-start | bytes 1160 | tf_op jit(solution)/shard_map/ppermute | solution.py:21
  85.6 9.3 %collective-permute-start.15 = (f32[3,32,1]{2,1,0:T(8,128)S(1)}, f32[3,32,1]{2,1,0:T(8,128)S(1)}, u32[]{:S(2)}, u32[]{:S(2)}) collective-permute-start(f32[3,32,1]{2,1,0:T(8,128)S(1)} %get-tuple-element.46), channel_id=1, source_target_pairs={{0,1},{1,2},{2,3},{3,4},{4,5},{5,6},{6,7},{8,9},{9,10},{10,11},{11... | collective-permute-start | bytes 1160 | tf_op jit(solution)/shard_map/ppermute | solution.py:20
  89.2 5.6 %collective-permute-start.12 = (f32[3,1,512]{2,1,0:T(1,128)S(1)}, f32[3,1,512]{2,1,0:T(1,128)S(1)}, u32[]{:S(2)}, u32[]{:S(2)}) collective-permute-start(f32[3,1,512]{2,1,0:T(1,128)S(1)} %get-tuple-element.48), channel_id=1, source_target_pairs={{8,0},{16,8},{24,16},{32,24},{40,32},{48,40},{56,48},{64,56},{72,6... | collective-permute-start | bytes 18440 | tf_op jit(solution)/shard_map/ppermute | solution.py:21
  90.5 5.0 %collective-permute-start.13 = (f32[3,1,512]{2,1,0:T(1,128)S(1)}, f32[3,1,512]{2,1,0:T(1,128)S(1)}, u32[]{:S(2)}, u32[]{:S(2)}) collective-permute-start(f32[3,1,512]{2,1,0:T(1,128)S(1)} %get-tuple-element.47), channel_id=1, source_target_pairs={{0,8},{8,16},{16,24},{24,32},{32,40},{40,48},{48,56},{56,64},{64,7... | collective-permute-start | bytes 18440 | tf_op jit(solution)/shard_map/ppermute | solution.py:20

commit v2 on v1

v2 whole, which is shorter than its diff:
```python
import itertools

import jax
import jax.numpy as jnp
from jax import lax
from jax.experimental import pallas as pl
from jax.experimental.pallas import tpu as pltpu
from jax.sharding import Mesh
from jax.sharding import PartitionSpec as P

ITERS = 3
LON = ("lon_0", "lon_1")
EVERY = ("ens", "lat", *LON)
SCALE = 2.0**-10
INTERPRET = False

ROWS, COLS = 32, 512
SUMS = 9
FIELDS = 12
HALO = 4
EDGE_AT = SUMS * 2 * 16
SIDE_AT = EDGE_AT + SUMS * 2 * HALO
PART_ROWS = SIDE_AT + 24

VMEM = pl.BlockSpec(memory_space=pltpu.VMEM)
SMEM = pl.BlockSpec(memory_space=pltpu.SMEM)


def lanes_of(field, shape):
    lane = lax.broadcasted_iota(jnp.int32, shape, 1)
    return (lane >= HALO * field) & (lane < HALO * (field + 1))


def pack_sides(columns, first):
    packed = jnp.zeros(columns[0].shape, jnp.float32)
    for f, x in enumerate(columns):
        shift = (HALO * f if first else HALO * f + HALO - 128) % 128
        packed = jnp.where(lanes_of(f, x.shape), pltpu.roll(x, shift, 1) if shift else x, packed)
    return packed


def unpack_side(packed, field, first):
    shift = (-HALO * field if first else 128 - HALO - HALO * field) % 128
    return pltpu.roll(packed, shift, 1) if shift else packed


def gev_kernel(maxima_ref, latent_ref, part_ref):
    block = pl.program_id(0)
    for half in range(2):
        cols = slice(256 * half, 256 * half + 256)
        loc_par = 10.0 * latent_ref[0, :, cols]
        per_scale = jnp.exp(-latent_ref[1, :, cols])
        shape_par = 0.1 * latent_ref[2, :, cols]
        per_shape = 1.0 / shape_par

        def add_one(m, sums):
            scaled = (maxima_ref[m, :, cols] - loc_par) * per_scale
            inside = 1.0 + shape_par * scaled
            exponent = jnp.log(inside) * per_shape
            rest = 1.0 - jnp.exp(-exponent)
            a = (shape_par + rest) / inside
            sa = scaled * a
            b = sa - 1.0
            c = exponent * rest - sa
            terms = (a, b, c, a * a, a * b, a * c, b * b, b * c, c * c)
            return tuple(s + t for s, t in zip(sums, terms))

        zero = jnp.zeros((8, 256), jnp.float32)
        sums = lax.fori_loop(0, maxima_ref.shape[0], add_one, (zero,) * SUMS, unroll=4)
        ka, kc = 10.0 * per_scale, 0.1 * per_shape
        factors = (ka, None, kc, ka * ka, ka, ka * kc, None, kc, kc * kc)
        sums = [s if k is None else s * k for s, k in zip(sums, factors)]

        owner = 2 * (block // 2) + half
        for f in range(SUMS):
            for t in range(2):
                at = pl.multiple_of((2 * f + t) * 16 + 8 * (block % 2), 8)
                part_ref[owner, pl.ds(at, 8), :] = sums[f][:, 128 * t : 128 * t + 128]

        def put_edge(to, rows):
            for f in range(SUMS):
                for t in range(2):
                    at = EDGE_AT + (2 * f + t) * HALO
                    part_ref[to, at : at + HALO, :] = sums[f][rows, 128 * t : 128 * t + 128]

        pl.when(block == 2)(lambda: put_edge(half, slice(0, HALO)))
        pl.when(block == 1)(lambda: put_edge(2 + half, slice(8 - HALO, 8)))

        near = slice(0, 128) if half else slice(128, 256)
        side = pack_sides([s[:, near] for s in sums], bool(half))

        def put_side(to, tile):
            part_ref[to, pl.ds(pl.multiple_of(SIDE_AT + 8 * tile, 8), 8), :] = side

        pl.when(block <= 2)(lambda: put_side(1 - half, block))
        pl.when(block >= 1)(lambda: put_side(3 - half, block - 1))


def placing(er, ec):
    return dict(
        rows=slice(8, 32) if er == 0 else slice(0, 24),
        cols=slice(128, 512) if ec == 0 else slice(0, 384),
        tile_rows=slice(0, 24) if er == 0 else slice(8, 32),
        tile_cols=slice(0, 384) if ec == 0 else slice(128, 512),
        inner_rows=slice(24, 28) if er == 0 else slice(4, 8),
        outer_rows=slice(4, 8) if er == 0 else slice(24, 28),
        own_edge=slice(8, 12) if er == 0 else slice(20, 24),
        tile_edge=slice(0, 4) if er == 0 else slice(28, 32),
        inner_cols=slice(384, 512) if ec == 0 else slice(0, 128),
        outer_cols=slice(0, 128) if ec == 0 else slice(384, 512),
        own_side=slice(128, 256) if ec == 0 else slice(256, 384),
        tile_side=slice(0, 128) if ec == 0 else slice(384, 512),
        corner=slice(0, 8) if er == 0 else slice(16, 24),
    )


def for_quarter(body):
    mine = lax.axis_index("ens")
    for e in range(4):
        pl.when(mine == e)(lambda e=e: body(e // 2, e % 2, placing(e // 2, e % 2)))


def join_kernel(got_ref, latent_ref, precision_ref, window_ref, edge_ref, side_ref, corner_ref):
    def body(er, ec, at):
        def total(start, rows):
            cut = slice(start, start + rows)
            return got_ref[0, cut, :] + got_ref[1, cut, :] + got_ref[2, cut, :] + got_ref[3, cut, :]

        window_ref[...] = jnp.zeros(window_ref.shape, jnp.float32)
        sides = total(SIDE_AT, 24)
        for f in range(SUMS):
            window_ref[f, at["rows"], at["inner_cols"]] = unpack_side(sides, f, ec == 0)
            for t in range(2):
                cols = slice(128 + 128 * t, 256 + 128 * t)
                window_ref[f, 8:24, cols] = total((2 * f + t) * 16, 16)
                window_ref[f, at["inner_rows"], cols] = total(EDGE_AT + (2 * f + t) * HALO, HALO)
        for k, diagonal in enumerate((3, 6, 8)):
            level = precision_ref[k, at["tile_rows"], at["tile_cols"]]
            here = latent_ref[k, at["tile_rows"], at["tile_cols"]]
            there = (at["rows"], at["cols"])
            window_ref[k, *there] = window_ref[k, *there] - level * here
            window_ref[diagonal, *there] = window_ref[diagonal, *there] + level
        for f in range(FIELDS):
            edge_ref[HALO * f : HALO * f + HALO, :] = (
                window_ref[f, at["own_edge"], at["cols"]]
                if f < SUMS
                else latent_ref[f - SUMS, at["tile_edge"], at["tile_cols"]]
            )
        columns = [window_ref[f, at["rows"], at["own_side"]] for f in range(SUMS)]
        columns += [latent_ref[k, at["tile_rows"], at["tile_side"]] for k in range(3)]
        side = pack_sides(columns, ec == 0)
        side_ref[...] = side
        corner_ref[...] = side[at["corner"], :]

    for_quarter(body)


def krylov_kernel(
    coupling_ref, window_ref, latent_ref, edge_ref, side_ref, corner_ref, basis_ref, moments_ref, full_ref
):
    def body(er, ec, at):
        full_ref[0:SUMS] = window_ref[...]
        full_ref[SUMS:FIELDS, at["rows"], at["cols"]] = latent_ref[:, at["tile_rows"], at["tile_cols"]]
        parts = [corner_ref[...], side_ref[...]] if er == 0 else [side_ref[...], corner_ref[...]]
        sides = jnp.concatenate(parts, axis=0)
        for f in range(FIELDS):
            full_ref[f, at["outer_rows"], at["cols"]] = edge_ref[HALO * f : HALO * f + HALO, :]
            full_ref[f, :, at["outer_cols"]] = unpack_side(sides, f, ec == 1)

    for_quarter(body)
    mine = lax.axis_index("ens")
    lon = lax.axis_index(LON[0]) * lax.axis_size(LON[1]) + lax.axis_index(LON[1])
    n_lon = lax.axis_size(LON[0]) * lax.axis_size(LON[1])
    shape = (ROWS, COLS)
    row = lax.broadcasted_iota(jnp.int32, shape, 0) + (
        lax.axis_index("lat") * ROWS + 16 * (mine // 2) - 8
    )
    col = lax.broadcasted_iota(jnp.int32, shape, 1) + (lon * COLS + 256 * (mine % 2) - 128)
    inside = (row >= 0) & (row < lax.axis_size("lat") * ROWS) & (col >= 0) & (col < n_lon * COLS)

    def mixed(field):
        laplace = []
        for x in field:
            beside = pltpu.roll(x, 1, 0) + pltpu.roll(x, ROWS - 1, 0)
            beside = beside + (pltpu.roll(x, 1, 1) + pltpu.roll(x, COLS - 1, 1))
            laplace.append(4.0 * x - beside)
        return [
            coupling_ref[k, 0] * laplace[0]
            + coupling_ref[k, 1] * laplace[1]
            + coupling_ref[k, 2] * laplace[2]
            for k in range(3)
        ]

    def operate(field):
        q = mixed(field)
        h = [full_ref[3 + k] for k in range(6)]
        x, y, z = field
        own = (h[0] * x + h[1] * y + h[2] * z, h[1] * x + h[3] * y + h[4] * z, h[2] * x + h[4] * y + h[5] * z)
        return [jnp.where(inside, SCALE * (a + b), 0.0) for a, b in zip(q, own)]

    prior = mixed([full_ref[SUMS + k] for k in range(3)])
    basis = [[jnp.where(inside, full_ref[k] - prior[k], 0.0) for k in range(3)]]
    for _ in range(ITERS):
        basis.append(operate(basis[-1]))
    own = [[x[8:24, 128:384] for x in field] for field in basis]
    for p in range(ITERS):
        for k in range(3):
            basis_ref[3 * p + k] = own[p][k]
    rows = []
    for k in range(2 * ITERS):
        a, b = own[k // 2], own[k - k // 2]
        product = a[0] * b[0] + a[1] * b[1] + a[2] * b[2]
        product = product[:, :128] + product[:, 128:]
        rows.append(jnp.sum(product, axis=0, keepdims=True))
    rows.append(jnp.zeros((2, 128), jnp.float32))
    moments_ref[...] = jnp.broadcast_to(jnp.concatenate(rows, axis=0)[None], moments_ref.shape)


def krylov_weights(m):
    def inner(p, q, shift):
        terms = [p[i] * q[j] * m[i + j + shift] for i in range(len(p)) for j in range(len(q))]
        return sum(terms[1:], terms[0])

    def combine(p, factor, q):
        both = [x + factor * y for x, y in zip(p, q)]
        return both + p[len(q) :] + [factor * y for y in q[len(p) :]]

    one = jnp.ones_like(m[0])
    zero = jnp.zeros_like(m[0])
    weights, residual, direction = [], [one], [one]
    norm_now = m[0]
    for iteration in range(ITERS):
        step_size = norm_now / inner(direction, direction, 1)
        weights = combine(weights, step_size, direction)
        if iteration + 1 < ITERS:
            residual = combine(residual, -step_size, [zero] + direction)
            norm_next = inner(residual, residual, 0)
            direction = combine(residual, norm_next / norm_now, direction)
            norm_now = norm_next
    return [SCALE * w for w in weights]


def update_kernel(moments_ref, latent_ref, *refs):
    basis_refs, solution_ref = refs[:-1], refs[-1]
    moments = jnp.sum(jnp.sum(moments_ref[...], axis=0), axis=1, keepdims=True)
    weights = krylov_weights([moments[k : k + 1, :] for k in range(2 * ITERS)])
    weights = [jnp.broadcast_to(w, (16, 256)) for w in weights]
    mine = lax.axis_index("ens")
    for back, basis_ref in enumerate(basis_refs):
        e = lax.rem(mine + (4 - back), 4)
        rows = pl.ds(pl.multiple_of(16 * (e // 2), 8), 16)
        cols = pl.ds(pl.multiple_of(256 * (e % 2), 128), 256)
        for k in range(3):
            step = weights[0] * basis_ref[k] + weights[1] * basis_ref[3 + k] + weights[2] * basis_ref[6 + k]
            solution_ref[k, rows, cols] = latent_ref[k, rows, cols] + step


def f32(*shape):
    return jax.ShapeDtypeStruct(shape, jnp.float32)


def to_neighbour(value, where):
    sizes = [lax.axis_size(axis) for axis in EVERY]
    n_lat, n_lon = sizes[1], sizes[2] * sizes[3]
    pairs = []
    for e, lat, lon in itertools.product(range(4), range(n_lat), range(n_lon)):
        e_to, lat_to, lon_to = where(e, lat, lon)
        if 0 <= lat_to < n_lat and 0 <= lon_to < n_lon:
            pairs.append(((e * n_lat + lat) * n_lon + lon, (e_to * n_lat + lat_to) * n_lon + lon_to))
    return lax.ppermute(value, EVERY, pairs)


def step_of(side):
    return 1 if side else -1


def per_device(maxima, latent, coupling, local_precision):
    depth = maxima.shape[0]
    part = pl.pallas_call(
        gev_kernel,
        grid=(4,),
        in_specs=[
            pl.BlockSpec((depth, 8, COLS), lambda i: (0, i, 0)),
            pl.BlockSpec((3, 8, COLS), lambda i: (0, i, 0)),
        ],
        out_specs=VMEM,
        out_shape=f32(4, PART_ROWS, 128),
        interpret=INTERPRET,
        name="gev",
    )(maxima, latent)
    got = lax.all_to_all(part, "ens", 0, 0, tiled=True)
    window, edge, side, corner = pl.pallas_call(
        join_kernel,
        in_specs=[VMEM] * 3,
        out_specs=[VMEM] * 4,
        out_shape=[f32(SUMS, ROWS, COLS), f32(FIELDS * HALO, 384), f32(24, 128), f32(8, 128)],
        interpret=INTERPRET,
        name="join",
    )(got, latent, local_precision)
    edge = to_neighbour(edge, lambda e, lat, lon: (e ^ 2, lat + step_of(e // 2), lon))
    side = to_neighbour(side, lambda e, lat, lon: (e ^ 1, lat, lon + step_of(e % 2)))
    corner = to_neighbour(corner, lambda e, lat, lon: (e ^ 3, lat + step_of(e // 2), lon + step_of(e % 2)))
    n_lat = lax.axis_size("lat")
    basis, moments = pl.pallas_call(
        krylov_kernel,
        in_specs=[SMEM] + [VMEM] * 5,
        out_specs=[VMEM] * 2,
        out_shape=[f32(3 * ITERS, 16, 256), f32(n_lat, 8, 128)],
        scratch_shapes=[pltpu.VMEM((FIELDS, ROWS, COLS), jnp.float32)],
        interpret=INTERPRET,
        name="krylov",
    )(coupling, window, latent, edge, side, corner)
    others = [lax.ppermute(basis, "ens", [(e, (e + k) % 4) for e in range(4)]) for k in range(1, 4)]
    moments = lax.all_to_all(moments, "lat", 0, 0, tiled=True).sum(axis=0)
    rest = ("ens", *LON)
    moments = jnp.broadcast_to(moments, (lax.axis_size(rest), *moments.shape))
    moments = lax.all_to_all(moments, rest, 0, 0, tiled=True)
    return pl.pallas_call(
        update_kernel,
        in_specs=[VMEM] * 6,
        out_specs=VMEM,
        out_shape=f32(3, ROWS, COLS),
        interpret=INTERPRET,
        name="update",
    )(moments, latent, basis, *others)


def solution(mesh):
    split = Mesh(
        mesh.devices.reshape(mesh.shape["ens"], mesh.shape["lat"], -1, 2),
        ("ens", "lat", "lon_0", "lon_1"),
    )
    placed = (P("ens", "lat", LON), P(None, "lat", LON), P(), P(None, "lat", LON))
    return jax.shard_map(
        per_device, mesh=split, in_specs=placed, out_specs=P(None, "lat", LON), check_vma=False
    )
```

time: 161 us -> 90.2 us (0.56)
  other arithmetic: 35.1 us -> 0.02 us
  blocking collectives: 38.6 us -> 13.4 us
  between operations: 13.8 us -> 0.15 us
  Pallas kernels: 0 us -> 13.2 us
  starting transfers between devices: 58.9 us -> 51.1 us
  local copies, waits for them, and re-layouts: 8.52 us -> 1.96 us
  waiting for transfers between devices: 4.42 us -> 9.69 us
    ppermute x16 -> x6, starting transfers between devices: 53.7 us -> 20.9 us  [the longest x3 10.5 us: to_neighbour(): return lax.ppermute(value, EVERY, pairs)]
    all_to_all x2 -> x1, blocking collectives: 38.6 us -> 13.4 us  [per_device(): got = lax.all_to_all(part, 'ens', 0, 0, tiled=True)]
    all_to_all x1 -> x2, starting transfers between devices: 5.13 us -> 30.2 us  [the longest x1 21.8 us: per_device(): moments = lax.all_to_all(moments, 'lat', 0, 0, tiled=True).sum(axis=0)]
    add x5 -> x0, other arithmetic: 23.1 us -> none  [the longest x4 22.4 us: mix_rows(): coupling[0, 0] * laplace_term[0] + coupling[0, 1] * laplace_term[1]]
    pallas_call x0 -> x4, Pallas kernels: none -> 13.2 us  [the longest x1 6.09 us: per_device(): pl.pallas_call(gev_kernel, grid=(4,), in_specs=[pl.BlockSpec((depth, 8, C...]
    reduce_sum x5 -> x1, other arithmetic: 6.92 us -> 0.02 us  [per_device(): moments = lax.all_to_all(moments, 'lat', 0, 0, tiled=True).sum(axis=0)]
    all_to_all x1 -> x2, waiting for transfers between devices: 2.46 us -> 8.79 us  [the longest x1 7.54 us: per_device(): moments = lax.all_to_all(moments, rest, 0, 0, tiled=True)]
    another operation x2 -> x0, local copies, waits for them, and re-layouts: 3.85 us -> none  [the longest x1 3.85 us: moments_total(): packed = jnp.stack([jnp.sum(p) for p in products])[None]]
  transfers between devices with their start and end apart: 17 -> 8, of which waited for: 5 -> 3; matrix products, arithmetic and copies ran while one was open for 4% -> 1% of each run, Pallas kernels for 0% -> 0%
where the time goes in v2:
time: 90.2 us; the launch traced here: 89.6 us
  starting transfers between devices  51.1 us (57%)
  blocking collectives  13.4 us (15%)
  Pallas kernels  13.2 us (15%)
  waiting for transfers between devices  9.69 us (11%)
  local copies, waits for them, and re-layouts  1.96 us (2%)
    all_to_all x1, starting transfers between devices, per_device(): moments = lax.all_to_all(moments, 'lat', 0, 0, tiled=True).sum(axis=0)  21.8 us
    all_to_all x1, blocking collectives, per_device(): got = lax.all_to_all(part, 'ens', 0, 0, tiled=True)  13.4 us
    ppermute x3, starting transfers between devices, to_neighbour(): return lax.ppermute(value, EVERY, pairs)  10.5 us
    ppermute x3, starting transfers between devices, per_device(): lax.ppermute(basis, 'ens', [(e, (e + k) % 4) for e in range(4)])  10.4 us
    all_to_all x1, starting transfers between devices, per_device(): moments = lax.all_to_all(moments, rest, 0, 0, tiled=True)  8.39 us
    all_to_all x1, waiting for transfers between devices, per_device(): moments = lax.all_to_all(moments, rest, 0, 0, tiled=True)  7.54 us
    pallas_call x1, Pallas kernels, per_device(): pl.pallas_call(gev_kernel, grid=(4,), in_specs=[pl.BlockSpec((depth, 8, C...  6.09 us
    pallas_call x1, Pallas kernels, per_device(): pl.pallas_call(krylov_kernel, in_specs=[SMEM] + [VMEM] * 5, out_specs=[VM...  2.63 us
  transfers between devices with their start and end apart: 8, of which 3 were waited for; matrix products, arithmetic and copies ran while one was open for 1% of the time, Pallas kernels for 0%

profile of v2, /device:TPU:1, one launch (start us, length us, event | category | flops | bytes accessed | tf_op | source)
XLA Modules:
  0.0 89.6 jit_solution(6194894726607465139)
XLA Ops:
  0.0 6.1 %gev.1 = f32[4,384,128]{2,1,0:T(8,128)} custom-call(f32[32,32,512]{2,1,0:T(8,128)} %maxima_ref.1, f32[3,32,512]{2,1,0:T(8,128)} %latent_ref.7), custom_call_target="tpu_custom_call" | custom-call | tf_op jit(solution)/shard_map/gev/pallas_call | solution.py:279
  6.1 13.4 %all_to_all.15.got_ref = f32[4,384,128]{2,1,0:T(8,128)} all-to-all(f32[4,384,128]{2,1,0:T(8,128)} %gev.1), channel_id=1, replica_groups=mesh['ens'=4,'lat'=16,'lon_0'=4,'lon_1'=2] {'ens'}, dimensions={0} | all-to-all | bytes 1572864 | tf_op jit(solution)/shard_map/all_to_all | solution.py:291
  19.5 2.3 %join.1 = (f32[9,32,512]{2,1,0:T(8,128)}, f32[48,384]{1,0:T(8,128)}, f32[24,128]{1,0:T(8,128)}, f32[8,128]{1,0:T(8,128)}) custom-call(f32[4,384,128]{2,1,0:T(8,128)} %all_to_all.15.got_ref, f32[3,32,512]{2,1,0:T(8,128)} %latent_ref.7, f32[3,32,512]{2,1,0:T(8,128)} %precision_ref.1), custom_call_target="tpu_custom_call" | custom-call | tf_op jit(solution)/shard_map/join/pallas_call | solution.py:292
  21.8 0.7 collective-permute-start
  22.5 9.2 %collective-permute-start.1 = (f32[24,128]{1,0:T(8,128)}, f32[24,128]{1,0:T(8,128)S(1)}, u32[]{:S(2)}, u32[]{:S(2)}) collective-permute-start(f32[24,128]{1,0:T(8,128)} %get-tuple-element.13), channel_id=1, source_target_pairs={{1,128},{2,129},{3,130},{4,131},{5,132},{6,133},{7,134},{9,136},{1... | collective-permute-start | bytes 36872 | tf_op jit(solution)/shard_map/ppermute | solution.py:270
  31.7 0.7 collective-permute-start.2
  32.4 0.0 collective-permute-done.2.corner_ref
  32.4 0.0 copy-start.6
  32.4 0.9 collective-permute-done.1.side_ref
  33.3 0.0 copy-start.5
  33.3 0.0 collective-permute-done.edge_ref
  33.3 0.0 copy-start.4
  33.3 0.0 copy-done.6
  33.3 0.6 copy-done.5
  33.9 0.0 copy-done.4
  33.9 2.6 %krylov.1 = (f32[9,16,256]{2,1,0:T(8,128)}, f32[16,8,128]{2,1,0:T(8,128)}) custom-call(f32[3,3]{1,0:T(4,128)} %coupling_ref.1, f32[9,32,512]{2,1,0:T(8,128)} %get-tuple-element.11.window_ref, f32[3,32,512]{2,1,0:T(8,128)} %latent_ref.7, f32[48,384]{1,0:T(8,128)} %copy-done.4, f32[24,128]{1,0:T(8,128)} %copy-done.5, f32[8,128]{1,0:T(8,128)} %copy-done.6), custom_call_target="tpu_custom_call" | custom-call | tf_op jit(solution)/shard_map/krylov/pallas_call | solution.py:304
  36.6 21.8 %all-to-all-start.1 = ((f32[16,8,128]{2,1,0:T(8,128)}), f32[16,8,128]{2,1,0:T(8,128)S(1)}, u32[]{:S(2)}, u32[]{:S(2)}) async-start(f32[16,8,128]{2,1,0:T(8,128)} %get-tuple-element.15), calls=%async_computation.1 | async-start | bytes 131072 | tf_op jit(solution)/shard_map/all_to_all | solution.py:314
  58.4 6.0 %collective-permute-start.5 = (f32[9,16,256]{2,1,0:T(8,128)}, f32[9,16,256]{2,1,0:T(8,128)S(1)}, u32[]{:S(2)}, u32[]{:S(2)}) collective-permute-start(f32[9,16,256]{2,1,0:T(8,128)} %get-tuple-element.16.refs_0_), channel_id=1, source_target_pairs={{0,384},{128,0},{256,128},{384,256},{1,385},{129,1},{257,129},{385... | collective-permute-start | bytes 442376 | tf_op jit(solution)/shard_map/ppermute | solution.py:313
  64.4 1.9 %collective-permute-start.4 = (f32[9,16,256]{2,1,0:T(8,128)}, f32[9,16,256]{2,1,0:T(8,128)S(1)}, u32[]{:S(2)}, u32[]{:S(2)}) collective-permute-start(f32[9,16,256]{2,1,0:T(8,128)} %get-tuple-element.16.refs_0_), channel_id=1, source_target_pairs={{0,256},{128,384},{256,0},{384,128},{1,257},{129,385},{257,1},{385... | collective-permute-start | bytes 442376 | tf_op jit(solution)/shard_map/ppermute | solution.py:313
  66.3 2.5 %collective-permute-start.3 = (f32[9,16,256]{2,1,0:T(8,128)}, f32[9,16,256]{2,1,0:T(8,128)S(1)}, u32[]{:S(2)}, u32[]{:S(2)}) collective-permute-start(f32[9,16,256]{2,1,0:T(8,128)} %get-tuple-element.16.refs_0_), channel_id=1, source_target_pairs={{0,128},{128,256},{256,384},{384,0},{1,129},{129,257},{257,385},{3... | collective-permute-start | bytes 442376 | tf_op jit(solution)/shard_map/ppermute | solution.py:313
  68.8 1.3 %all-to-all-done.1 = f32[16,8,128]{2,1,0:T(8,128)S(1)} async-done(((f32[16,8,128]{2,1,0:T(8,128)}), f32[16,8,128]{2,1,0:T(8,128)S(1)}, u32[]{:S(2)}, u32[]{:S(2)}) %all-to-all-start.1) | async-done | bytes 65568 | tf_op jit(solution)/shard_map/all_to_all | solution.py:314
  70.1 0.7 broadcast_in_dim.3
  70.7 8.4 %all-to-all-start.2 = ((f32[32,8,128]{2,1,0:T(8,128)}), f32[32,8,128]{2,1,0:T(8,128)S(1)}, u32[]{:S(2)}, u32[]{:S(2)}) async-start(f32[32,8,128]{2,1,0:T(8,128)} %broadcast_in_dim.3), calls=%async_computation.2 | async-start | bytes 262144 | tf_op jit(solution)/shard_map/all_to_all | solution.py:317
  79.1 0.0 collective-permute-done.5.refs_3_
  79.2 0.0 copy-start.1
  79.2 0.0 collective-permute-done.4.refs_2_
  79.2 0.0 copy-start.2
  79.2 0.0 collective-permute-done.3.refs_1_
  79.2 0.0 copy-start.3
  79.2 7.5 %all-to-all-done.2.moments_ref = f32[32,8,128]{2,1,0:T(8,128)S(1)} async-done(((f32[32,8,128]{2,1,0:T(8,128)}), f32[32,8,128]{2,1,0:T(8,128)S(1)}, u32[]{:S(2)}, u32[]{:S(2)}) %all-to-all-start.2) | async-done | bytes 131104 | tf_op jit(solution)/shard_map/all_to_all | solution.py:317
  86.7 0.0 copy-done.1
  86.7 0.0 copy-done.2
  86.8 0.0 copy-done.3
  86.8 0.0 copy-start
  86.8 0.6 copy-done
  87.4 2.2 %update.1 = f32[3,32,512]{2,1,0:T(8,128)} custom-call(f32[32,8,128]{2,1,0:T(8,128)} %copy-done, f32[3,32,512]{2,1,0:T(8,128)} %latent_ref.7, f32[9,16,256]{2,1,0:T(8,128)} %get-tuple-element.16.refs_0_, f32[9,16,256]{2,1,0:T(8,128)} %copy-done.3, f32[9,16,256]{2,1,0:T(8,128)} %copy-done.2, f32[9,16,256]{2,1,0:T(8,128)} %copy-done.1), custom_call_target="tpu_custom_call" | custom-call | tf_op jit(solution)/shard_map/update/pallas_call | solution.py:318
  (1 shorter events, 0.0 us)
Async XLA Ops:
  21.8 11.5 %collective-permute-start = (f32[48,384]{1,0:T(8,128)}, f32[48,384]{1,0:T(8,128)S(1)}, u32[]{:S(2)}, u32[]{:S(2)}) collective-permute-start(f32[48,384]{1,0:T(8,128)} %get-tuple-element.12), channel_id=1, source_target_pairs={{8,256},{9,257},{10,258},{11,259},{12,260},{13,261},{14,262},{15,2... | collective-permute-start | bytes 221192 | tf_op jit(solution)/shard_map/ppermute | solution.py:270
  22.5 10.8 %collective-permute-start.1 = (f32[24,128]{1,0:T(8,128)}, f32[24,128]{1,0:T(8,128)S(1)}, u32[]{:S(2)}, u32[]{:S(2)}) collective-permute-start(f32[24,128]{1,0:T(8,128)} %get-tuple-element.13), channel_id=1, source_target_pairs={{1,128},{2,129},{3,130},{4,131},{5,132},{6,133},{7,134},{9,136},{1... | collective-permute-start | bytes 36872 | tf_op jit(solution)/shard_map/ppermute | solution.py:270
  31.7 0.7 collective-permute-start.2
  32.4 0.9 %copy-start.6 = (f32[8,128]{1,0:T(8,128)}, f32[8,128]{1,0:T(8,128)S(1)}, u32[]{:S(2)}) copy-start(f32[8,128]{1,0:T(8,128)S(1)} %collective-permute-done.2.corner_ref) | copy-start | bytes 12292
  33.3 0.6 copy-start.5
  33.3 0.6 copy-start.4
  36.6 33.5 %all-to-all-start.1 = ((f32[16,8,128]{2,1,0:T(8,128)}), f32[16,8,128]{2,1,0:T(8,128)S(1)}, u32[]{:S(2)}, u32[]{:S(2)}) async-start(f32[16,8,128]{2,1,0:T(8,128)} %get-tuple-element.15), calls=%async_computation.1 | async-start | bytes 131072 | tf_op jit(solution)/shard_map/all_to_all | solution.py:314
  58.4 20.8 %collective-permute-start.5 = (f32[9,16,256]{2,1,0:T(8,128)}, f32[9,16,256]{2,1,0:T(8,128)S(1)}, u32[]{:S(2)}, u32[]{:S(2)}) collective-permute-start(f32[9,16,256]{2,1,0:T(8,128)} %get-tuple-element.16.refs_0_), channel_id=1, source_target_pairs={{0,384},{128,0},{256,128},{384,256},{1,385},{129,1},{257,129},{385... | collective-permute-start | bytes 442376 | tf_op jit(solution)/shard_map/ppermute | solution.py:313
  64.4 14.8 %collective-permute-start.4 = (f32[9,16,256]{2,1,0:T(8,128)}, f32[9,16,256]{2,1,0:T(8,128)S(1)}, u32[]{:S(2)}, u32[]{:S(2)}) collective-permute-start(f32[9,16,256]{2,1,0:T(8,128)} %get-tuple-element.16.refs_0_), channel_id=1, source_target_pairs={{0,256},{128,384},{256,0},{384,128},{1,257},{129,385},{257,1},{385... | collective-permute-start | bytes 442376 | tf_op jit(solution)/shard_map/ppermute | solution.py:313
  66.3 12.9 %collective-permute-start.3 = (f32[9,16,256]{2,1,0:T(8,128)}, f32[9,16,256]{2,1,0:T(8,128)S(1)}, u32[]{:S(2)}, u32[]{:S(2)}) collective-permute-start(f32[9,16,256]{2,1,0:T(8,128)} %get-tuple-element.16.refs_0_), channel_id=1, source_target_pairs={{0,128},{128,256},{256,384},{384,0},{1,129},{129,257},{257,385},{3... | collective-permute-start | bytes 442376 | tf_op jit(solution)/shard_map/ppermute | solution.py:313
  70.7 16.0 %all-to-all-start.2 = ((f32[32,8,128]{2,1,0:T(8,128)}), f32[32,8,128]{2,1,0:T(8,128)S(1)}, u32[]{:S(2)}, u32[]{:S(2)}) async-start(f32[32,8,128]{2,1,0:T(8,128)} %broadcast_in_dim.3), calls=%async_computation.2 | async-start | bytes 262144 | tf_op jit(solution)/shard_map/all_to_all | solution.py:317
  79.2 7.6 %copy-start.1 = (f32[9,16,256]{2,1,0:T(8,128)}, f32[9,16,256]{2,1,0:T(8,128)S(1)}, u32[]{:S(2)}) copy-start(f32[9,16,256]{2,1,0:T(8,128)S(1)} %collective-permute-done.5.refs_3_) | copy-start | bytes 442372
  79.2 7.6 %copy-start.2 = (f32[9,16,256]{2,1,0:T(8,128)}, f32[9,16,256]{2,1,0:T(8,128)S(1)}, u32[]{:S(2)}) copy-start(f32[9,16,256]{2,1,0:T(8,128)S(1)} %collective-permute-done.4.refs_2_) | copy-start | bytes 442372
  79.2 7.6 %copy-start.3 = (f32[9,16,256]{2,1,0:T(8,128)}, f32[9,16,256]{2,1,0:T(8,128)S(1)}, u32[]{:S(2)}) copy-start(f32[9,16,256]{2,1,0:T(8,128)S(1)} %collective-permute-done.3.refs_1_) | copy-start | bytes 442372
  86.8 0.7 copy-start

commit v3 on v2

--- a/solution.py
+++ b/solution.py
@@ -42,6 +42,14 @@
 def unpack_side(packed, field, first):
     shift = (-HALO * field if first else 128 - HALO - HALO * field) % 128
     return pltpu.roll(packed, shift, 1) if shift else packed
+
+
+def place_of_lon():
+    return lax.axis_index(LON[0]) * lax.axis_size(LON[1]) + lax.axis_index(LON[1])
+
+
+def swapped(e):
+    return 2 * ((e // 2 + lax.axis_index("lat")) % 2) + (e + place_of_lon()) % 2
 
 
 def gev_kernel(maxima_ref, latent_ref, part_ref):
@@ -71,7 +79,7 @@
         factors = (ka, None, kc, ka * ka, ka, ka * kc, None, kc, kc * kc)
         sums = [s if k is None else s * k for s, k in zip(sums, factors)]
 
-        owner = 2 * (block // 2) + half
+        owner = swapped(2 * (block // 2) + half)
         for f in range(SUMS):
             for t in range(2):
                 at = pl.multiple_of((2 * f + t) * 16 + 8 * (block % 2), 8)
@@ -81,7 +89,7 @@
             for f in range(SUMS):
                 for t in range(2):
                     at = EDGE_AT + (2 * f + t) * HALO
-                    part_ref[to, at : at + HALO, :] = sums[f][rows, 128 * t : 128 * t + 128]
+                    part_ref[swapped(to), at : at + HALO, :] = sums[f][rows, 128 * t : 128 * t + 128]
 
         pl.when(block == 2)(lambda: put_edge(half, slice(0, HALO)))
         pl.when(block == 1)(lambda: put_edge(2 + half, slice(8 - HALO, 8)))
@@ -90,7 +98,7 @@
         side = pack_sides([s[:, near] for s in sums], bool(half))
 
         def put_side(to, tile):
-            part_ref[to, pl.ds(pl.multiple_of(SIDE_AT + 8 * tile, 8), 8), :] = side
+            part_ref[swapped(to), pl.ds(pl.multiple_of(SIDE_AT + 8 * tile, 8), 8), :] = side
 
         pl.when(block <= 2)(lambda: put_side(1 - half, block))
         pl.when(block >= 1)(lambda: put_side(3 - half, block - 1))
@@ -115,9 +123,9 @@
 
 
 def for_quarter(body):
-    mine = lax.axis_index("ens")
-    for e in range(4):
-        pl.when(mine == e)(lambda e=e: body(e // 2, e % 2, placing(e // 2, e % 2)))
+    mine = swapped(lax.axis_index("ens"))
+    for q in range(4):
+        pl.when(mine == q)(lambda q=q: body(q // 2, q % 2, placing(q // 2, q % 2)))
 
 
 def join_kernel(got_ref, latent_ref, precision_ref, window_ref, edge_ref, side_ref, corner_ref):
@@ -168,8 +176,8 @@
             full_ref[f, :, at["outer_cols"]] = unpack_side(sides, f, ec == 1)
 
     for_quarter(body)
-    mine = lax.axis_index("ens")
-    lon = lax.axis_index(LON[0]) * lax.axis_size(LON[1]) + lax.axis_index(LON[1])
+    mine = swapped(lax.axis_index("ens"))
+    lon = place_of_lon()
     n_lon = lax.axis_size(LON[0]) * lax.axis_size(LON[1])
     shape = (ROWS, COLS)
     row = lax.broadcasted_iota(jnp.int32, shape, 0) + (
@@ -247,31 +255,37 @@
     weights = [jnp.broadcast_to(w, (16, 256)) for w in weights]
     mine = lax.axis_index("ens")
     for back, basis_ref in enumerate(basis_refs):
-        e = lax.rem(mine + (4 - back), 4)
-        rows = pl.ds(pl.multiple_of(16 * (e // 2), 8), 16)
-        cols = pl.ds(pl.multiple_of(256 * (e % 2), 128), 256)
+        q = swapped(lax.rem(mine + (4 - back), 4))
+        rows = pl.ds(pl.multiple_of(16 * (q // 2), 8), 16)
+        cols = pl.ds(pl.multiple_of(256 * (q % 2), 128), 256)
         for k in range(3):
             step = weights[0] * basis_ref[k] + weights[1] * basis_ref[3 + k] + weights[2] * basis_ref[6 + k]
             solution_ref[k, rows, cols] = latent_ref[k, rows, cols] + step
 
 
 def f32(*shape):
-    return jax.ShapeDtypeStruct(shape, jnp.float32)
-
-
-def to_neighbour(value, where):
+    if INTERPRET:
+        return jax.ShapeDtypeStruct(shape, jnp.float32)
+    return pltpu.VMEM(shape, jnp.float32)
+
+
+def near(*arrays):
+    if INTERPRET:
+        return arrays
+    return tuple(pltpu.with_memory_space_constraint(a, pltpu.VMEM) for a in arrays)
+
+
+def to_neighbour(value, across_lat, across_lon):
     sizes = [lax.axis_size(axis) for axis in EVERY]
     n_lat, n_lon = sizes[1], sizes[2] * sizes[3]
     pairs = []
     for e, lat, lon in itertools.product(range(4), range(n_lat), range(n_lon)):
-        e_to, lat_to, lon_to = where(e, lat, lon)
+        lower, right = (e // 2 + lat) % 2, (e + lon) % 2
+        lat_to = lat + (2 * lower - 1) * across_lat
+        lon_to = lon + (2 * right - 1) * across_lon
         if 0 <= lat_to < n_lat and 0 <= lon_to < n_lon:
-            pairs.append(((e * n_lat + lat) * n_lon + lon, (e_to * n_lat + lat_to) * n_lon + lon_to))
+            pairs.append(((e * n_lat + lat) * n_lon + lon, (e * n_lat + lat_to) * n_lon + lon_to))
     return lax.ppermute(value, EVERY, pairs)
-
-
-def step_of(side):
-    return 1 if side else -1
 
 
 def per_device(maxima, latent, coupling, local_precision):
@@ -296,10 +310,10 @@
         out_shape=[f32(SUMS, ROWS, COLS), f32(FIELDS * HALO, 384), f32(24, 128), f32(8, 128)],
         interpret=INTERPRET,
         name="join",
-    )(got, latent, local_precision)
-    edge = to_neighbour(edge, lambda e, lat, lon: (e ^ 2, lat + step_of(e // 2), lon))
-    side = to_neighbour(side, lambda e, lat, lon: (e ^ 1, lat, lon + step_of(e % 2)))
-    corner = to_neighbour(corner, lambda e, lat, lon: (e ^ 3, lat + step_of(e // 2), lon + step_of(e % 2)))
+    )(*near(got), latent, local_precision)
+    edge = to_neighbour(edge, 1, 0)
+    side = to_neighbour(side, 0, 1)
+    corner = to_neighbour(corner, 1, 1)
     n_lat = lax.axis_size("lat")
     basis, moments = pl.pallas_call(
         krylov_kernel,
@@ -309,7 +323,7 @@
         scratch_shapes=[pltpu.VMEM((FIELDS, ROWS, COLS), jnp.float32)],
         interpret=INTERPRET,
         name="krylov",
-    )(coupling, window, latent, edge, side, corner)
+    )(coupling, *near(window), latent, *near(edge, side, corner))
     others = [lax.ppermute(basis, "ens", [(e, (e + k) % 4) for e in range(4)]) for k in range(1, 4)]
     moments = lax.all_to_all(moments, "lat", 0, 0, tiled=True).sum(axis=0)
     rest = ("ens", *LON)
@@ -319,10 +333,10 @@
         update_kernel,
         in_specs=[VMEM] * 6,
         out_specs=VMEM,
-        out_shape=f32(3, ROWS, COLS),
+        out_shape=jax.ShapeDtypeStruct((3, ROWS, COLS), jnp.float32),
         interpret=INTERPRET,
         name="update",
-    )(moments, latent, basis, *others)
+    )(*near(moments), latent, *near(basis, *others))
 
 
 def solution(mesh):

time: 90.2 us -> 81.9 us (0.908)
  starting transfers between devices: 51.1 us -> 44 us
  waiting for transfers between devices: 9.69 us -> 12.7 us
  Pallas kernels: 13.2 us -> 10.8 us
  local copies, waits for them, and re-layouts: 1.96 us -> 0.67 us
    all_to_all x1, starting transfers between devices: 8.39 us -> 5.16 us  [per_device(): moments = lax.all_to_all(moments, rest, 0, 0, tiled=True)]
    ppermute x3, starting transfers between devices: 10.4 us -> 7.2 us  [per_device(): lax.ppermute(basis, 'ens', [(e, (e + k) % 4) for e in range(4)])]
    all_to_all x1, waiting for transfers between devices: 1.25 us -> 4.44 us  [per_device(): moments = lax.all_to_all(moments, 'lat', 0, 0, tiled=True).sum(axis=0)]
    ppermute x3, starting transfers between devices: 10.5 us -> 9.23 us  [to_neighbour(): return lax.ppermute(value, EVERY, pairs)]
    unnamed x14 -> x0, local copies, waits for them, and re-layouts: 1.29 us -> none
    pallas_call x1, Pallas kernels: 2.3 us -> 1.2 us  [per_device(): pl.pallas_call(join_kernel, in_specs=[VMEM] * 3, out_specs=[VMEM] * 4, ou...]
where the time goes in v3:
time: 81.9 us; the launch traced here: 81.4 us
  starting transfers between devices  44 us (54%)
  blocking collectives  13.1 us (16%)
  waiting for transfers between devices  12.7 us (16%)
  Pallas kernels  10.8 us (13%)
    all_to_all x1, starting transfers between devices, per_device(): moments = lax.all_to_all(moments, 'lat', 0, 0, tiled=True).sum(axis=0)  22.4 us
    all_to_all x1, blocking collectives, per_device(): got = lax.all_to_all(part, 'ens', 0, 0, tiled=True)  13.1 us
    ppermute x3, starting transfers between devices, to_neighbour(): return lax.ppermute(value, EVERY, pairs)  9.23 us
    all_to_all x1, waiting for transfers between devices, per_device(): moments = lax.all_to_all(moments, rest, 0, 0, tiled=True)  7.57 us
    ppermute x3, starting transfers between devices, per_device(): lax.ppermute(basis, 'ens', [(e, (e + k) % 4) for e in range(4)])  7.2 us
    pallas_call x1, Pallas kernels, per_device(): pl.pallas_call(gev_kernel, grid=(4,), in_specs=[pl.BlockSpec((depth, 8, C...  5.35 us
    all_to_all x1, starting transfers between devices, per_device(): moments = lax.all_to_all(moments, rest, 0, 0, tiled=True)  5.16 us
    all_to_all x1, waiting for transfers between devices, per_device(): moments = lax.all_to_all(moments, 'lat', 0, 0, tiled=True).sum(axis=0)  4.44 us
  transfers between devices with their start and end apart: 8, of which 3 were waited for; matrix products, arithmetic and copies ran while one was open for 1% of the time, Pallas kernels for 0%

profile of v3, /device:TPU:1, one launch (start us, length us, event | category | flops | bytes accessed | tf_op | source)
XLA Modules:
  0.0 81.4 jit_solution(13322465113621050353)
XLA Ops:
  0.0 5.3 %gev.1 = f32[4,384,128]{2,1,0:T(8,128)S(1)} custom-call(f32[32,32,512]{2,1,0:T(8,128)} %maxima_ref.1, f32[3,32,512]{2,1,0:T(8,128)} %latent_ref.7), custom_call_target="tpu_custom_call" | custom-call | tf_op jit(solution)/shard_map/gev/pallas_call | solution.py:293
  5.3 13.1 %all_to_all.15.got_ref = f32[4,384,128]{2,1,0:T(8,128)S(1)} all-to-all(f32[4,384,128]{2,1,0:T(8,128)S(1)} %gev.1), channel_id=1, replica_groups=mesh['ens'=4,'lat'=16,'lon_0'=4,'lon_1'=2] {'ens'}, dimensions={0} | all-to-all | bytes 1572864 | tf_op jit(solution)/shard_map/all_to_all | solution.py:305
  18.5 1.2 %join.1 = (f32[9,32,512]{2,1,0:T(8,128)S(1)}, f32[48,384]{1,0:T(8,128)S(1)}, f32[24,128]{1,0:T(8,128)S(1)}, f32[8,128]{1,0:T(8,128)S(1)}) custom-call(f32[4,384,128]{2,1,0:T(8,128)S(1)} %all_to_all.15.got_ref, f32[3,32,512]{2,1,0:T(8,128)} %latent_ref.7, f32[3,32,512]{2,1,0:T(8,128)} %precision_ref.1), custom_call_target="tpu_custom_call" | custom-call | tf_op jit(solution)/shard_map/join/pallas_call | solution.py:306
  19.7 0.7 collective-permute-start
  20.4 7.9 %collective-permute-start.1 = (f32[24,128]{1,0:T(8,128)S(1)}, f32[24,128]{1,0:T(8,128)S(1)}, u32[]{:S(2)}, u32[]{:S(2)}) collective-permute-start(f32[24,128]{1,0:T(8,128)S(1)} %get-tuple-element.13), channel_id=1, source_target_pairs={{1,2},{2,1},{3,4},{4,3},{5,6},{6,5},{9,10},{10,9},{11,12},{12,11},... | collective-permute-start | bytes 36872 | tf_op jit(solution)/shard_map/ppermute | solution.py:288
  28.3 0.7 collective-permute-start.2
  28.9 0.0 collective-permute-done.2.corner_ref
  28.9 0.7 collective-permute-done.1.side_ref
  29.6 0.0 collective-permute-done.edge_ref
  29.6 2.4 %krylov.1 = (f32[9,16,256]{2,1,0:T(8,128)S(1)}, f32[16,8,128]{2,1,0:T(8,128)}) custom-call(f32[3,3]{1,0:T(4,128)} %coupling_ref.1, f32[9,32,512]{2,1,0:T(8,128)S(1)} %get-tuple-element.11.window_ref, f32[3,32,512]{2,1,0:T(8,128)} %latent_ref.7, f32[48,384]{1,0:T(8,128)S(1)} %collective-permute-done.edge_ref, f32[24,128]{1,0:T(8,128)S(1)} %collective-permute-done.1.side_ref, ...), custom_call_target="tpu_custom_call" | custom-call | tf_op jit(solution)/shard_map/krylov/pallas_call | solution.py:318
  32.0 22.4 %all-to-all-start.1 = ((f32[16,8,128]{2,1,0:T(8,128)}), f32[16,8,128]{2,1,0:T(8,128)S(1)}, u32[]{:S(2)}, u32[]{:S(2)}) async-start(f32[16,8,128]{2,1,0:T(8,128)} %get-tuple-element.15), calls=%async_computation.1 | async-start | bytes 131072 | tf_op jit(solution)/shard_map/all_to_all | solution.py:328
  54.4 1.9 %collective-permute-start.5 = (f32[9,16,256]{2,1,0:T(8,128)S(1)}, f32[9,16,256]{2,1,0:T(8,128)S(1)}, u32[]{:S(2)}, u32[]{:S(2)}) collective-permute-start(f32[9,16,256]{2,1,0:T(8,128)S(1)} %get-tuple-element.16.refs_0_), channel_id=1, source_target_pairs={{0,384},{128,0},{256,128},{384,256},{1,385},{129,1},{257,129},{385... | collective-permute-start | bytes 442376 | tf_op jit(solution)/shard_map/ppermute | solution.py:327
  56.4 2.0 %collective-permute-start.4 = (f32[9,16,256]{2,1,0:T(8,128)S(1)}, f32[9,16,256]{2,1,0:T(8,128)S(1)}, u32[]{:S(2)}, u32[]{:S(2)}) collective-permute-start(f32[9,16,256]{2,1,0:T(8,128)S(1)} %get-tuple-element.16.refs_0_), channel_id=1, source_target_pairs={{0,256},{128,384},{256,0},{384,128},{1,257},{129,385},{257,1},{385... | collective-permute-start | bytes 442376 | tf_op jit(solution)/shard_map/ppermute | solution.py:327
  58.4 3.3 %collective-permute-start.3 = (f32[9,16,256]{2,1,0:T(8,128)S(1)}, f32[9,16,256]{2,1,0:T(8,128)S(1)}, u32[]{:S(2)}, u32[]{:S(2)}) collective-permute-start(f32[9,16,256]{2,1,0:T(8,128)S(1)} %get-tuple-element.16.refs_0_), channel_id=1, source_target_pairs={{0,128},{128,256},{256,384},{384,0},{1,129},{129,257},{257,385},{3... | collective-permute-start | bytes 442376 | tf_op jit(solution)/shard_map/ppermute | solution.py:327
  61.7 4.4 %all-to-all-done.1 = f32[16,8,128]{2,1,0:T(8,128)S(1)} async-done(((f32[16,8,128]{2,1,0:T(8,128)}), f32[16,8,128]{2,1,0:T(8,128)S(1)}, u32[]{:S(2)}, u32[]{:S(2)}) %all-to-all-start.1) | async-done | bytes 65568 | tf_op jit(solution)/shard_map/all_to_all | solution.py:328
  66.1 0.7 broadcast_in_dim.3
  66.8 5.2 %all-to-all-start.2 = ((f32[32,8,128]{2,1,0:T(8,128)}), f32[32,8,128]{2,1,0:T(8,128)S(1)}, u32[]{:S(2)}, u32[]{:S(2)}) async-start(f32[32,8,128]{2,1,0:T(8,128)} %broadcast_in_dim.3), calls=%async_computation.2 | async-start | bytes 262144 | tf_op jit(solution)/shard_map/all_to_all | solution.py:331
  72.0 0.0 collective-permute-done.5.refs_3_
  72.0 0.0 collective-permute-done.4.refs_2_
  72.0 0.0 collective-permute-done.3.refs_1_
  72.0 7.6 %all-to-all-done.2.moments_ref = f32[32,8,128]{2,1,0:T(8,128)S(1)} async-done(((f32[32,8,128]{2,1,0:T(8,128)}), f32[32,8,128]{2,1,0:T(8,128)S(1)}, u32[]{:S(2)}, u32[]{:S(2)}) %all-to-all-start.2) | async-done | bytes 131104 | tf_op jit(solution)/shard_map/all_to_all | solution.py:331
  79.6 1.9 %update.1 = f32[3,32,512]{2,1,0:T(8,128)} custom-call(f32[32,8,128]{2,1,0:T(8,128)S(1)} %all-to-all-done.2.moments_ref, f32[3,32,512]{2,1,0:T(8,128)} %latent_ref.7, f32[9,16,256]{2,1,0:T(8,128)S(1)} %get-tuple-element.16.refs_0_, f32[9,16,256]{2,1,0:T(8,128)S(1)} %collective-permute-done.3.refs_1_, f32[9,16,256]{2,1,0:T(8,128)S(1)} %collective-permute-done.4.refs_2_, ...), custom_call_target="tpu_custom_call" | custom-call | tf_op jit(solution)/shard_map/update/pallas_call | solution.py:332
  (1 shorter events, 0.0 us)
Async XLA Ops:
  19.7 9.9 %collective-permute-start = (f32[48,384]{1,0:T(8,128)S(1)}, f32[48,384]{1,0:T(8,128)S(1)}, u32[]{:S(2)}, u32[]{:S(2)}) collective-permute-start(f32[48,384]{1,0:T(8,128)S(1)} %get-tuple-element.12), channel_id=1, source_target_pairs={{8,16},{9,17},{10,18},{11,19},{12,20},{13,21},{14,22},{15,23},{16,... | collective-permute-start | bytes 221192 | tf_op jit(solution)/shard_map/ppermute | solution.py:288
  20.4 9.3 %collective-permute-start.1 = (f32[24,128]{1,0:T(8,128)S(1)}, f32[24,128]{1,0:T(8,128)S(1)}, u32[]{:S(2)}, u32[]{:S(2)}) collective-permute-start(f32[24,128]{1,0:T(8,128)S(1)} %get-tuple-element.13), channel_id=1, source_target_pairs={{1,2},{2,1},{3,4},{4,3},{5,6},{6,5},{9,10},{10,9},{11,12},{12,11},... | collective-permute-start | bytes 36872 | tf_op jit(solution)/shard_map/ppermute | solution.py:288
  28.3 0.7 collective-permute-start.2
  32.0 34.1 %all-to-all-start.1 = ((f32[16,8,128]{2,1,0:T(8,128)}), f32[16,8,128]{2,1,0:T(8,128)S(1)}, u32[]{:S(2)}, u32[]{:S(2)}) async-start(f32[16,8,128]{2,1,0:T(8,128)} %get-tuple-element.15), calls=%async_computation.1 | async-start | bytes 131072 | tf_op jit(solution)/shard_map/all_to_all | solution.py:328
  54.4 17.5 %collective-permute-start.5 = (f32[9,16,256]{2,1,0:T(8,128)S(1)}, f32[9,16,256]{2,1,0:T(8,128)S(1)}, u32[]{:S(2)}, u32[]{:S(2)}) collective-permute-start(f32[9,16,256]{2,1,0:T(8,128)S(1)} %get-tuple-element.16.refs_0_), channel_id=1, source_target_pairs={{0,384},{128,0},{256,128},{384,256},{1,385},{129,1},{257,129},{385... | collective-permute-start | bytes 442376 | tf_op jit(solution)/shard_map/ppermute | solution.py:327
  56.4 15.6 %collective-permute-start.4 = (f32[9,16,256]{2,1,0:T(8,128)S(1)}, f32[9,16,256]{2,1,0:T(8,128)S(1)}, u32[]{:S(2)}, u32[]{:S(2)}) collective-permute-start(f32[9,16,256]{2,1,0:T(8,128)S(1)} %get-tuple-element.16.refs_0_), channel_id=1, source_target_pairs={{0,256},{128,384},{256,0},{384,128},{1,257},{129,385},{257,1},{385... | collective-permute-start | bytes 442376 | tf_op jit(solution)/shard_map/ppermute | solution.py:327
  58.4 13.6 %collective-permute-start.3 = (f32[9,16,256]{2,1,0:T(8,128)S(1)}, f32[9,16,256]{2,1,0:T(8,128)S(1)}, u32[]{:S(2)}, u32[]{:S(2)}) collective-permute-start(f32[9,16,256]{2,1,0:T(8,128)S(1)} %get-tuple-element.16.refs_0_), channel_id=1, source_target_pairs={{0,128},{128,256},{256,384},{384,0},{1,129},{129,257},{257,385},{3... | collective-permute-start | bytes 442376 | tf_op jit(solution)/shard_map/ppermute | solution.py:327
  66.8 12.8 %all-to-all-start.2 = ((f32[32,8,128]{2,1,0:T(8,128)}), f32[32,8,128]{2,1,0:T(8,128)S(1)}, u32[]{:S(2)}, u32[]{:S(2)}) async-start(f32[32,8,128]{2,1,0:T(8,128)} %broadcast_in_dim.3), calls=%async_computation.2 | async-start | bytes 262144 | tf_op jit(solution)/shard_map/all_to_all | solution.py:331

commit v4 on v3

--- a/solution.py
+++ b/solution.py
@@ -12,6 +12,7 @@
 LON = ("lon_0", "lon_1")
 EVERY = ("ens", "lat", *LON)
 SCALE = 2.0**-10
+LN2 = 0.6931471805599453
 INTERPRET = False
 
 ROWS, COLS = 32, 512
@@ -59,23 +60,23 @@
         loc_par = 10.0 * latent_ref[0, :, cols]
         per_scale = jnp.exp(-latent_ref[1, :, cols])
         shape_par = 0.1 * latent_ref[2, :, cols]
-        per_shape = 1.0 / shape_par
+        per_shape = -1.0 / (LN2 * shape_par)
 
         def add_one(m, sums):
             scaled = (maxima_ref[m, :, cols] - loc_par) * per_scale
             inside = 1.0 + shape_par * scaled
-            exponent = jnp.log(inside) * per_shape
-            rest = 1.0 - jnp.exp(-exponent)
+            power = jnp.log(inside) * per_shape
+            rest = 1.0 - jnp.exp2(power)
             a = (shape_par + rest) / inside
             sa = scaled * a
             b = sa - 1.0
-            c = exponent * rest - sa
+            c = power * rest * -LN2 - sa
             terms = (a, b, c, a * a, a * b, a * c, b * b, b * c, c * c)
             return tuple(s + t for s, t in zip(sums, terms))
 
         zero = jnp.zeros((8, 256), jnp.float32)
-        sums = lax.fori_loop(0, maxima_ref.shape[0], add_one, (zero,) * SUMS, unroll=4)
-        ka, kc = 10.0 * per_scale, 0.1 * per_shape
+        sums = lax.fori_loop(0, maxima_ref.shape[0], add_one, (zero,) * SUMS, unroll=8)
+        ka, kc = 10.0 * per_scale, 0.1 / shape_par
         factors = (ka, None, kc, ka * ka, ka, ka * kc, None, kc, kc * kc)
         sums = [s if k is None else s * k for s, k in zip(sums, factors)]
 
@@ -214,14 +215,14 @@
     for p in range(ITERS):
         for k in range(3):
             basis_ref[3 * p + k] = own[p][k]
-    rows = []
+    lane = lax.broadcasted_iota(jnp.int32, (1, 128), 1)
+    moments = jnp.zeros((1, 128), jnp.float32)
     for k in range(2 * ITERS):
         a, b = own[k // 2], own[k - k // 2]
         product = a[0] * b[0] + a[1] * b[1] + a[2] * b[2]
-        product = product[:, :128] + product[:, 128:]
-        rows.append(jnp.sum(product, axis=0, keepdims=True))
-    rows.append(jnp.zeros((2, 128), jnp.float32))
-    moments_ref[...] = jnp.broadcast_to(jnp.concatenate(rows, axis=0)[None], moments_ref.shape)
+        total = jnp.sum(jnp.sum(product, axis=0, keepdims=True), axis=1, keepdims=True)
+        moments = jnp.where(lane == k, total, moments)
+    moments_ref[...] = jnp.broadcast_to(moments[None], moments_ref.shape)
 
 
 def krylov_weights(m):
@@ -250,9 +251,9 @@
 
 def update_kernel(moments_ref, latent_ref, *refs):
     basis_refs, solution_ref = refs[:-1], refs[-1]
-    moments = jnp.sum(jnp.sum(moments_ref[...], axis=0), axis=1, keepdims=True)
-    weights = krylov_weights([moments[k : k + 1, :] for k in range(2 * ITERS)])
-    weights = [jnp.broadcast_to(w, (16, 256)) for w in weights]
+    moments = jnp.sum(moments_ref[...], axis=0)
+    moments = [jnp.broadcast_to(moments[:, k : k + 1], (8, 128)) for k in range(2 * ITERS)]
+    weights = [jnp.tile(w, (2, 2)) for w in krylov_weights(moments)]
     mine = lax.axis_index("ens")
     for back, basis_ref in enumerate(basis_refs):
         q = swapped(lax.rem(mine + (4 - back), 4))
@@ -310,7 +311,7 @@
         out_shape=[f32(SUMS, ROWS, COLS), f32(FIELDS * HALO, 384), f32(24, 128), f32(8, 128)],
         interpret=INTERPRET,
         name="join",
-    )(*near(got), latent, local_precision)
+    )(*near(got, latent, local_precision))
     edge = to_neighbour(edge, 1, 0)
     side = to_neighbour(side, 0, 1)
     corner = to_neighbour(corner, 1, 1)
@@ -319,13 +320,18 @@
         krylov_kernel,
         in_specs=[SMEM] + [VMEM] * 5,
         out_specs=[VMEM] * 2,
-        out_shape=[f32(3 * ITERS, 16, 256), f32(n_lat, 8, 128)],
+        out_shape=[f32(3 * ITERS, 16, 256), f32(n_lat, 1, 128)],
         scratch_shapes=[pltpu.VMEM((FIELDS, ROWS, COLS), jnp.float32)],
         interpret=INTERPRET,
         name="krylov",
-    )(coupling, *near(window), latent, *near(edge, side, corner))
-    others = [lax.ppermute(basis, "ens", [(e, (e + k) % 4) for e in range(4)]) for k in range(1, 4)]
+    )(coupling, *near(window, latent, edge, side, corner))
+
+    def from_back(values, back):
+        return lax.ppermute(values, "ens", [(e, (e + back) % 4) for e in range(4)])
+
     moments = lax.all_to_all(moments, "lat", 0, 0, tiled=True).sum(axis=0)
+    later, moments = lax.optimization_barrier((basis, moments))
+    others = [from_back(basis, 1), from_back(later, 2), from_back(basis, 3)]
     rest = ("ens", *LON)
     moments = jnp.broadcast_to(moments, (lax.axis_size(rest), *moments.shape))
     moments = lax.all_to_all(moments, rest, 0, 0, tiled=True)
@@ -336,7 +342,7 @@
         out_shape=jax.ShapeDtypeStruct((3, ROWS, COLS), jnp.float32),
         interpret=INTERPRET,
         name="update",
-    )(*near(moments), latent, *near(basis, *others))
+    )(*near(moments, latent, basis, *others))
 
 
 def solution(mesh):

time: 81.9 us -> 82 us (level)
  blocking collectives: 13.1 us -> 27.7 us
  waiting for transfers between devices: 12.7 us -> 6.65 us
  starting transfers between devices: 44 us -> 38.8 us
  Pallas kernels: 10.8 us -> 8.22 us
    all_to_all x0 -> x1, blocking collectives: none -> 14.6 us  [per_device(): moments = lax.all_to_all(moments, rest, 0, 0, tiled=True)]
    all_to_all x1 -> x0, waiting for transfers between devices: 7.57 us -> none  [per_device(): moments = lax.all_to_all(moments, rest, 0, 0, tiled=True)]
    all_to_all x1 -> x0, starting transfers between devices: 5.16 us -> none  [per_device(): moments = lax.all_to_all(moments, rest, 0, 0, tiled=True)]
    all_to_all x1, waiting for transfers between devices: 4.44 us -> 5.96 us  [per_device(): moments = lax.all_to_all(moments, 'lat', 0, 0, tiled=True).sum(axis=0)]
    pallas_call x1, Pallas kernels: 1.2 us -> 0.18 us  [per_device(): pl.pallas_call(join_kernel, in_specs=[VMEM] * 3, out_specs=[VMEM] * 4, ou...]
    pallas_call x1, Pallas kernels: 1.86 us -> 0.93 us  [per_device(): pl.pallas_call(update_kernel, in_specs=[VMEM] * 6, out_specs=VMEM, out_sh...]
  transfers between devices with their start and end apart: 8 -> 7, of which waited for: 3 -> 2; matrix products, arithmetic and copies ran while one was open for 1% -> 0% of each run, Pallas kernels for 0% -> 0%
where the time goes in v4:
time: 82 us; the launch traced here: 81.6 us
  starting transfers between devices  38.8 us (47%)
  blocking collectives  27.7 us (34%)
  Pallas kernels  8.22 us (10%)
  waiting for transfers between devices  6.65 us (8%)
    all_to_all x1, starting transfers between devices, per_device(): moments = lax.all_to_all(moments, 'lat', 0, 0, tiled=True).sum(axis=0)  22.4 us
    all_to_all x1, blocking collectives, per_device(): moments = lax.all_to_all(moments, rest, 0, 0, tiled=True)  14.6 us
    all_to_all x1, blocking collectives, per_device(): got = lax.all_to_all(part, 'ens', 0, 0, tiled=True)  13.1 us
    ppermute x3, starting transfers between devices, to_neighbour(): return lax.ppermute(value, EVERY, pairs)  9.24 us
    ppermute x3, starting transfers between devices, from_back(): return lax.ppermute(values, 'ens', [(e, (e + back) % 4) for e in range(4)])  7.19 us
    all_to_all x1, waiting for transfers between devices, per_device(): moments = lax.all_to_all(moments, 'lat', 0, 0, tiled=True).sum(axis=0)  5.96 us
    pallas_call x1, Pallas kernels, per_device(): pl.pallas_call(gev_kernel, grid=(4,), in_specs=[pl.BlockSpec((depth, 8, C...  4.96 us
    pallas_call x1, Pallas kernels, per_device(): pl.pallas_call(krylov_kernel, in_specs=[SMEM] + [VMEM] * 5, out_specs=[VM...  2.16 us
  transfers between devices with their start and end apart: 7, of which 2 were waited for; matrix products, arithmetic and copies ran while one was open for 0% of the time, Pallas kernels for 0%

profile of v4, /device:TPU:1, one launch (start us, length us, event | category | flops | bytes accessed | tf_op | source)
XLA Modules:
  0.0 81.6 jit_solution(5172915460266000001)
XLA Ops:
  0.0 0.0 copy-start
  0.0 0.0 copy-start.1
  0.0 5.0 %gev.1 = f32[4,384,128]{2,1,0:T(8,128)S(1)} custom-call(f32[32,32,512]{2,1,0:T(8,128)} %maxima_ref.1, f32[3,32,512]{2,1,0:T(8,128)} %latent_ref.7), custom_call_target="tpu_custom_call" | custom-call | tf_op jit(solution)/shard_map/gev/pallas_call | solution.py:294
  5.0 13.1 %all_to_all.15.got_ref = f32[4,384,128]{2,1,0:T(8,128)S(1)} all-to-all(f32[4,384,128]{2,1,0:T(8,128)S(1)} %gev.1), channel_id=1, replica_groups=mesh['ens'=4,'lat'=16,'lon_0'=4,'lon_1'=2] {'ens'}, dimensions={0} | all-to-all | bytes 1572864 | tf_op jit(solution)/shard_map/all_to_all | solution.py:306
  18.1 0.0 copy-done
  18.1 0.0 copy-done.1
  18.1 0.2 join.1
  18.3 0.7 collective-permute-start
  19.0 7.9 %collective-permute-start.1 = (f32[24,128]{1,0:T(8,128)S(1)}, f32[24,128]{1,0:T(8,128)S(1)}, u32[]{:S(2)}, u32[]{:S(2)}) collective-permute-start(f32[24,128]{1,0:T(8,128)S(1)} %get-tuple-element.15), channel_id=1, source_target_pairs={{1,2},{2,1},{3,4},{4,3},{5,6},{6,5},{9,10},{10,9},{11,12},{12,11},... | collective-permute-start | bytes 36872 | tf_op jit(solution)/shard_map/ppermute | solution.py:289
  26.9 0.7 collective-permute-start.2
  27.6 0.0 collective-permute-done.2.corner_ref
  27.6 0.7 collective-permute-done.1.side_ref
  28.2 0.0 collective-permute-done.edge_ref
  28.2 2.2 %krylov.1 = (f32[9,16,256]{2,1,0:T(8,128)S(1)}, f32[16,1,128]{2,1,0:T(1,128)}) custom-call(f32[3,3]{1,0:T(4,128)} %coupling_ref.1, f32[9,32,512]{2,1,0:T(8,128)S(1)} %get-tuple-element.13.window_ref, f32[3,32,512]{2,1,0:T(8,128)S(1)} %copy-done, f32[48,384]{1,0:T(8,128)S(1)} %collective-permute-done.edge_ref, f32[24,128]{1,0:T(8,128)S(1)} %collective-permute-done.1.side_ref, ...), custom_call_target="tpu_custom_call" | custom-call | tf_op jit(solution)/shard_map/krylov/pallas_call | solution.py:319
  30.4 22.4 %all-to-all-start.1 = ((f32[16,1,128]{2,1,0:T(1,128)}), f32[16,1,128]{2,1,0:T(1,128)S(1)}, u32[]{:S(2)}, u32[]{:S(2)}) async-start(f32[16,1,128]{2,1,0:T(1,128)} %get-tuple-element.18), calls=%async_computation.1 | async-start | bytes 16384 | tf_op jit(solution)/shard_map/all_to_all | solution.py:332
  52.8 1.9 %collective-permute-start.5 = (f32[9,16,256]{2,1,0:T(8,128)S(1)}, f32[9,16,256]{2,1,0:T(8,128)S(1)}, u32[]{:S(2)}, u32[]{:S(2)}) collective-permute-start(f32[9,16,256]{2,1,0:T(8,128)S(1)} %get-tuple-element.20.refs_0_), channel_id=1, source_target_pairs={{0,384},{128,0},{256,128},{384,256},{1,385},{129,1},{257,129},{385... | collective-permute-start | bytes 442376 | tf_op jit(solution)/shard_map/ppermute | solution.py:330
  54.8 3.4 %collective-permute-start.3 = (f32[9,16,256]{2,1,0:T(8,128)S(1)}, f32[9,16,256]{2,1,0:T(8,128)S(1)}, u32[]{:S(2)}, u32[]{:S(2)}) collective-permute-start(f32[9,16,256]{2,1,0:T(8,128)S(1)} %get-tuple-element.20.refs_0_), channel_id=1, source_target_pairs={{0,128},{128,256},{256,384},{384,0},{1,129},{129,257},{257,385},{3... | collective-permute-start | bytes 442376 | tf_op jit(solution)/shard_map/ppermute | solution.py:330
  58.1 6.0 %all-to-all-done.1 = f32[16,1,128]{2,1,0:T(1,128)S(1)} async-done(((f32[16,1,128]{2,1,0:T(1,128)}), f32[16,1,128]{2,1,0:T(1,128)S(1)}, u32[]{:S(2)}, u32[]{:S(2)}) %all-to-all-start.1) | async-done | bytes 8224 | tf_op jit(solution)/shard_map/all_to_all | solution.py:332
  64.1 1.9 %collective-permute-start.4 = (f32[9,16,256]{2,1,0:T(8,128)S(1)}, f32[9,16,256]{2,1,0:T(8,128)S(1)}, u32[]{:S(2)}, u32[]{:S(2)}) collective-permute-start(f32[9,16,256]{2,1,0:T(8,128)S(1)} %get-tuple-element.20.refs_0_), channel_id=1, source_target_pairs={{0,256},{128,384},{256,0},{384,128},{1,257},{129,385},{257,1},{385... | collective-permute-start | bytes 442376 | tf_op jit(solution)/shard_map/ppermute | solution.py:330
  66.0 14.6 %all_to_all.16.moments_ref = f32[32,1,128]{2,1,0:T(1,128)S(1)} all-to-all(f32[32,1,128]{2,1,0:T(1,128)S(1)} %broadcast_in_dim.3), channel_id=1, replica_groups=mesh['ens'=4,'lat'=16,'lon_0'=4,'lon_1'=2] {'ens','lon_0','lon_1'}, dimensions={0} | all-to-all | bytes 32768 | tf_op jit(solution)/shard_map/all_to_all | solution.py:337
  80.7 0.0 collective-permute-done.5.refs_3_
  80.7 0.0 collective-permute-done.3.refs_1_
  80.7 0.0 collective-permute-done.4.refs_2_
  80.7 0.9 %update.1 = f32[3,32,512]{2,1,0:T(8,128)} custom-call(f32[32,1,128]{2,1,0:T(1,128)S(1)} %all_to_all.16.moments_ref, f32[3,32,512]{2,1,0:T(8,128)S(1)} %copy-done, f32[9,16,256]{2,1,0:T(8,128)S(1)} %get-tuple-element.20.refs_0_, f32[9,16,256]{2,1,0:T(8,128)S(1)} %collective-permute-done.3.refs_1_, f32[9,16,256]{2,1,0:T(8,128)S(1)} %collective-permute-done.4.refs_2_, ...), custom_call_target="tpu_custom_call" | custom-call | tf_op jit(solution)/shard_map/update/pallas_call | solution.py:338
  (2 shorter events, 0.0 us)
Async XLA Ops:
  0.0 18.1 %copy-start = (f32[3,32,512]{2,1,0:T(8,128)S(1)}, f32[3,32,512]{2,1,0:T(8,128)}, u32[]{:S(2)}) copy-start(f32[3,32,512]{2,1,0:T(8,128)} %latent_ref.7) | copy-start | bytes 589828
  0.0 18.1 %copy-start.1 = (f32[3,32,512]{2,1,0:T(8,128)S(1)}, f32[3,32,512]{2,1,0:T(8,128)}, u32[]{:S(2)}) copy-start(f32[3,32,512]{2,1,0:T(8,128)} %precision_ref.1) | copy-start | bytes 589828
  18.3 10.0 %collective-permute-start = (f32[48,384]{1,0:T(8,128)S(1)}, f32[48,384]{1,0:T(8,128)S(1)}, u32[]{:S(2)}, u32[]{:S(2)}) collective-permute-start(f32[48,384]{1,0:T(8,128)S(1)} %get-tuple-element.14), channel_id=1, source_target_pairs={{8,16},{9,17},{10,18},{11,19},{12,20},{13,21},{14,22},{15,23},{16,... | collective-permute-start | bytes 221192 | tf_op jit(solution)/shard_map/ppermute | solution.py:289
  19.0 9.3 %collective-permute-start.1 = (f32[24,128]{1,0:T(8,128)S(1)}, f32[24,128]{1,0:T(8,128)S(1)}, u32[]{:S(2)}, u32[]{:S(2)}) collective-permute-start(f32[24,128]{1,0:T(8,128)S(1)} %get-tuple-element.15), channel_id=1, source_target_pairs={{1,2},{2,1},{3,4},{4,3},{5,6},{6,5},{9,10},{10,9},{11,12},{12,11},... | collective-permute-start | bytes 36872 | tf_op jit(solution)/shard_map/ppermute | solution.py:289
  26.9 0.7 collective-permute-start.2
  30.4 33.7 %all-to-all-start.1 = ((f32[16,1,128]{2,1,0:T(1,128)}), f32[16,1,128]{2,1,0:T(1,128)S(1)}, u32[]{:S(2)}, u32[]{:S(2)}) async-start(f32[16,1,128]{2,1,0:T(1,128)} %get-tuple-element.18), calls=%async_computation.1 | async-start | bytes 16384 | tf_op jit(solution)/shard_map/all_to_all | solution.py:332
  52.8 27.8 %collective-permute-start.5 = (f32[9,16,256]{2,1,0:T(8,128)S(1)}, f32[9,16,256]{2,1,0:T(8,128)S(1)}, u32[]{:S(2)}, u32[]{:S(2)}) collective-permute-start(f32[9,16,256]{2,1,0:T(8,128)S(1)} %get-tuple-element.20.refs_0_), channel_id=1, source_target_pairs={{0,384},{128,0},{256,128},{384,256},{1,385},{129,1},{257,129},{385... | collective-permute-start | bytes 442376 | tf_op jit(solution)/shard_map/ppermute | solution.py:330
  54.8 25.9 %collective-permute-start.3 = (f32[9,16,256]{2,1,0:T(8,128)S(1)}, f32[9,16,256]{2,1,0:T(8,128)S(1)}, u32[]{:S(2)}, u32[]{:S(2)}) collective-permute-start(f32[9,16,256]{2,1,0:T(8,128)S(1)} %get-tuple-element.20.refs_0_), channel_id=1, source_target_pairs={{0,128},{128,256},{256,384},{384,0},{1,129},{129,257},{257,385},{3... | collective-permute-start | bytes 442376 | tf_op jit(solution)/shard_map/ppermute | solution.py:330
  64.1 16.6 %collective-permute-start.4 = (f32[9,16,256]{2,1,0:T(8,128)S(1)}, f32[9,16,256]{2,1,0:T(8,128)S(1)}, u32[]{:S(2)}, u32[]{:S(2)}) collective-permute-start(f32[9,16,256]{2,1,0:T(8,128)S(1)} %get-tuple-element.20.refs_0_), channel_id=1, source_target_pairs={{0,256},{128,384},{256,0},{384,128},{1,257},{129,385},{257,1},{385... | collective-permute-start | bytes 442376 | tf_op jit(solution)/shard_map/ppermute | solution.py:330

commit v5 on v4

--- a/solution.py
+++ b/solution.py
@@ -8,6 +8,7 @@
 from jax.sharding import Mesh
 from jax.sharding import PartitionSpec as P
 
+
 ITERS = 3
 LON = ("lon_0", "lon_1")
 EVERY = ("ens", "lat", *LON)
@@ -19,9 +20,14 @@
 SUMS = 9
 FIELDS = 12
 HALO = 4
+DEPTH = (3,) * 3 + (2,) * 6 + (4,) * 3
+ABOVE = [sum(DEPTH[:f]) for f in range(FIELDS)]
 EDGE_AT = SUMS * 2 * 16
-SIDE_AT = EDGE_AT + SUMS * 2 * HALO
+SIDE_AT = EDGE_AT + 48
 PART_ROWS = SIDE_AT + 24
+BLOCK = 40
+BEND_AT = 2 * BLOCK
+EDGE_ROWS = BEND_AT + 8
 
 VMEM = pl.BlockSpec(memory_space=pltpu.VMEM)
 SMEM = pl.BlockSpec(memory_space=pltpu.SMEM)
@@ -86,14 +92,15 @@
                 at = pl.multiple_of((2 * f + t) * 16 + 8 * (block % 2), 8)
                 part_ref[owner, pl.ds(at, 8), :] = sums[f][:, 128 * t : 128 * t + 128]
 
-        def put_edge(to, rows):
+        def put_edge(to, top):
             for f in range(SUMS):
+                rows = slice(0, DEPTH[f]) if top else slice(8 - DEPTH[f], 8)
                 for t in range(2):
-                    at = EDGE_AT + (2 * f + t) * HALO
-                    part_ref[swapped(to), at : at + HALO, :] = sums[f][rows, 128 * t : 128 * t + 128]
-
-        pl.when(block == 2)(lambda: put_edge(half, slice(0, HALO)))
-        pl.when(block == 1)(lambda: put_edge(2 + half, slice(8 - HALO, 8)))
+                    at = EDGE_AT + 24 * t + ABOVE[f]
+                    part_ref[swapped(to), at : at + DEPTH[f], :] = sums[f][rows, 128 * t : 128 * t + 128]
+
+        pl.when(block == 2)(lambda: put_edge(half, True))
+        pl.when(block == 1)(lambda: put_edge(2 + half, False))
 
         near = slice(0, 128) if half else slice(128, 256)
         side = pack_sides([s[:, near] for s in sums], bool(half))
@@ -111,10 +118,14 @@
         cols=slice(128, 512) if ec == 0 else slice(0, 384),
         tile_rows=slice(0, 24) if er == 0 else slice(8, 32),
         tile_cols=slice(0, 384) if ec == 0 else slice(128, 512),
-        inner_rows=slice(24, 28) if er == 0 else slice(4, 8),
-        outer_rows=slice(4, 8) if er == 0 else slice(24, 28),
-        own_edge=slice(8, 12) if er == 0 else slice(20, 24),
-        tile_edge=slice(0, 4) if er == 0 else slice(28, 32),
+        inner_rows=[slice(24, 24 + d) if er == 0 else slice(8 - d, 8) for d in DEPTH],
+        outer_rows=[slice(8 - d, 8) if er == 0 else slice(24, 24 + d) for d in DEPTH],
+        outer_tile=slice(0, 8) if er == 0 else slice(24, 32),
+        own_edge=[slice(8, 8 + d) if er == 0 else slice(24 - d, 24) for d in DEPTH],
+        own_tile=slice(8, 16) if er == 0 else slice(16, 24),
+        tile_edge=slice(0, HALO) if er == 0 else slice(32 - HALO, 32),
+        tile_tile=slice(0, 8) if er == 0 else slice(24, 32),
+        tile_inner=slice(256, 384) if ec == 0 else slice(128, 256),
         inner_cols=slice(384, 512) if ec == 0 else slice(0, 128),
         outer_cols=slice(0, 128) if ec == 0 else slice(384, 512),
         own_side=slice(128, 256) if ec == 0 else slice(256, 384),
@@ -129,7 +140,7 @@
         pl.when(mine == q)(lambda q=q: body(q // 2, q % 2, placing(q // 2, q % 2)))
 
 
-def join_kernel(got_ref, latent_ref, precision_ref, window_ref, edge_ref, side_ref, corner_ref):
+def join_kernel(got_ref, latent_ref, precision_ref, window_ref, send_ref):
     def body(er, ec, at):
         def total(start, rows):
             cut = slice(start, start + rows)
@@ -142,38 +153,51 @@
             for t in range(2):
                 cols = slice(128 + 128 * t, 256 + 128 * t)
                 window_ref[f, 8:24, cols] = total((2 * f + t) * 16, 16)
-                window_ref[f, at["inner_rows"], cols] = total(EDGE_AT + (2 * f + t) * HALO, HALO)
+                window_ref[f, at["inner_rows"][f], cols] = total(EDGE_AT + 24 * t + ABOVE[f], DEPTH[f])
         for k, diagonal in enumerate((3, 6, 8)):
             level = precision_ref[k, at["tile_rows"], at["tile_cols"]]
             here = latent_ref[k, at["tile_rows"], at["tile_cols"]]
             there = (at["rows"], at["cols"])
             window_ref[k, *there] = window_ref[k, *there] - level * here
             window_ref[diagonal, *there] = window_ref[diagonal, *there] + level
+        over = 2 * (1 - er) + ec
         for f in range(FIELDS):
-            edge_ref[HALO * f : HALO * f + HALO, :] = (
-                window_ref[f, at["own_edge"], at["cols"]]
-                if f < SUMS
-                else latent_ref[f - SUMS, at["tile_edge"], at["tile_cols"]]
-            )
+            for t in range(2):
+                rows = slice(BLOCK * t + ABOVE[f], BLOCK * t + ABOVE[f] + DEPTH[f])
+                tile_cols = slice(256 * ec + 128 * t, 256 * ec + 128 * t + 128)
+                send_ref[over, rows, :] = (
+                    window_ref[f, at["own_edge"][f], 128 + 128 * t : 256 + 128 * t]
+                    if f < SUMS
+                    else latent_ref[f - SUMS, at["tile_edge"], tile_cols]
+                )
+        columns = [window_ref[f, at["own_tile"], at["inner_cols"]] for f in range(SUMS)]
+        columns += [latent_ref[k, at["tile_tile"], at["tile_inner"]] for k in range(3)]
+        send_ref[over, BEND_AT:EDGE_ROWS, :] = pack_sides(columns, ec == 0)
         columns = [window_ref[f, at["rows"], at["own_side"]] for f in range(SUMS)]
         columns += [latent_ref[k, at["tile_rows"], at["tile_side"]] for k in range(3)]
         side = pack_sides(columns, ec == 0)
-        side_ref[...] = side
-        corner_ref[...] = side[at["corner"], :]
+        send_ref[2 * er + 1 - ec, 0:24, :] = side
+        send_ref[3 - 2 * er - ec, 0:8, :] = side[at["corner"], :]
 
     for_quarter(body)
 
 
 def krylov_kernel(
-    coupling_ref, window_ref, latent_ref, edge_ref, side_ref, corner_ref, basis_ref, moments_ref, full_ref
+    coupling_ref, window_ref, latent_ref, got_ref, basis_ref, moments_ref, full_ref
 ):
     def body(er, ec, at):
         full_ref[0:SUMS] = window_ref[...]
         full_ref[SUMS:FIELDS, at["rows"], at["cols"]] = latent_ref[:, at["tile_rows"], at["tile_cols"]]
-        parts = [corner_ref[...], side_ref[...]] if er == 0 else [side_ref[...], corner_ref[...]]
+        side, corner = got_ref[2 * er + 1 - ec, 0:24, :], got_ref[3 - 2 * er - ec, 0:8, :]
+        parts = [corner, side] if er == 0 else [side, corner]
         sides = jnp.concatenate(parts, axis=0)
+        over = 2 * (1 - er) + ec
+        bend = got_ref[over, BEND_AT:EDGE_ROWS, :]
         for f in range(FIELDS):
-            full_ref[f, at["outer_rows"], at["cols"]] = edge_ref[HALO * f : HALO * f + HALO, :]
+            for t in range(2):
+                rows = slice(BLOCK * t + ABOVE[f], BLOCK * t + ABOVE[f] + DEPTH[f])
+                full_ref[f, at["outer_rows"][f], 128 + 128 * t : 256 + 128 * t] = got_ref[over, rows, :]
+            full_ref[f, at["outer_tile"], at["inner_cols"]] = unpack_side(bend, f, ec == 0)
             full_ref[f, :, at["outer_cols"]] = unpack_side(sides, f, ec == 1)
 
     for_quarter(body)
@@ -207,7 +231,7 @@
         own = (h[0] * x + h[1] * y + h[2] * z, h[1] * x + h[3] * y + h[4] * z, h[2] * x + h[4] * y + h[5] * z)
         return [jnp.where(inside, SCALE * (a + b), 0.0) for a, b in zip(q, own)]
 
-    prior = mixed([full_ref[SUMS + k] for k in range(3)])
+    prior = mixed([jnp.where(inside, full_ref[SUMS + k], 0.0) for k in range(3)])
     basis = [[jnp.where(inside, full_ref[k] - prior[k], 0.0) for k in range(3)]]
     for _ in range(ITERS):
         basis.append(operate(basis[-1]))
@@ -255,7 +279,7 @@
     moments = [jnp.broadcast_to(moments[:, k : k + 1], (8, 128)) for k in range(2 * ITERS)]
     weights = [jnp.tile(w, (2, 2)) for w in krylov_weights(moments)]
     mine = lax.axis_index("ens")
-    for back, basis_ref in enumerate(basis_refs):
+    for back, basis_ref in zip((0, 2, 1, 3), basis_refs):
         q = swapped(lax.rem(mine + (4 - back), 4))
         rows = pl.ds(pl.multiple_of(16 * (q // 2), 8), 16)
         cols = pl.ds(pl.multiple_of(256 * (q % 2), 128), 256)
@@ -276,17 +300,15 @@
     return tuple(pltpu.with_memory_space_constraint(a, pltpu.VMEM) for a in arrays)
 
 
-def to_neighbour(value, across_lat, across_lon):
+def around_vertices():
     sizes = [lax.axis_size(axis) for axis in EVERY]
     n_lat, n_lon = sizes[1], sizes[2] * sizes[3]
-    pairs = []
+    groups = {}
     for e, lat, lon in itertools.product(range(4), range(n_lat), range(n_lon)):
         lower, right = (e // 2 + lat) % 2, (e + lon) % 2
-        lat_to = lat + (2 * lower - 1) * across_lat
-        lon_to = lon + (2 * right - 1) * across_lon
-        if 0 <= lat_to < n_lat and 0 <= lon_to < n_lon:
-            pairs.append(((e * n_lat + lat) * n_lon + lon, (e * n_lat + lat_to) * n_lon + lon_to))
-    return lax.ppermute(value, EVERY, pairs)
+        vertex = (e, (lat + lower) % n_lat, (lon + right) % n_lon)
+        groups.setdefault(vertex, {})[2 * lower + right] = (e * n_lat + lat) * n_lon + lon
+    return [[group[q] for q in range(4)] for group in groups.values()]
 
 
 def per_device(maxima, latent, coupling, local_precision):
@@ -304,34 +326,34 @@
         name="gev",
     )(maxima, latent)
     got = lax.all_to_all(part, "ens", 0, 0, tiled=True)
-    window, edge, side, corner = pl.pallas_call(
+    window, halo = pl.pallas_call(
         join_kernel,
         in_specs=[VMEM] * 3,
-        out_specs=[VMEM] * 4,
-        out_shape=[f32(SUMS, ROWS, COLS), f32(FIELDS * HALO, 384), f32(24, 128), f32(8, 128)],
+        out_specs=[VMEM] * 2,
+        out_shape=[f32(SUMS, ROWS, COLS), f32(4, EDGE_ROWS, 128)],
         interpret=INTERPRET,
         name="join",
     )(*near(got, latent, local_precision))
-    edge = to_neighbour(edge, 1, 0)
-    side = to_neighbour(side, 0, 1)
-    corner = to_neighbour(corner, 1, 1)
+    halo = lax.all_to_all(halo, EVERY, 0, 0, axis_index_groups=around_vertices(), tiled=True)
     n_lat = lax.axis_size("lat")
     basis, moments = pl.pallas_call(
         krylov_kernel,
-        in_specs=[SMEM] + [VMEM] * 5,
+        in_specs=[SMEM] + [VMEM] * 3,
         out_specs=[VMEM] * 2,
         out_shape=[f32(3 * ITERS, 16, 256), f32(n_lat, 1, 128)],
         scratch_shapes=[pltpu.VMEM((FIELDS, ROWS, COLS), jnp.float32)],
         interpret=INTERPRET,
         name="krylov",
-    )(coupling, *near(window, latent, edge, side, corner))
+    )(coupling, *near(window, latent, halo))
 
     def from_back(values, back):
         return lax.ppermute(values, "ens", [(e, (e + back) % 4) for e in range(4)])
 
-    moments = lax.all_to_all(moments, "lat", 0, 0, tiled=True).sum(axis=0)
-    later, moments = lax.optimization_barrier((basis, moments))
-    others = [from_back(basis, 1), from_back(later, 2), from_back(basis, 3)]
+    moments = lax.all_to_all(moments, "lat", 0, 0, tiled=True)
+    moments = moments.sum(axis=0)
+    others = []
+    for back in (2, 1, 3):
+        others.append(from_back(basis, back))
     rest = ("ens", *LON)
     moments = jnp.broadcast_to(moments, (lax.axis_size(rest), *moments.shape))
     moments = lax.all_to_all(moments, rest, 0, 0, tiled=True)

time: 82 us -> 84.3 us (1.028)
  blocking collectives: 27.7 us -> 68.9 us
  starting transfers between devices: 38.8 us -> 7.2 us
  waiting for transfers between devices: 6.65 us -> 0.01 us
    all_to_all x0 -> x2, blocking collectives: none -> 39.9 us  [the longest x1 22 us: per_device(): lax.all_to_all(halo, EVERY, 0, 0, axis_index_groups=around_vertices(), ti...]
    all_to_all x1 -> x0, starting transfers between devices: 22.4 us -> none  [per_device(): moments = lax.all_to_all(moments, 'lat', 0, 0, tiled=True).sum(axis=0)]
    ppermute x3 -> x0, starting transfers between devices: 9.24 us -> none  [to_neighbour(): return lax.ppermute(value, EVERY, pairs)]
    all_to_all x1 -> x0, waiting for transfers between devices: 5.96 us -> none  [per_device(): moments = lax.all_to_all(moments, 'lat', 0, 0, tiled=True).sum(axis=0)]
    all_to_all x1, blocking collectives: 14.6 us -> 16.2 us  [per_device(): moments = lax.all_to_all(moments, rest, 0, 0, tiled=True)]
  transfers between devices with their start and end apart: 7 -> 3, of which waited for: 2 -> 0; matrix products, arithmetic and copies ran while one was open for 0% -> 0% of each run, Pallas kernels for 0% -> 0%
where the time goes in v5:
time: 84.3 us; the launch traced here: 83.9 us
  blocking collectives  68.9 us (82%)
  Pallas kernels  7.65 us (9%)
  starting transfers between devices  7.2 us (9%)
    all_to_all x1, blocking collectives, per_device(): lax.all_to_all(halo, EVERY, 0, 0, axis_index_groups=around_vertices(), ti...  22 us
    all_to_all x1, blocking collectives, per_device(): moments = lax.all_to_all(moments, 'lat', 0, 0, tiled=True)  17.8 us
    all_to_all x1, blocking collectives, per_device(): moments = lax.all_to_all(moments, rest, 0, 0, tiled=True)  16.2 us
    all_to_all x1, blocking collectives, per_device(): got = lax.all_to_all(part, 'ens', 0, 0, tiled=True)  12.9 us
    ppermute x3, starting transfers between devices, from_back(): return lax.ppermute(values, 'ens', [(e, (e + back) % 4) for e in range(4)])  7.2 us
    pallas_call x1, Pallas kernels, per_device(): pl.pallas_call(gev_kernel, grid=(4,), in_specs=[pl.BlockSpec((depth, 8, C...  4.96 us
  transfers between devices with their start and end apart: 3, of which 0 were waited for; matrix products, arithmetic and copies ran while one was open for 0% of the time, Pallas kernels for 0%

profile of v5, /device:TPU:1, one launch (start us, length us, event | category | flops | bytes accessed | tf_op | source)
XLA Modules:
  0.0 83.9 jit_solution(12264053469162800593)
XLA Ops:
  0.0 0.0 copy-start
  0.0 0.0 copy-start.1
  0.0 5.0 %gev.1 = f32[4,360,128]{2,1,0:T(8,128)S(1)} custom-call(f32[32,32,512]{2,1,0:T(8,128)} %maxima_ref.1, f32[3,32,512]{2,1,0:T(8,128)} %latent_ref.7), custom_call_target="tpu_custom_call" | custom-call | tf_op jit(solution)/shard_map/gev/pallas_call | solution.py:316
  5.0 12.9 %all_to_all.20.got_ref = f32[4,360,128]{2,1,0:T(8,128)S(1)} all-to-all(f32[4,360,128]{2,1,0:T(8,128)S(1)} %gev.1), channel_id=1, replica_groups=mesh['ens'=4,'lat'=16,'lon_0'=4,'lon_1'=2] {'ens'}, dimensions={0} | all-to-all | bytes 1474560 | tf_op jit(solution)/shard_map/all_to_all | solution.py:328
  17.8 0.0 copy-done
  17.8 0.0 copy-done.1
  17.8 0.2 join.1
  18.0 22.0 %all_to_all.21.got_ref = f32[4,88,128]{2,1,0:T(8,128)S(1)} all-to-all(f32[4,88,128]{2,1,0:T(8,128)S(1)} %get-tuple-element.10), channel_id=1, replica_groups={{0,7,120,127},{2,1,122,121},{4,3,124,123},{6,5,126,125},{16,23,8,15},{1..., dimensions={0} | all-to-all | bytes 360448 | tf_op jit(solution)/shard_map/all_to_all | solution.py:337
  40.1 1.6 %krylov.1 = (f32[9,16,256]{2,1,0:T(8,128)S(1)}, f32[16,1,128]{2,1,0:T(1,128)S(1)}) custom-call(f32[3,3]{1,0:T(4,128)} %coupling_ref.1, f32[9,32,512]{2,1,0:T(8,128)S(1)} %get-tuple-element.9.window_ref, f32[3,32,512]{2,1,0:T(8,128)S(1)} %copy-done, f32[4,88,128]{2,1,0:T(8,128)S(1)} %all_to_all.21.got_ref), custom_call_target="tpu_custom_call" | custom-call | tf_op jit(solution)/shard_map/krylov/pallas_call | solution.py:339
  41.6 1.9 %collective-permute-start.2 = (f32[9,16,256]{2,1,0:T(8,128)S(1)}, f32[9,16,256]{2,1,0:T(8,128)S(1)}, u32[]{:S(2)}, u32[]{:S(2)}) collective-permute-start(f32[9,16,256]{2,1,0:T(8,128)S(1)} %get-tuple-element.12.refs_0_), channel_id=1, source_target_pairs={{0,384},{128,0},{256,128},{384,256},{1,385},{129,1},{257,129},{385... | collective-permute-start | bytes 442376 | tf_op jit(solution)/shard_map/ppermute | solution.py:350
  43.6 3.4 %collective-permute-start.1 = (f32[9,16,256]{2,1,0:T(8,128)S(1)}, f32[9,16,256]{2,1,0:T(8,128)S(1)}, u32[]{:S(2)}, u32[]{:S(2)}) collective-permute-start(f32[9,16,256]{2,1,0:T(8,128)S(1)} %get-tuple-element.12.refs_0_), channel_id=1, source_target_pairs={{0,128},{128,256},{256,384},{384,0},{1,129},{129,257},{257,385},{3... | collective-permute-start | bytes 442376 | tf_op jit(solution)/shard_map/ppermute | solution.py:350
  46.9 1.9 %collective-permute-start = (f32[9,16,256]{2,1,0:T(8,128)S(1)}, f32[9,16,256]{2,1,0:T(8,128)S(1)}, u32[]{:S(2)}, u32[]{:S(2)}) collective-permute-start(f32[9,16,256]{2,1,0:T(8,128)S(1)} %get-tuple-element.12.refs_0_), channel_id=1, source_target_pairs={{0,256},{128,384},{256,0},{384,128},{1,257},{129,385},{257,1},{385... | collective-permute-start | bytes 442376 | tf_op jit(solution)/shard_map/ppermute | solution.py:350
  48.9 17.8 %all_to_all.22 = f32[16,1,128]{2,1,0:T(1,128)S(1)} all-to-all(f32[16,1,128]{2,1,0:T(1,128)S(1)} %get-tuple-element.11), channel_id=1, replica_groups=mesh['ens'=4,'lat'=16,'lon_0'=4,'lon_1'=2] {'lat'}, dimensions={0} | all-to-all | bytes 16384 | tf_op jit(solution)/shard_map/all_to_all | solution.py:352
  66.8 16.2 %all_to_all.23.moments_ref = f32[32,1,128]{2,1,0:T(1,128)S(1)} all-to-all(f32[32,1,128]{2,1,0:T(1,128)S(1)} %broadcast_in_dim.3), channel_id=1, replica_groups=mesh['ens'=4,'lat'=16,'lon_0'=4,'lon_1'=2] {'ens','lon_0','lon_1'}, dimensions={0} | all-to-all | bytes 32768 | tf_op jit(solution)/shard_map/all_to_all | solution.py:359
  82.9 0.0 collective-permute-done.2.refs_3_
  82.9 0.0 collective-permute-done.1.refs_2_
  83.0 0.0 collective-permute-done.refs_1_
  83.0 0.9 %update.1 = f32[3,32,512]{2,1,0:T(8,128)} custom-call(f32[32,1,128]{2,1,0:T(1,128)S(1)} %all_to_all.23.moments_ref, f32[3,32,512]{2,1,0:T(8,128)S(1)} %copy-done, f32[9,16,256]{2,1,0:T(8,128)S(1)} %get-tuple-element.12.refs_0_, f32[9,16,256]{2,1,0:T(8,128)S(1)} %collective-permute-done.refs_1_, f32[9,16,256]{2,1,0:T(8,128)S(1)} %collective-permute-done.1.refs_2_, ...), custom_call_target="tpu_custom_call" | custom-call | tf_op jit(solution)/shard_map/update/pallas_call | solution.py:360
  (2 shorter events, 0.0 us)
Async XLA Ops:
  0.0 17.8 %copy-start = (f32[3,32,512]{2,1,0:T(8,128)S(1)}, f32[3,32,512]{2,1,0:T(8,128)}, u32[]{:S(2)}) copy-start(f32[3,32,512]{2,1,0:T(8,128)} %latent_ref.7) | copy-start | bytes 589828
  0.0 17.8 %copy-start.1 = (f32[3,32,512]{2,1,0:T(8,128)S(1)}, f32[3,32,512]{2,1,0:T(8,128)}, u32[]{:S(2)}) copy-start(f32[3,32,512]{2,1,0:T(8,128)} %precision_ref.1) | copy-start | bytes 589828
  41.6 41.3 %collective-permute-start.2 = (f32[9,16,256]{2,1,0:T(8,128)S(1)}, f32[9,16,256]{2,1,0:T(8,128)S(1)}, u32[]{:S(2)}, u32[]{:S(2)}) collective-permute-start(f32[9,16,256]{2,1,0:T(8,128)S(1)} %get-tuple-element.12.refs_0_), channel_id=1, source_target_pairs={{0,384},{128,0},{256,128},{384,256},{1,385},{129,1},{257,129},{385... | collective-permute-start | bytes 442376 | tf_op jit(solution)/shard_map/ppermute | solution.py:350
  43.6 39.4 %collective-permute-start.1 = (f32[9,16,256]{2,1,0:T(8,128)S(1)}, f32[9,16,256]{2,1,0:T(8,128)S(1)}, u32[]{:S(2)}, u32[]{:S(2)}) collective-permute-start(f32[9,16,256]{2,1,0:T(8,128)S(1)} %get-tuple-element.12.refs_0_), channel_id=1, source_target_pairs={{0,128},{128,256},{256,384},{384,0},{1,129},{129,257},{257,385},{3... | collective-permute-start | bytes 442376 | tf_op jit(solution)/shard_map/ppermute | solution.py:350
  46.9 36.0 %collective-permute-start = (f32[9,16,256]{2,1,0:T(8,128)S(1)}, f32[9,16,256]{2,1,0:T(8,128)S(1)}, u32[]{:S(2)}, u32[]{:S(2)}) collective-permute-start(f32[9,16,256]{2,1,0:T(8,128)S(1)} %get-tuple-element.12.refs_0_), channel_id=1, source_target_pairs={{0,256},{128,384},{256,0},{384,128},{1,257},{129,385},{257,1},{385... | collective-permute-start | bytes 442376 | tf_op jit(solution)/shard_map/ppermute | solution.py:350

commit v6 on v5

--- a/solution.py
+++ b/solution.py
@@ -30,7 +30,6 @@
 EDGE_ROWS = BEND_AT + 8
 
 VMEM = pl.BlockSpec(memory_space=pltpu.VMEM)
-SMEM = pl.BlockSpec(memory_space=pltpu.SMEM)
 
 
 def lanes_of(field, shape):
@@ -211,6 +210,10 @@
     col = lax.broadcasted_iota(jnp.int32, shape, 1) + (lon * COLS + 256 * (mine % 2) - 128)
     inside = (row >= 0) & (row < lax.axis_size("lat") * ROWS) & (col >= 0) & (col < n_lon * COLS)
 
+    coupling = [
+        [jnp.broadcast_to(coupling_ref[k : k + 1, j : j + 1], shape) for j in range(3)] for k in range(3)
+    ]
+
     def mixed(field):
         laplace = []
         for x in field:
@@ -218,9 +221,7 @@
             beside = beside + (pltpu.roll(x, 1, 1) + pltpu.roll(x, COLS - 1, 1))
             laplace.append(4.0 * x - beside)
         return [
-            coupling_ref[k, 0] * laplace[0]
-            + coupling_ref[k, 1] * laplace[1]
-            + coupling_ref[k, 2] * laplace[2]
+            coupling[k][0] * laplace[0] + coupling[k][1] * laplace[1] + coupling[k][2] * laplace[2]
             for k in range(3)
         ]
 
@@ -279,7 +280,7 @@
     moments = [jnp.broadcast_to(moments[:, k : k + 1], (8, 128)) for k in range(2 * ITERS)]
     weights = [jnp.tile(w, (2, 2)) for w in krylov_weights(moments)]
     mine = lax.axis_index("ens")
-    for back, basis_ref in zip((0, 2, 1, 3), basis_refs):
+    for back, basis_ref in zip((0, 1, 3, 2), basis_refs):
         q = swapped(lax.rem(mine + (4 - back), 4))
         rows = pl.ds(pl.multiple_of(16 * (q // 2), 8), 16)
         cols = pl.ds(pl.multiple_of(256 * (q % 2), 128), 256)
@@ -338,13 +339,13 @@
     n_lat = lax.axis_size("lat")
     basis, moments = pl.pallas_call(
         krylov_kernel,
-        in_specs=[SMEM] + [VMEM] * 3,
+        in_specs=[VMEM] * 4,
         out_specs=[VMEM] * 2,
         out_shape=[f32(3 * ITERS, 16, 256), f32(n_lat, 1, 128)],
         scratch_shapes=[pltpu.VMEM((FIELDS, ROWS, COLS), jnp.float32)],
         interpret=INTERPRET,
         name="krylov",
-    )(coupling, *near(window, latent, halo))
+    )(*near(coupling, window, latent, halo))
 
     def from_back(values, back):
         return lax.ppermute(values, "ens", [(e, (e + back) % 4) for e in range(4)])
@@ -352,7 +353,7 @@
     moments = lax.all_to_all(moments, "lat", 0, 0, tiled=True)
     moments = moments.sum(axis=0)
     others = []
-    for back in (2, 1, 3):
+    for back in (1, 3, 2):
         others.append(from_back(basis, back))
     rest = ("ens", *LON)
     moments = jnp.broadcast_to(moments, (lax.axis_size(rest), *moments.shape))

time: 84.3 us -> 83.6 us (level)
  no operation moved by 1% of the time
where the time goes in v6:
time: 83.6 us; the launch traced here: 83.2 us
  blocking collectives  68.9 us (82%)
  starting transfers between devices  7.2 us (9%)
  Pallas kernels  6.96 us (8%)
    all_to_all x1, blocking collectives, per_device(): lax.all_to_all(halo, EVERY, 0, 0, axis_index_groups=around_vertices(), ti...  22 us
    all_to_all x1, blocking collectives, per_device(): moments = lax.all_to_all(moments, 'lat', 0, 0, tiled=True)  17.8 us
    all_to_all x1, blocking collectives, per_device(): moments = lax.all_to_all(moments, rest, 0, 0, tiled=True)  16.2 us
    all_to_all x1, blocking collectives, per_device(): got = lax.all_to_all(part, 'ens', 0, 0, tiled=True)  12.9 us
    ppermute x3, starting transfers between devices, from_back(): return lax.ppermute(values, 'ens', [(e, (e + back) % 4) for e in range(4)])  7.2 us
    pallas_call x1, Pallas kernels, per_device(): pl.pallas_call(gev_kernel, grid=(4,), in_specs=[pl.BlockSpec((depth, 8, C...  4.96 us
  transfers between devices with their start and end apart: 3, of which 0 were waited for; matrix products, arithmetic and copies ran while one was open for 0% of the time, Pallas kernels for 0%

profile of v6, /device:TPU:1, one launch (start us, length us, event | category | flops | bytes accessed | tf_op | source)
XLA Modules:
  0.0 83.2 jit_solution(16902689250097970750)
XLA Ops:
  0.0 0.0 copy-start
  0.0 0.0 copy-start.1
  0.0 5.0 %gev.1 = f32[4,360,128]{2,1,0:T(8,128)S(1)} custom-call(f32[32,32,512]{2,1,0:T(8,128)} %maxima_ref.1, f32[3,32,512]{2,1,0:T(8,128)} %latent_ref.7), custom_call_target="tpu_custom_call" | custom-call | tf_op jit(solution)/shard_map/gev/pallas_call | solution.py:317
  5.0 0.0 copy-start.2
  5.0 12.9 %all_to_all.20.got_ref = f32[4,360,128]{2,1,0:T(8,128)S(1)} all-to-all(f32[4,360,128]{2,1,0:T(8,128)S(1)} %gev.1), channel_id=1, replica_groups=mesh['ens'=4,'lat'=16,'lon_0'=4,'lon_1'=2] {'ens'}, dimensions={0} | all-to-all | bytes 1474560 | tf_op jit(solution)/shard_map/all_to_all | solution.py:329
  17.8 0.0 copy-done
  17.9 0.0 copy-done.1
  17.9 0.2 join.1
  18.1 22.0 %all_to_all.21.got_ref = f32[4,88,128]{2,1,0:T(8,128)S(1)} all-to-all(f32[4,88,128]{2,1,0:T(8,128)S(1)} %get-tuple-element.10), channel_id=1, replica_groups={{0,7,120,127},{2,1,122,121},{4,3,124,123},{6,5,126,125},{16,23,8,15},{1..., dimensions={0} | all-to-all | bytes 360448 | tf_op jit(solution)/shard_map/all_to_all | solution.py:338
  40.1 0.0 copy-done.2
  40.1 0.9 %krylov.1 = (f32[9,16,256]{2,1,0:T(8,128)S(1)}, f32[16,1,128]{2,1,0:T(1,128)S(1)}) custom-call(f32[3,3]{1,0:T(4,128)S(1)} %copy-done.2, f32[9,32,512]{2,1,0:T(8,128)S(1)} %get-tuple-element.9.window_ref, f32[3,32,512]{2,1,0:T(8,128)S(1)} %copy-done, f32[4,88,128]{2,1,0:T(8,128)S(1)} %all_to_all.21.got_ref), custom_call_target="tpu_custom_call" | custom-call | tf_op jit(solution)/shard_map/krylov/pallas_call | solution.py:340
  41.0 1.9 %collective-permute-start.2 = (f32[9,16,256]{2,1,0:T(8,128)S(1)}, f32[9,16,256]{2,1,0:T(8,128)S(1)}, u32[]{:S(2)}, u32[]{:S(2)}) collective-permute-start(f32[9,16,256]{2,1,0:T(8,128)S(1)} %get-tuple-element.12.refs_0_), channel_id=1, source_target_pairs={{0,256},{128,384},{256,0},{384,128},{1,257},{129,385},{257,1},{385... | collective-permute-start | bytes 442376 | tf_op jit(solution)/shard_map/ppermute | solution.py:351
  42.9 3.2 %collective-permute-start.1 = (f32[9,16,256]{2,1,0:T(8,128)S(1)}, f32[9,16,256]{2,1,0:T(8,128)S(1)}, u32[]{:S(2)}, u32[]{:S(2)}) collective-permute-start(f32[9,16,256]{2,1,0:T(8,128)S(1)} %get-tuple-element.12.refs_0_), channel_id=1, source_target_pairs={{0,384},{128,0},{256,128},{384,256},{1,385},{129,1},{257,129},{385... | collective-permute-start | bytes 442376 | tf_op jit(solution)/shard_map/ppermute | solution.py:351
  46.0 2.1 %collective-permute-start = (f32[9,16,256]{2,1,0:T(8,128)S(1)}, f32[9,16,256]{2,1,0:T(8,128)S(1)}, u32[]{:S(2)}, u32[]{:S(2)}) collective-permute-start(f32[9,16,256]{2,1,0:T(8,128)S(1)} %get-tuple-element.12.refs_0_), channel_id=1, source_target_pairs={{0,128},{128,256},{256,384},{384,0},{1,129},{129,257},{257,385},{3... | collective-permute-start | bytes 442376 | tf_op jit(solution)/shard_map/ppermute | solution.py:351
  48.2 17.8 %all_to_all.22 = f32[16,1,128]{2,1,0:T(1,128)S(1)} all-to-all(f32[16,1,128]{2,1,0:T(1,128)S(1)} %get-tuple-element.11), channel_id=1, replica_groups=mesh['ens'=4,'lat'=16,'lon_0'=4,'lon_1'=2] {'lat'}, dimensions={0} | all-to-all | bytes 16384 | tf_op jit(solution)/shard_map/all_to_all | solution.py:353
  66.1 16.2 %all_to_all.23.moments_ref = f32[32,1,128]{2,1,0:T(1,128)S(1)} all-to-all(f32[32,1,128]{2,1,0:T(1,128)S(1)} %broadcast_in_dim.3), channel_id=1, replica_groups=mesh['ens'=4,'lat'=16,'lon_0'=4,'lon_1'=2] {'ens','lon_0','lon_1'}, dimensions={0} | all-to-all | bytes 32768 | tf_op jit(solution)/shard_map/all_to_all | solution.py:360
  82.3 0.0 collective-permute-done.2.refs_3_
  82.3 0.0 collective-permute-done.1.refs_2_
  82.3 0.0 collective-permute-done.refs_1_
  82.3 0.9 %update.1 = f32[3,32,512]{2,1,0:T(8,128)} custom-call(f32[32,1,128]{2,1,0:T(1,128)S(1)} %all_to_all.23.moments_ref, f32[3,32,512]{2,1,0:T(8,128)S(1)} %copy-done, f32[9,16,256]{2,1,0:T(8,128)S(1)} %get-tuple-element.12.refs_0_, f32[9,16,256]{2,1,0:T(8,128)S(1)} %collective-permute-done.refs_1_, f32[9,16,256]{2,1,0:T(8,128)S(1)} %collective-permute-done.1.refs_2_, ...), custom_call_target="tpu_custom_call" | custom-call | tf_op jit(solution)/shard_map/update/pallas_call | solution.py:361
  (2 shorter events, 0.0 us)
Async XLA Ops:
  0.0 17.9 %copy-start = (f32[3,32,512]{2,1,0:T(8,128)S(1)}, f32[3,32,512]{2,1,0:T(8,128)}, u32[]{:S(2)}) copy-start(f32[3,32,512]{2,1,0:T(8,128)} %latent_ref.7) | copy-start | bytes 589828
  0.0 17.9 %copy-start.1 = (f32[3,32,512]{2,1,0:T(8,128)S(1)}, f32[3,32,512]{2,1,0:T(8,128)}, u32[]{:S(2)}) copy-start(f32[3,32,512]{2,1,0:T(8,128)} %precision_ref.1) | copy-start | bytes 589828
  5.0 35.1 %copy-start.2 = (f32[3,3]{1,0:T(4,128)S(1)}, f32[3,3]{1,0:T(4,128)}, u32[]{:S(2)}) copy-start(f32[3,3]{1,0:T(4,128)} %coupling_ref.1) | copy-start | bytes 112
  41.0 41.3 %collective-permute-start.2 = (f32[9,16,256]{2,1,0:T(8,128)S(1)}, f32[9,16,256]{2,1,0:T(8,128)S(1)}, u32[]{:S(2)}, u32[]{:S(2)}) collective-permute-start(f32[9,16,256]{2,1,0:T(8,128)S(1)} %get-tuple-element.12.refs_0_), channel_id=1, source_target_pairs={{0,256},{128,384},{256,0},{384,128},{1,257},{129,385},{257,1},{385... | collective-permute-start | bytes 442376 | tf_op jit(solution)/shard_map/ppermute | solution.py:351
  42.9 39.4 %collective-permute-start.1 = (f32[9,16,256]{2,1,0:T(8,128)S(1)}, f32[9,16,256]{2,1,0:T(8,128)S(1)}, u32[]{:S(2)}, u32[]{:S(2)}) collective-permute-start(f32[9,16,256]{2,1,0:T(8,128)S(1)} %get-tuple-element.12.refs_0_), channel_id=1, source_target_pairs={{0,384},{128,0},{256,128},{384,256},{1,385},{129,1},{257,129},{385... | collective-permute-start | bytes 442376 | tf_op jit(solution)/shard_map/ppermute | solution.py:351
  46.0 36.2 %collective-permute-start = (f32[9,16,256]{2,1,0:T(8,128)S(1)}, f32[9,16,256]{2,1,0:T(8,128)S(1)}, u32[]{:S(2)}, u32[]{:S(2)}) collective-permute-start(f32[9,16,256]{2,1,0:T(8,128)S(1)} %get-tuple-element.12.refs_0_), channel_id=1, source_target_pairs={{0,128},{128,256},{256,384},{384,0},{1,129},{129,257},{257,385},{3... | collective-permute-start | bytes 442376 | tf_op jit(solution)/shard_map/ppermute | solution.py:351

commit v7 on v6

--- a/solution.py
+++ b/solution.py
@@ -336,12 +336,12 @@
         name="join",
     )(*near(got, latent, local_precision))
     halo = lax.all_to_all(halo, EVERY, 0, 0, axis_index_groups=around_vertices(), tiled=True)
-    n_lat = lax.axis_size("lat")
+    n_column = lax.axis_size(("lat", LON[1]))
     basis, moments = pl.pallas_call(
         krylov_kernel,
         in_specs=[VMEM] * 4,
         out_specs=[VMEM] * 2,
-        out_shape=[f32(3 * ITERS, 16, 256), f32(n_lat, 1, 128)],
+        out_shape=[f32(3 * ITERS, 16, 256), f32(n_column, 1, 128)],
         scratch_shapes=[pltpu.VMEM((FIELDS, ROWS, COLS), jnp.float32)],
         interpret=INTERPRET,
         name="krylov",
@@ -350,12 +350,12 @@
     def from_back(values, back):
         return lax.ppermute(values, "ens", [(e, (e + back) % 4) for e in range(4)])
 
-    moments = lax.all_to_all(moments, "lat", 0, 0, tiled=True)
+    moments = lax.all_to_all(moments, ("lat", LON[1]), 0, 0, tiled=True)
     moments = moments.sum(axis=0)
     others = []
     for back in (1, 3, 2):
         others.append(from_back(basis, back))
-    rest = ("ens", *LON)
+    rest = ("ens", LON[0])
     moments = jnp.broadcast_to(moments, (lax.axis_size(rest), *moments.shape))
     moments = lax.all_to_all(moments, rest, 0, 0, tiled=True)
     return pl.pallas_call(

time: 83.6 us -> 82.1 us (0.982)
  blocking collectives: 68.9 us -> 67.5 us
    all_to_all x1, blocking collectives: 16.2 us -> 12.6 us  [per_device(): moments = lax.all_to_all(moments, rest, 0, 0, tiled=True)]
    all_to_all x1, blocking collectives: 17.8 us -> 19.9 us  [per_device(): moments = lax.all_to_all(moments, ('lat', LON[1]), 0, 0, tiled=True)]
where the time goes in v7:
time: 82.1 us; the launch traced here: 81.7 us
  blocking collectives  67.5 us (82%)
  starting transfers between devices  7.2 us (9%)
  Pallas kernels  6.95 us (8%)
    all_to_all x1, blocking collectives, per_device(): lax.all_to_all(halo, EVERY, 0, 0, axis_index_groups=around_vertices(), ti...  22 us
    all_to_all x1, blocking collectives, per_device(): moments = lax.all_to_all(moments, ('lat', LON[1]), 0, 0, tiled=True)  19.9 us
    all_to_all x1, blocking collectives, per_device(): got = lax.all_to_all(part, 'ens', 0, 0, tiled=True)  12.9 us
    all_to_all x1, blocking collectives, per_device(): moments = lax.all_to_all(moments, rest, 0, 0, tiled=True)  12.6 us
    ppermute x3, starting transfers between devices, from_back(): return lax.ppermute(values, 'ens', [(e, (e + back) % 4) for e in range(4)])  7.2 us
    pallas_call x1, Pallas kernels, per_device(): pl.pallas_call(gev_kernel, grid=(4,), in_specs=[pl.BlockSpec((depth, 8, C...  4.96 us
  transfers between devices with their start and end apart: 3, of which 0 were waited for; matrix products, arithmetic and copies ran while one was open for 0% of the time, Pallas kernels for 0%

profile of v7, /device:TPU:1, one launch (start us, length us, event | category | flops | bytes accessed | tf_op | source)
XLA Modules:
  0.0 81.7 jit_solution(10707169934861413086)
XLA Ops:
  0.0 0.0 copy-start
  0.0 0.0 copy-start.1
  0.0 5.0 %gev.1 = f32[4,360,128]{2,1,0:T(8,128)S(1)} custom-call(f32[32,32,512]{2,1,0:T(8,128)} %maxima_ref.1, f32[3,32,512]{2,1,0:T(8,128)} %latent_ref.7), custom_call_target="tpu_custom_call" | custom-call | tf_op jit(solution)/shard_map/gev/pallas_call | solution.py:317
  5.0 0.0 copy-start.2
  5.0 12.9 %all_to_all.20.got_ref = f32[4,360,128]{2,1,0:T(8,128)S(1)} all-to-all(f32[4,360,128]{2,1,0:T(8,128)S(1)} %gev.1), channel_id=1, replica_groups=mesh['ens'=4,'lat'=16,'lon_0'=4,'lon_1'=2] {'ens'}, dimensions={0} | all-to-all | bytes 1474560 | tf_op jit(solution)/shard_map/all_to_all | solution.py:329
  17.8 0.0 copy-done
  17.9 0.0 copy-done.1
  17.9 0.2 join.1
  18.1 22.0 %all_to_all.21.got_ref = f32[4,88,128]{2,1,0:T(8,128)S(1)} all-to-all(f32[4,88,128]{2,1,0:T(8,128)S(1)} %get-tuple-element.10), channel_id=1, replica_groups={{0,7,120,127},{2,1,122,121},{4,3,124,123},{6,5,126,125},{16,23,8,15},{1..., dimensions={0} | all-to-all | bytes 360448 | tf_op jit(solution)/shard_map/all_to_all | solution.py:338
  40.1 0.0 copy-done.2
  40.1 0.9 %krylov.1 = (f32[9,16,256]{2,1,0:T(8,128)S(1)}, f32[32,1,128]{2,1,0:T(1,128)S(1)}) custom-call(f32[3,3]{1,0:T(4,128)S(1)} %copy-done.2, f32[9,32,512]{2,1,0:T(8,128)S(1)} %get-tuple-element.9.window_ref, f32[3,32,512]{2,1,0:T(8,128)S(1)} %copy-done, f32[4,88,128]{2,1,0:T(8,128)S(1)} %all_to_all.21.got_ref), custom_call_target="tpu_custom_call" | custom-call | tf_op jit(solution)/shard_map/krylov/pallas_call | solution.py:340
  41.0 1.9 %collective-permute-start.2 = (f32[9,16,256]{2,1,0:T(8,128)S(1)}, f32[9,16,256]{2,1,0:T(8,128)S(1)}, u32[]{:S(2)}, u32[]{:S(2)}) collective-permute-start(f32[9,16,256]{2,1,0:T(8,128)S(1)} %get-tuple-element.12.refs_0_), channel_id=1, source_target_pairs={{0,256},{128,384},{256,0},{384,128},{1,257},{129,385},{257,1},{385... | collective-permute-start | bytes 442376 | tf_op jit(solution)/shard_map/ppermute | solution.py:351
  42.9 3.2 %collective-permute-start.1 = (f32[9,16,256]{2,1,0:T(8,128)S(1)}, f32[9,16,256]{2,1,0:T(8,128)S(1)}, u32[]{:S(2)}, u32[]{:S(2)}) collective-permute-start(f32[9,16,256]{2,1,0:T(8,128)S(1)} %get-tuple-element.12.refs_0_), channel_id=1, source_target_pairs={{0,384},{128,0},{256,128},{384,256},{1,385},{129,1},{257,129},{385... | collective-permute-start | bytes 442376 | tf_op jit(solution)/shard_map/ppermute | solution.py:351
  46.1 2.1 %collective-permute-start = (f32[9,16,256]{2,1,0:T(8,128)S(1)}, f32[9,16,256]{2,1,0:T(8,128)S(1)}, u32[]{:S(2)}, u32[]{:S(2)}) collective-permute-start(f32[9,16,256]{2,1,0:T(8,128)S(1)} %get-tuple-element.12.refs_0_), channel_id=1, source_target_pairs={{0,128},{128,256},{256,384},{384,0},{1,129},{129,257},{257,385},{3... | collective-permute-start | bytes 442376 | tf_op jit(solution)/shard_map/ppermute | solution.py:351
  48.2 19.9 %all_to_all.22 = f32[32,1,128]{2,1,0:T(1,128)S(1)} all-to-all(f32[32,1,128]{2,1,0:T(1,128)S(1)} %get-tuple-element.11), channel_id=1, replica_groups=mesh['ens'=4,'lat'=16,'lon_0'=4,'lon_1'=2] {'lat','lon_1'}, dimensions={0} | all-to-all | bytes 32768 | tf_op jit(solution)/shard_map/all_to_all | solution.py:353
  68.1 0.1 reduce_sum.9
  68.2 12.6 %all_to_all.23.moments_ref = f32[16,1,128]{2,1,0:T(1,128)S(1)} all-to-all(f32[16,1,128]{2,1,0:T(1,128)S(1)} %broadcast_in_dim.3), channel_id=1, replica_groups=mesh['ens'=4,'lat'=16,'lon_0'=4,'lon_1'=2] {'ens','lon_0'}, dimensions={0} | all-to-all | bytes 16384 | tf_op jit(solution)/shard_map/all_to_all | solution.py:360
  80.8 0.0 collective-permute-done.2.refs_3_
  80.8 0.0 collective-permute-done.1.refs_2_
  80.8 0.0 collective-permute-done.refs_1_
  80.8 0.9 %update.1 = f32[3,32,512]{2,1,0:T(8,128)} custom-call(f32[16,1,128]{2,1,0:T(1,128)S(1)} %all_to_all.23.moments_ref, f32[3,32,512]{2,1,0:T(8,128)S(1)} %copy-done, f32[9,16,256]{2,1,0:T(8,128)S(1)} %get-tuple-element.12.refs_0_, f32[9,16,256]{2,1,0:T(8,128)S(1)} %collective-permute-done.refs_1_, f32[9,16,256]{2,1,0:T(8,128)S(1)} %collective-permute-done.1.refs_2_, ...), custom_call_target="tpu_custom_call" | custom-call | tf_op jit(solution)/shard_map/update/pallas_call | solution.py:361
  (1 shorter events, 0.0 us)
Async XLA Ops:
  0.0 17.9 %copy-start = (f32[3,32,512]{2,1,0:T(8,128)S(1)}, f32[3,32,512]{2,1,0:T(8,128)}, u32[]{:S(2)}) copy-start(f32[3,32,512]{2,1,0:T(8,128)} %latent_ref.7) | copy-start | bytes 589828
  0.0 17.9 %copy-start.1 = (f32[3,32,512]{2,1,0:T(8,128)S(1)}, f32[3,32,512]{2,1,0:T(8,128)}, u32[]{:S(2)}) copy-start(f32[3,32,512]{2,1,0:T(8,128)} %precision_ref.1) | copy-start | bytes 589828
  5.0 35.1 %copy-start.2 = (f32[3,3]{1,0:T(4,128)S(1)}, f32[3,3]{1,0:T(4,128)}, u32[]{:S(2)}) copy-start(f32[3,3]{1,0:T(4,128)} %coupling_ref.1) | copy-start | bytes 112
  41.0 39.9 %collective-permute-start.2 = (f32[9,16,256]{2,1,0:T(8,128)S(1)}, f32[9,16,256]{2,1,0:T(8,128)S(1)}, u32[]{:S(2)}, u32[]{:S(2)}) collective-permute-start(f32[9,16,256]{2,1,0:T(8,128)S(1)} %get-tuple-element.12.refs_0_), channel_id=1, source_target_pairs={{0,256},{128,384},{256,0},{384,128},{1,257},{129,385},{257,1},{385... | collective-permute-start | bytes 442376 | tf_op jit(solution)/shard_map/ppermute | solution.py:351
  42.9 37.9 %collective-permute-start.1 = (f32[9,16,256]{2,1,0:T(8,128)S(1)}, f32[9,16,256]{2,1,0:T(8,128)S(1)}, u32[]{:S(2)}, u32[]{:S(2)}) collective-permute-start(f32[9,16,256]{2,1,0:T(8,128)S(1)} %get-tuple-element.12.refs_0_), channel_id=1, source_target_pairs={{0,384},{128,0},{256,128},{384,256},{1,385},{129,1},{257,129},{385... | collective-permute-start | bytes 442376 | tf_op jit(solution)/shard_map/ppermute | solution.py:351
  46.1 34.8 %collective-permute-start = (f32[9,16,256]{2,1,0:T(8,128)S(1)}, f32[9,16,256]{2,1,0:T(8,128)S(1)}, u32[]{:S(2)}, u32[]{:S(2)}) collective-permute-start(f32[9,16,256]{2,1,0:T(8,128)S(1)} %get-tuple-element.12.refs_0_), channel_id=1, source_target_pairs={{0,128},{128,256},{256,384},{384,0},{1,129},{129,257},{257,385},{3... | collective-permute-start | bytes 442376 | tf_op jit(solution)/shard_map/ppermute | solution.py:351

commit v8 on v7

--- a/solution.py
+++ b/solution.py
@@ -22,11 +22,11 @@
 HALO = 4
 DEPTH = (3,) * 3 + (2,) * 6 + (4,) * 3
 ABOVE = [sum(DEPTH[:f]) for f in range(FIELDS)]
-EDGE_AT = SUMS * 2 * 16
-SIDE_AT = EDGE_AT + 48
-PART_ROWS = SIDE_AT + 24
-BLOCK = 40
-BEND_AT = 2 * BLOCK
+SIDE_AT = SUMS * 2 * 16
+EDGE_AT = SIDE_AT + 8
+PART_ROWS = EDGE_AT + 48
+BLOCK = 33
+BEND_AT = 72
 EDGE_ROWS = BEND_AT + 8
 
 VMEM = pl.BlockSpec(memory_space=pltpu.VMEM)
@@ -80,7 +80,7 @@
             return tuple(s + t for s, t in zip(sums, terms))
 
         zero = jnp.zeros((8, 256), jnp.float32)
-        sums = lax.fori_loop(0, maxima_ref.shape[0], add_one, (zero,) * SUMS, unroll=8)
+        sums = lax.fori_loop(0, maxima_ref.shape[0], add_one, (zero,) * SUMS, unroll=16)
         ka, kc = 10.0 * per_scale, 0.1 / shape_par
         factors = (ka, None, kc, ka * ka, ka, ka * kc, None, kc, kc * kc)
         sums = [s if k is None else s * k for s, k in zip(sums, factors)]
@@ -95,7 +95,7 @@
             for f in range(SUMS):
                 rows = slice(0, DEPTH[f]) if top else slice(8 - DEPTH[f], 8)
                 for t in range(2):
-                    at = EDGE_AT + 24 * t + ABOVE[f]
+                    at = EDGE_AT + 21 * t + ABOVE[f]
                     part_ref[swapped(to), at : at + DEPTH[f], :] = sums[f][rows, 128 * t : 128 * t + 128]
 
         pl.when(block == 2)(lambda: put_edge(half, True))
@@ -105,10 +105,15 @@
         side = pack_sides([s[:, near] for s in sums], bool(half))
 
         def put_side(to, tile):
-            part_ref[swapped(to), pl.ds(pl.multiple_of(SIDE_AT + 8 * tile, 8), 8), :] = side
-
-        pl.when(block <= 2)(lambda: put_side(1 - half, block))
-        pl.when(block >= 1)(lambda: put_side(3 - half, block - 1))
+            at = HALO * SUMS * tile
+            shifted = pltpu.roll(side, at, 1) if at else side
+            here = part_ref[swapped(to), SIDE_AT : SIDE_AT + 8, :]
+            lane = lax.broadcasted_iota(jnp.int32, (8, 128), 1)
+            part_ref[swapped(to), SIDE_AT : SIDE_AT + 8, :] = jnp.where(lane >= at, shifted, here)
+
+        for i in range(3):
+            pl.when(block == i)(lambda i=i: put_side(1 - half, i))
+            pl.when(block == i + 1)(lambda i=i: put_side(3 - half, i))
 
 
 def placing(er, ec):
@@ -146,13 +151,15 @@
             return got_ref[0, cut, :] + got_ref[1, cut, :] + got_ref[2, cut, :] + got_ref[3, cut, :]
 
         window_ref[...] = jnp.zeros(window_ref.shape, jnp.float32)
-        sides = total(SIDE_AT, 24)
+        sides = total(SIDE_AT, 8)
+        sides = [pltpu.roll(sides, 128 - HALO * SUMS * i, 1) if i else sides for i in range(3)]
+        sides = jnp.concatenate(sides, axis=0)
         for f in range(SUMS):
             window_ref[f, at["rows"], at["inner_cols"]] = unpack_side(sides, f, ec == 0)
             for t in range(2):
                 cols = slice(128 + 128 * t, 256 + 128 * t)
                 window_ref[f, 8:24, cols] = total((2 * f + t) * 16, 16)
-                window_ref[f, at["inner_rows"][f], cols] = total(EDGE_AT + 24 * t + ABOVE[f], DEPTH[f])
+                window_ref[f, at["inner_rows"][f], cols] = total(EDGE_AT + 21 * t + ABOVE[f], DEPTH[f])
         for k, diagonal in enumerate((3, 6, 8)):
             level = precision_ref[k, at["tile_rows"], at["tile_cols"]]
             here = latent_ref[k, at["tile_rows"], at["tile_cols"]]
@@ -280,7 +287,7 @@
     moments = [jnp.broadcast_to(moments[:, k : k + 1], (8, 128)) for k in range(2 * ITERS)]
     weights = [jnp.tile(w, (2, 2)) for w in krylov_weights(moments)]
     mine = lax.axis_index("ens")
-    for back, basis_ref in zip((0, 1, 3, 2), basis_refs):
+    for back, basis_ref in zip((0, 3, 1, 2), basis_refs):
         q = swapped(lax.rem(mine + (4 - back), 4))
         rows = pl.ds(pl.multiple_of(16 * (q // 2), 8), 16)
         cols = pl.ds(pl.multiple_of(256 * (q % 2), 128), 256)
@@ -353,7 +360,7 @@
     moments = lax.all_to_all(moments, ("lat", LON[1]), 0, 0, tiled=True)
     moments = moments.sum(axis=0)
     others = []
-    for back in (1, 3, 2):
+    for back in (3, 1, 2):
         others.append(from_back(basis, back))
     rest = ("ens", LON[0])
     moments = jnp.broadcast_to(moments, (lax.axis_size(rest), *moments.shape))

time: 82.1 us -> 81.9 us (level)
  blocking collectives: 67.5 us -> 65.8 us
  starting transfers between devices: 7.2 us -> 8.41 us
    all_to_all x1, blocking collectives: 12.6 us -> 11.2 us  [per_device(): moments = lax.all_to_all(moments, rest, 0, 0, tiled=True)]
    ppermute x3, starting transfers between devices: 7.2 us -> 8.41 us  [from_back(): return lax.ppermute(values, 'ens', [(e, (e + back) % 4) for e in range(4)])]
where the time goes in v8:
time: 81.9 us; the launch traced here: 81.5 us
  blocking collectives  65.8 us (80%)
  starting transfers between devices  8.41 us (10%)
  Pallas kernels  7.1 us (9%)
    all_to_all x1, blocking collectives, per_device(): lax.all_to_all(halo, EVERY, 0, 0, axis_index_groups=around_vertices(), ti...  21.7 us
    all_to_all x1, blocking collectives, per_device(): moments = lax.all_to_all(moments, ('lat', LON[1]), 0, 0, tiled=True)  20.1 us
    all_to_all x1, blocking collectives, per_device(): got = lax.all_to_all(part, 'ens', 0, 0, tiled=True)  12.8 us
    all_to_all x1, blocking collectives, per_device(): moments = lax.all_to_all(moments, rest, 0, 0, tiled=True)  11.2 us
    ppermute x3, starting transfers between devices, from_back(): return lax.ppermute(values, 'ens', [(e, (e + back) % 4) for e in range(4)])  8.41 us
    pallas_call x1, Pallas kernels, per_device(): pl.pallas_call(gev_kernel, grid=(4,), in_specs=[pl.BlockSpec((depth, 8, C...  5.08 us
  transfers between devices with their start and end apart: 3, of which 0 were waited for; matrix products, arithmetic and copies ran while one was open for 0% of the time, Pallas kernels for 0%

profile of v8, /device:TPU:1, one launch (start us, length us, event | category | flops | bytes accessed | tf_op | source)
XLA Modules:
  0.0 81.5 jit_solution(17989894808713245952)
XLA Ops:
  0.0 0.0 copy-start
  0.0 0.0 copy-start.1
  0.0 5.1 %gev.1 = f32[4,344,128]{2,1,0:T(8,128)S(1)} custom-call(f32[32,32,512]{2,1,0:T(8,128)} %maxima_ref.1, f32[3,32,512]{2,1,0:T(8,128)} %latent_ref.7), custom_call_target="tpu_custom_call" | custom-call | tf_op jit(solution)/shard_map/gev/pallas_call | solution.py:324
  5.1 0.0 copy-start.2
  5.1 12.8 %all_to_all.20.got_ref = f32[4,344,128]{2,1,0:T(8,128)S(1)} all-to-all(f32[4,344,128]{2,1,0:T(8,128)S(1)} %gev.1), channel_id=1, replica_groups=mesh['ens'=4,'lat'=16,'lon_0'=4,'lon_1'=2] {'ens'}, dimensions={0} | all-to-all | bytes 1409024 | tf_op jit(solution)/shard_map/all_to_all | solution.py:336
  17.9 0.0 copy-done
  17.9 0.0 copy-done.1
  17.9 0.2 join.1
  18.1 21.7 %all_to_all.21.got_ref = f32[4,80,128]{2,1,0:T(8,128)S(1)} all-to-all(f32[4,80,128]{2,1,0:T(8,128)S(1)} %get-tuple-element.10), channel_id=1, replica_groups={{0,7,120,127},{2,1,122,121},{4,3,124,123},{6,5,126,125},{16,23,8,15},{1..., dimensions={0} | all-to-all | bytes 327680 | tf_op jit(solution)/shard_map/all_to_all | solution.py:345
  39.9 0.0 copy-done.2
  39.9 0.9 %krylov.1 = (f32[9,16,256]{2,1,0:T(8,128)S(1)}, f32[32,1,128]{2,1,0:T(1,128)S(1)}) custom-call(f32[3,3]{1,0:T(4,128)S(1)} %copy-done.2, f32[9,32,512]{2,1,0:T(8,128)S(1)} %get-tuple-element.9.window_ref, f32[3,32,512]{2,1,0:T(8,128)S(1)} %copy-done, f32[4,80,128]{2,1,0:T(8,128)S(1)} %all_to_all.21.got_ref), custom_call_target="tpu_custom_call" | custom-call | tf_op jit(solution)/shard_map/krylov/pallas_call | solution.py:347
  40.7 1.9 %collective-permute-start.2 = (f32[9,16,256]{2,1,0:T(8,128)S(1)}, f32[9,16,256]{2,1,0:T(8,128)S(1)}, u32[]{:S(2)}, u32[]{:S(2)}) collective-permute-start(f32[9,16,256]{2,1,0:T(8,128)S(1)} %get-tuple-element.12.refs_0_), channel_id=1, source_target_pairs={{0,256},{128,384},{256,0},{384,128},{1,257},{129,385},{257,1},{385... | collective-permute-start | bytes 442376 | tf_op jit(solution)/shard_map/ppermute | solution.py:358
  42.7 1.9 %collective-permute-start.1 = (f32[9,16,256]{2,1,0:T(8,128)S(1)}, f32[9,16,256]{2,1,0:T(8,128)S(1)}, u32[]{:S(2)}, u32[]{:S(2)}) collective-permute-start(f32[9,16,256]{2,1,0:T(8,128)S(1)} %get-tuple-element.12.refs_0_), channel_id=1, source_target_pairs={{0,128},{128,256},{256,384},{384,0},{1,129},{129,257},{257,385},{3... | collective-permute-start | bytes 442376 | tf_op jit(solution)/shard_map/ppermute | solution.py:358
  44.6 4.6 %collective-permute-start = (f32[9,16,256]{2,1,0:T(8,128)S(1)}, f32[9,16,256]{2,1,0:T(8,128)S(1)}, u32[]{:S(2)}, u32[]{:S(2)}) collective-permute-start(f32[9,16,256]{2,1,0:T(8,128)S(1)} %get-tuple-element.12.refs_0_), channel_id=1, source_target_pairs={{0,384},{128,0},{256,128},{384,256},{1,385},{129,1},{257,129},{385... | collective-permute-start | bytes 442376 | tf_op jit(solution)/shard_map/ppermute | solution.py:358
  49.2 20.1 %all_to_all.22 = f32[32,1,128]{2,1,0:T(1,128)S(1)} all-to-all(f32[32,1,128]{2,1,0:T(1,128)S(1)} %get-tuple-element.11), channel_id=1, replica_groups=mesh['ens'=4,'lat'=16,'lon_0'=4,'lon_1'=2] {'lat','lon_1'}, dimensions={0} | all-to-all | bytes 32768 | tf_op jit(solution)/shard_map/all_to_all | solution.py:360
  69.2 0.1 reduce_sum.9
  69.3 11.2 %all_to_all.23.moments_ref = f32[16,1,128]{2,1,0:T(1,128)S(1)} all-to-all(f32[16,1,128]{2,1,0:T(1,128)S(1)} %broadcast_in_dim.3), channel_id=1, replica_groups=mesh['ens'=4,'lat'=16,'lon_0'=4,'lon_1'=2] {'ens','lon_0'}, dimensions={0} | all-to-all | bytes 16384 | tf_op jit(solution)/shard_map/all_to_all | solution.py:367
  80.5 0.0 collective-permute-done.2.refs_3_
  80.5 0.0 collective-permute-done.1.refs_2_
  80.6 0.0 collective-permute-done.refs_1_
  80.6 0.9 %update.1 = f32[3,32,512]{2,1,0:T(8,128)} custom-call(f32[16,1,128]{2,1,0:T(1,128)S(1)} %all_to_all.23.moments_ref, f32[3,32,512]{2,1,0:T(8,128)S(1)} %copy-done, f32[9,16,256]{2,1,0:T(8,128)S(1)} %get-tuple-element.12.refs_0_, f32[9,16,256]{2,1,0:T(8,128)S(1)} %collective-permute-done.refs_1_, f32[9,16,256]{2,1,0:T(8,128)S(1)} %collective-permute-done.1.refs_2_, ...), custom_call_target="tpu_custom_call" | custom-call | tf_op jit(solution)/shard_map/update/pallas_call | solution.py:368
  (1 shorter events, 0.0 us)
Async XLA Ops:
  0.0 17.9 %copy-start = (f32[3,32,512]{2,1,0:T(8,128)S(1)}, f32[3,32,512]{2,1,0:T(8,128)}, u32[]{:S(2)}) copy-start(f32[3,32,512]{2,1,0:T(8,128)} %latent_ref.7) | copy-start | bytes 589828
  0.0 17.9 %copy-start.1 = (f32[3,32,512]{2,1,0:T(8,128)S(1)}, f32[3,32,512]{2,1,0:T(8,128)}, u32[]{:S(2)}) copy-start(f32[3,32,512]{2,1,0:T(8,128)} %precision_ref.1) | copy-start | bytes 589828
  5.1 34.8 %copy-start.2 = (f32[3,3]{1,0:T(4,128)S(1)}, f32[3,3]{1,0:T(4,128)}, u32[]{:S(2)}) copy-start(f32[3,3]{1,0:T(4,128)} %coupling_ref.1) | copy-start | bytes 112
  40.7 39.8 %collective-permute-start.2 = (f32[9,16,256]{2,1,0:T(8,128)S(1)}, f32[9,16,256]{2,1,0:T(8,128)S(1)}, u32[]{:S(2)}, u32[]{:S(2)}) collective-permute-start(f32[9,16,256]{2,1,0:T(8,128)S(1)} %get-tuple-element.12.refs_0_), channel_id=1, source_target_pairs={{0,256},{128,384},{256,0},{384,128},{1,257},{129,385},{257,1},{385... | collective-permute-start | bytes 442376 | tf_op jit(solution)/shard_map/ppermute | solution.py:358
  42.7 37.9 %collective-permute-start.1 = (f32[9,16,256]{2,1,0:T(8,128)S(1)}, f32[9,16,256]{2,1,0:T(8,128)S(1)}, u32[]{:S(2)}, u32[]{:S(2)}) collective-permute-start(f32[9,16,256]{2,1,0:T(8,128)S(1)} %get-tuple-element.12.refs_0_), channel_id=1, source_target_pairs={{0,128},{128,256},{256,384},{384,0},{1,129},{129,257},{257,385},{3... | collective-permute-start | bytes 442376 | tf_op jit(solution)/shard_map/ppermute | solution.py:358
  44.6 36.0 %collective-permute-start = (f32[9,16,256]{2,1,0:T(8,128)S(1)}, f32[9,16,256]{2,1,0:T(8,128)S(1)}, u32[]{:S(2)}, u32[]{:S(2)}) collective-permute-start(f32[9,16,256]{2,1,0:T(8,128)S(1)} %get-tuple-element.12.refs_0_), channel_id=1, source_target_pairs={{0,384},{128,0},{256,128},{384,256},{1,385},{129,1},{257,129},{385... | collective-permute-start | bytes 442376 | tf_op jit(solution)/shard_map/ppermute | solution.py:358
